TPU v7x, 512 devices: a whole 4x4x16 slice. The times are simulated.
512 devices in a mesh: seq: 128 (over z, x_hi, y), head: 4 (over x_lo, core).
Axes of the slice: x: 4 (x_hi: 2, x_lo: 2; x = x_hi * 2 + x_lo), y: 4, z: 16, core: 2. Of those that a mesh axis runs over, the one named last changes fastest.
Arguments:
- q_old: bfloat16 [28672, 2048], P(('seq', 'head')), may hold values from -6 to 6
- k_old: bfloat16 [28672, 1024], P(('seq', 'head')), may hold values from -6 to 6
- value_old_layout: bfloat16 [28672, 1024], P(('seq', 'head')), may hold values from -6 to 6
- dout_old: bfloat16 [28672, 2048], P(('seq', 'head')), may hold values from -6 to 6
- old_offsets: int32 [129], replicated, may hold values from 0 to 16384, as said below
- new_offsets: int32 [129], replicated, may hold values from 0 to 16384, as said below
Outputs:
- attn_out: bfloat16 [28672, 2048], P('seq', 'head')
- grad_query_out: bfloat16 [28672, 2048], P('seq', 'head')
- grad_key_out: bfloat16 [28672, 1024], P('seq', 'head')
- grad_value_out: bfloat16 [28672, 1024], P('seq', 'head')
Inputs may be any that keep to these rules, and one draw needn't show every extreme that they name: old_offsets[0] = 0 and old_offsets[128] = 16384; old_offsets[j] lies within 48 of j * 128, at exactly -48 for some j and +48 for some j; some block has exactly 224 positions. new_offsets[0] = 0 and new_offsets[128] = 16384; new_offsets[j] lies within 48 of j * 128, at exactly -48 for some j and +48 for some j; some block has exactly 224 positions; for some j, 96 positions of old block j lie in new block j + 1, and for some j, 96 positions of old block j lie in new block j - 1.
All inputs are finite; a program needn't handle non-finite values.
Results may differ from a plain program's by a relative error of at most 0.02.
Values may be sent and summed in bfloat16 or wider, within the bound.
No kernel may reach another device: no remote copies, remote signals or barrier semaphores. Data moves between devices by JAX's collectives and lax.ppermute only.
A program may use at most 64 MiB of HBM per device.

v0:
```python
import jax
import jax.numpy as jnp
from jax import lax
from jax.sharding import PartitionSpec as P

TOK_DEV = 128
ATTEND_WINDOW = 1024
HEAD_SIZE = 128


query_scale = 168.0 ** (-0.5)


def shifted(value, axis, steps):
    count = lax.axis_size(axis)
    initial, last = (max(0, -steps), min(count, count - steps))
    return lax.ppermute(value, axis, [(source, source + steps) for source in range(initial, last)])


def relocate(row_data, source, target, slot_slack, out_rows):
    device = lax.axis_index("seq")
    own_rows = row_data.shape[0]
    first_row = source[device]
    end_row = source[device + 1]
    tail_start = jnp.maximum(end_row - first_row - slot_slack, 0)
    tail_rows = lax.dynamic_slice_in_dim(row_data, tail_start, slot_slack, 0)
    head_rows = row_data[:slot_slack]
    from_left = shifted(tail_rows, "seq", 1)
    from_right = shifted(head_rows, "seq", -1)
    before_row = source[jnp.maximum(device - 1, 0)]
    left_start = before_row + jnp.maximum(first_row - before_row - slot_slack, 0)
    candidates = jnp.concatenate([from_left, row_data, from_right], axis=0)
    targets = target[device] + jnp.arange(out_rows, dtype=jnp.int32)
    selected = jnp.where(
        targets < first_row,
        targets - left_start,
        jnp.where(
            targets < end_row,
            slot_slack + targets - first_row,
            slot_slack + own_rows + targets - end_row,
        ),
    )
    selected = jnp.clip(selected, 0, candidates.shape[0] - 1)
    is_live = targets < target[device + 1]
    return jnp.where(
        is_live[:, None], jnp.take(candidates, selected, axis=0), jnp.zeros((), row_data.dtype)
    )


def key_window(key_value, farthest, nearest):
    device = lax.axis_index("seq")
    devices = lax.axis_size("seq")
    gathered, places, live_parts = ([], [], [])
    for distance in range(farthest, nearest - 1, -1):
        if distance == 0:
            arrived = key_value
        else:
            arrived = shifted(key_value, "seq", distance)
        source_block = device - distance
        gathered.append(arrived)
        places.append(source_block * TOK_DEV + jnp.arange(TOK_DEV, dtype=jnp.int32))
        live_parts.append(jnp.full((TOK_DEV,), (source_block >= 0) & (source_block < devices)))
    return (jnp.concatenate(gathered, axis=0), jnp.concatenate(places), jnp.concatenate(live_parts))


def return_grads(grads, farthest, nearest):
    summed = None
    for position, distance in enumerate(range(farthest, nearest - 1, -1)):
        block = grads[position * TOK_DEV : (position + 1) * TOK_DEV]
        if distance == 0:
            arrived = block
        else:
            arrived = shifted(block.astype(jnp.bfloat16), "seq", -distance).astype(block.dtype)
        summed = arrived if summed is None else summed + arrived
    return summed


def attend(
    queries, grads_out, key_rows, value_rows, query_places, query_live, key_places, key_live
):
    head_count = queries.shape[1] // HEAD_SIZE
    kv_count = key_rows.shape[1] // HEAD_SIZE
    heads_per_group = head_count // kv_count
    gap_rows = query_places[:, None] - key_places[None, :]
    allowed = (gap_rows >= 0) & (gap_rows < ATTEND_WINDOW) & query_live[:, None] & key_live[None, :]
    contract_last = (((1,), (1,)), ((), ()))
    contract_first = (((0,), (0,)), ((), ()))
    attn_parts, query_grads, key_grads, value_grads = ([], [], [], [])
    for kv_head in range(kv_count):
        key_head = key_rows[:, kv_head * HEAD_SIZE : (kv_head + 1) * HEAD_SIZE]
        value_head = value_rows[:, kv_head * HEAD_SIZE : (kv_head + 1) * HEAD_SIZE]
        key_total = jnp.zeros((key_rows.shape[0], HEAD_SIZE), jnp.float32)
        value_total = jnp.zeros((key_rows.shape[0], HEAD_SIZE), jnp.float32)
        for member in range(heads_per_group):
            head_number = kv_head * heads_per_group + member
            query_head = queries[:, head_number * HEAD_SIZE : (head_number + 1) * HEAD_SIZE]
            grad_head = grads_out[:, head_number * HEAD_SIZE : (head_number + 1) * HEAD_SIZE]
            scores = (
                lax.dot_general(
                    query_head, key_head, contract_last, preferred_element_type=jnp.float32
                )
                * query_scale
            )
            scores = jnp.where(allowed, scores, -1e30)
            row_max = jnp.max(scores, axis=1, keepdims=True)
            weights = jnp.where(allowed, jnp.exp(scores - row_max), 0.0)
            row_total = jnp.sum(weights, axis=1, keepdims=True)
            probabilities = weights / jnp.where(query_live[:, None], row_total, 1.0)
            rounded = probabilities.astype(jnp.bfloat16)
            head_out = jnp.dot(rounded, value_head, preferred_element_type=jnp.float32).astype(
                jnp.bfloat16
            )
            row_delta = jnp.sum(
                grad_head.astype(jnp.float32) * head_out.astype(jnp.float32), axis=1, keepdims=True
            )
            grad_prob = lax.dot_general(
                grad_head, value_head, contract_last, preferred_element_type=jnp.float32
            )
            grad_score = (probabilities * (grad_prob - row_delta) * query_scale).astype(
                jnp.bfloat16
            )
            query_grads.append(
                jnp.dot(grad_score, key_head, preferred_element_type=jnp.float32).astype(
                    jnp.bfloat16
                )
            )
            key_total = key_total + lax.dot_general(
                grad_score, query_head, contract_first, preferred_element_type=jnp.float32
            )
            value_total = value_total + lax.dot_general(
                rounded, grad_head, contract_first, preferred_element_type=jnp.float32
            )
            attn_parts.append(head_out)
        key_grads.append(key_total)
        value_grads.append(value_total)
    return (
        jnp.concatenate(attn_parts, axis=1),
        jnp.concatenate(query_grads, axis=1),
        jnp.concatenate(key_grads, axis=1),
        jnp.concatenate(value_grads, axis=1),
    )


def on_device(q_old, k_old, value_old_layout, dout_old, old_offsets, new_offsets):
    query_rows, grad_rows, key_rows, value_rows = (
        lax.all_to_all(q_old, "head", split_axis=1, concat_axis=0, tiled=True),
        lax.all_to_all(dout_old, "head", split_axis=1, concat_axis=0, tiled=True),
        lax.all_to_all(k_old, "head", split_axis=1, concat_axis=0, tiled=True),
        lax.all_to_all(value_old_layout, "head", split_axis=1, concat_axis=0, tiled=True),
    )
    device = lax.axis_index("seq")
    devices = lax.axis_size("seq")
    even_offsets = jnp.arange(devices + 1, dtype=jnp.int32) * TOK_DEV
    query_width = query_rows.shape[1]
    key_width = key_rows.shape[1]
    slot_rows = query_rows.shape[0]
    slot_slack = (slot_rows - TOK_DEV) // 2
    halo_blocks = ATTEND_WINDOW // TOK_DEV
    relocated = relocate(
        jnp.concatenate([query_rows, grad_rows, key_rows, value_rows], axis=1),
        old_offsets,
        even_offsets,
        slot_slack,
        TOK_DEV,
    )
    queries = relocated[:, :query_width]
    grads_out = relocated[:, query_width : 2 * query_width]
    buffered, key_places, key_live = key_window(relocated[:, 2 * query_width :], halo_blocks, 0)
    query_places = device * TOK_DEV + jnp.arange(TOK_DEV, dtype=jnp.int32)
    query_live = jnp.full((TOK_DEV,), True)
    attn, grad_query, key_grad, value_grad = attend(
        queries,
        grads_out,
        buffered[:, :key_width],
        buffered[:, key_width:],
        query_places,
        query_live,
        key_places,
        key_live,
    )
    pair_grads = return_grads(
        jnp.concatenate([key_grad, value_grad], axis=1), halo_blocks, 0
    ).astype(jnp.bfloat16)
    placed = relocate(
        jnp.concatenate([attn, grad_query, pair_grads], axis=1),
        even_offsets,
        new_offsets,
        slot_slack,
        slot_rows,
    )
    attn_out = placed[:, :query_width]
    grad_query_out = placed[:, query_width : 2 * query_width]
    grad_key_out = placed[:, 2 * query_width : 2 * query_width + key_width]
    grad_value_out = placed[:, 2 * query_width + key_width :]
    return (attn_out, grad_query_out, grad_key_out, grad_value_out)


def solution(mesh):
    return jax.shard_map(
        on_device,
        mesh=mesh,
        in_specs=(
            P(("seq", "head"), None),
            P(("seq", "head"), None),
            P(("seq", "head"), None),
            P(("seq", "head"), None),
            P(),
            P(),
        ),
        out_specs=(P("seq", "head"), P("seq", "head"), P("seq", "head"), P("seq", "head")),
        check_vma=False,
    )
```

profile of v0, /device:TPU:252, one launch (start us, length us, event | category | flops | bytes accessed | tf_op | source)
XLA Modules:
  0.0 177.2 jit_solution(12901380850973274010)
XLA Ops:
  0.6 1.6 copy.33
  2.2 3.3 %all-to-all-start.2 = ((bf16[56,4,256]{2,0,1:T(8,128)(2,1)}), bf16[56,4,256]{2,0,1:T(8,128)(2,1)S(1)}, u32[]{:S(2)}, u32[]{:S(2)}) async-start(bf16[56,4,256]{2,0,1:T(8,128)(2,1)} %bitcast.43), calls=%async_computation.2 | async-start | bytes 229376 | tf_op jit(solution)/shard_map/all_to_all | solution.py:148
  5.6 1.5 fusion.95
  10.2 1.2 fusion.81
  11.4 1.6 copy.32
  13.0 1.6 copy.31
  14.6 0.7 copy.30
  15.4 3.3 %all-to-all-start.3 = ((bf16[56,4,256]{2,0,1:T(8,128)(2,1)}), bf16[56,4,256]{2,0,1:T(8,128)(2,1)S(1)}, u32[]{:S(2)}, u32[]{:S(2)}) async-start(bf16[56,4,256]{2,0,1:T(8,128)(2,1)} %bitcast.42), calls=%async_computation.3 | async-start | bytes 229376 | tf_op jit(solution)/shard_map/all_to_all | solution.py:149
  18.7 4.4 %all-to-all-done.3 = bf16[56,4,256]{2,0,1:T(8,128)(2,1)S(1)} async-done(((bf16[56,4,256]{2,0,1:T(8,128)(2,1)}), bf16[56,4,256]{2,0,1:T(8,128)(2,1)S(1)}, u32[]{:S(2)}, u32[]{:S(2)}) %all-to-all-start.3) | async-done | bytes 114720 | tf_op jit(solution)/shard_map/all_to_all | solution.py:149
  23.1 3.4 %all-to-all-start = ((bf16[56,4,512]{2,0,1:T(8,128)(2,1)}), bf16[56,4,512]{2,0,1:T(8,128)(2,1)S(1)}, u32[]{:S(2)}, u32[]{:S(2)}) async-start(bf16[56,4,512]{2,0,1:T(8,128)(2,1)} %bitcast.41), calls=%async_computation | async-start | bytes 458752 | tf_op jit(solution)/shard_map/all_to_all | solution.py:146
  26.5 0.6 compare_select_fusion
  27.2 5.0 %all-to-all-done = bf16[56,4,512]{2,0,1:T(8,128)(2,1)S(1)} async-done(((bf16[56,4,512]{2,0,1:T(8,128)(2,1)}), bf16[56,4,512]{2,0,1:T(8,128)(2,1)S(1)}, u32[]{:S(2)}, u32[]{:S(2)}) %all-to-all-start) | async-done | bytes 229408 | tf_op jit(solution)/shard_map/all_to_all | solution.py:146
  32.1 3.4 %all-to-all-start.1 = ((bf16[56,4,512]{2,0,1:T(8,128)(2,1)}), bf16[56,4,512]{2,0,1:T(8,128)(2,1)S(1)}, u32[]{:S(2)}, u32[]{:S(2)}) async-start(bf16[56,4,512]{2,0,1:T(8,128)(2,1)} %bitcast.40), calls=%async_computation.1 | async-start | bytes 458752 | tf_op jit(solution)/shard_map/all_to_all | solution.py:147
  35.5 5.6 %all-to-all-done.1 = bf16[56,4,512]{2,0,1:T(8,128)(2,1)S(1)} async-done(((bf16[56,4,512]{2,0,1:T(8,128)(2,1)}), bf16[56,4,512]{2,0,1:T(8,128)(2,1)S(1)}, u32[]{:S(2)}, u32[]{:S(2)}) %all-to-all-start.1) | async-done | bytes 229408 | tf_op jit(solution)/shard_map/all_to_all | solution.py:147
  41.2 4.6 %collective-permute-start = (bf16[48,1536]{1,0:T(8,128)(2,1)S(1)}, bf16[48,1536]{1,0:T(8,128)(2,1)S(1)}, u32[]{:S(2)}, u32[]{:S(2)}) collective-permute-start(bf16[48,1536]{1,0:T(8,128)(2,1)S(1)} %get-tuple-element.24), channel_id=1, source_target_pairs={{0,4},{4,8},{8,12},{12,16},{16,20},{20,24},{24,28},{28,32},{32,36}... | collective-permute-start | bytes 442376 | tf_op jit(solution)/shard_map/ppermute | solution.py:17
  45.9 1.9 %collective-permute-start.1 = (bf16[48,1536]{1,0:T(8,128)(2,1)S(1)}, bf16[48,1536]{1,0:T(8,128)(2,1)S(1)}, u32[]{:S(2)}, u32[]{:S(2)}) collective-permute-start(bf16[48,1536]{1,0:T(8,128)(2,1)S(1)} %get-tuple-element.25), channel_id=1, source_target_pairs={{4,0},{8,4},{12,8},{16,12},{20,16},{24,20},{28,24},{32,28},{36,32}... | collective-permute-start | bytes 442376 | tf_op jit(solution)/shard_map/ppermute | solution.py:17
  47.8 1.2 compare_and_fusion
  49.0 9.6 %collective-permute-done.1 = bf16[48,1536]{1,0:T(8,128)(2,1)S(1)} collective-permute-done((bf16[48,1536]{1,0:T(8,128)(2,1)S(1)}, bf16[48,1536]{1,0:T(8,128)(2,1)S(1)}, u32[]{:S(2)}, u32[]{:S(2)}) %collective-permute-start.1) | collective-permute-done | bytes 147488 | tf_op jit(solution)/shard_map/ppermute | solution.py:17
  58.7 0.9 gather_fusion
  59.9 1.9 %collective-permute-start.2 = (bf16[128,512]{0,1:T(8,128)(2,1)S(1)}, bf16[128,512]{0,1:T(8,128)(2,1)S(1)}, u32[]{:S(2)}, u32[]{:S(2)}) collective-permute-start(bf16[128,512]{0,1:T(8,128)(2,1)S(1)} %slice.142), channel_id=1, source_target_pairs={{0,32},{4,36},{8,40},{12,44},{16,48},{20,52},{24,56},{28,60},{32,6... | collective-permute-start | bytes 393224 | tf_op jit(solution)/shard_map/ppermute | solution.py:17
  61.8 0.6 compare_and_fusion.1
  64.6 1.9 %collective-permute-start.3 = (bf16[128,512]{0,1:T(8,128)(2,1)S(1)}, bf16[128,512]{0,1:T(8,128)(2,1)S(1)}, u32[]{:S(2)}, u32[]{:S(2)}) collective-permute-start(bf16[128,512]{0,1:T(8,128)(2,1)S(1)} %slice.142), channel_id=1, source_target_pairs={{0,28},{4,32},{8,36},{12,40},{16,44},{20,48},{24,52},{28,56},{32,6... | collective-permute-start | bytes 393224 | tf_op jit(solution)/shard_map/ppermute | solution.py:17
  66.5 7.8 %collective-permute-start.9 = (bf16[128,512]{0,1:T(8,128)(2,1)S(1)}, bf16[128,512]{0,1:T(8,128)(2,1)S(1)}, u32[]{:S(2)}, u32[]{:S(2)}) collective-permute-start(bf16[128,512]{0,1:T(8,128)(2,1)S(1)} %slice.142), channel_id=1, source_target_pairs={{0,4},{4,8},{8,12},{12,16},{16,20},{20,24},{24,28},{28,32},{32,36}... | collective-permute-start | bytes 393224 | tf_op jit(solution)/shard_map/ppermute | solution.py:17
  74.3 1.9 %collective-permute-start.8 = (bf16[128,512]{0,1:T(8,128)(2,1)S(1)}, bf16[128,512]{0,1:T(8,128)(2,1)S(1)}, u32[]{:S(2)}, u32[]{:S(2)}) collective-permute-start(bf16[128,512]{0,1:T(8,128)(2,1)S(1)} %slice.142), channel_id=1, source_target_pairs={{0,8},{4,12},{8,16},{12,20},{16,24},{20,28},{24,32},{28,36},{32,40... | collective-permute-start | bytes 393224 | tf_op jit(solution)/shard_map/ppermute | solution.py:17
  76.2 4.3 %collective-permute-start.7 = (bf16[128,512]{0,1:T(8,128)(2,1)S(1)}, bf16[128,512]{0,1:T(8,128)(2,1)S(1)}, u32[]{:S(2)}, u32[]{:S(2)}) collective-permute-start(bf16[128,512]{0,1:T(8,128)(2,1)S(1)} %slice.142), channel_id=1, source_target_pairs={{0,12},{4,16},{8,20},{12,24},{16,28},{20,32},{24,36},{28,40},{32,4... | collective-permute-start | bytes 393224 | tf_op jit(solution)/shard_map/ppermute | solution.py:17
  80.6 3.5 %collective-permute-start.4 = (bf16[128,512]{0,1:T(8,128)(2,1)S(1)}, bf16[128,512]{0,1:T(8,128)(2,1)S(1)}, u32[]{:S(2)}, u32[]{:S(2)}) collective-permute-start(bf16[128,512]{0,1:T(8,128)(2,1)S(1)} %slice.142), channel_id=1, source_target_pairs={{0,24},{4,28},{8,32},{12,36},{16,40},{20,44},{24,48},{28,52},{32,5... | collective-permute-start | bytes 393224 | tf_op jit(solution)/shard_map/ppermute | solution.py:17
  84.1 8.6 %collective-permute-start.5 = (bf16[128,512]{0,1:T(8,128)(2,1)S(1)}, bf16[128,512]{0,1:T(8,128)(2,1)S(1)}, u32[]{:S(2)}, u32[]{:S(2)}) collective-permute-start(bf16[128,512]{0,1:T(8,128)(2,1)S(1)} %slice.142), channel_id=1, source_target_pairs={{0,20},{4,24},{8,28},{12,32},{16,36},{20,40},{24,44},{28,48},{32,5... | collective-permute-start | bytes 393224 | tf_op jit(solution)/shard_map/ppermute | solution.py:17
  92.7 4.7 %collective-permute-start.6 = (bf16[128,512]{0,1:T(8,128)(2,1)S(1)}, bf16[128,512]{0,1:T(8,128)(2,1)S(1)}, u32[]{:S(2)}, u32[]{:S(2)}) collective-permute-start(bf16[128,512]{0,1:T(8,128)(2,1)S(1)} %slice.142), channel_id=1, source_target_pairs={{0,16},{4,20},{8,24},{12,28},{16,32},{20,36},{24,40},{28,44},{32,4... | collective-permute-start | bytes 393224 | tf_op jit(solution)/shard_map/ppermute | solution.py:17
  97.6 3.5 %collective-permute-done.6 = bf16[128,512]{0,1:T(8,128)(2,1)S(1)} collective-permute-done((bf16[128,512]{0,1:T(8,128)(2,1)S(1)}, bf16[128,512]{0,1:T(8,128)(2,1)S(1)}, u32[]{:S(2)}, u32[]{:S(2)}) %collective-permute-start.6) | collective-permute-done | bytes 131104 | tf_op jit(solution)/shard_map/ppermute | solution.py:17
  103.1 0.7 fusion.29
  110.6 1.9 %collective-permute-start.10 = (bf16[128,512]{0,1:T(8,128)(2,1)S(1)}, bf16[128,512]{0,1:T(8,128)(2,1)S(1)}, u32[]{:S(2)}, u32[]{:S(2)}) collective-permute-start(bf16[128,512]{0,1:T(8,128)(2,1)S(1)} %get-tuple-element.12), channel_id=1, source_target_pairs={{32,0},{36,4},{40,8},{44,12},{48,16},{52,20},{56,24},{60,28},{64,3... | collective-permute-start | bytes 393224 | tf_op jit(solution)/shard_map/ppermute | solution.py:17
  112.6 5.0 %collective-permute-start.17 = (bf16[128,512]{0,1:T(8,128)(2,1)S(1)}, bf16[128,512]{0,1:T(8,128)(2,1)S(1)}, u32[]{:S(2)}, u32[]{:S(2)}) collective-permute-start(bf16[128,512]{0,1:T(8,128)(2,1)S(1)} %get-tuple-element.13), channel_id=1, source_target_pairs={{4,0},{8,4},{12,8},{16,12},{20,16},{24,20},{28,24},{32,28},{36,32}... | collective-permute-start | bytes 393224 | tf_op jit(solution)/shard_map/ppermute | solution.py:17
  117.6 1.9 %collective-permute-start.16 = (bf16[128,512]{0,1:T(8,128)(2,1)S(1)}, bf16[128,512]{0,1:T(8,128)(2,1)S(1)}, u32[]{:S(2)}, u32[]{:S(2)}) collective-permute-start(bf16[128,512]{0,1:T(8,128)(2,1)S(1)} %get-tuple-element.14), channel_id=1, source_target_pairs={{8,0},{12,4},{16,8},{20,12},{24,16},{28,20},{32,24},{36,28},{40,32... | collective-permute-start | bytes 393224 | tf_op jit(solution)/shard_map/ppermute | solution.py:17
  119.5 7.4 %collective-permute-start.15 = (bf16[128,512]{0,1:T(8,128)(2,1)S(1)}, bf16[128,512]{0,1:T(8,128)(2,1)S(1)}, u32[]{:S(2)}, u32[]{:S(2)}) collective-permute-start(bf16[128,512]{0,1:T(8,128)(2,1)S(1)} %get-tuple-element.15), channel_id=1, source_target_pairs={{12,0},{16,4},{20,8},{24,12},{28,16},{32,20},{36,24},{40,28},{44,3... | collective-permute-start | bytes 393224 | tf_op jit(solution)/shard_map/ppermute | solution.py:17
  126.9 3.2 %collective-permute-start.14 = (bf16[128,512]{0,1:T(8,128)(2,1)S(1)}, bf16[128,512]{0,1:T(8,128)(2,1)S(1)}, u32[]{:S(2)}, u32[]{:S(2)}) collective-permute-start(bf16[128,512]{0,1:T(8,128)(2,1)S(1)} %get-tuple-element.16), channel_id=1, source_target_pairs={{16,0},{20,4},{24,8},{28,12},{32,16},{36,20},{40,24},{44,28},{48,3... | collective-permute-start | bytes 393224 | tf_op jit(solution)/shard_map/ppermute | solution.py:17
  130.4 5.1 %collective-permute-start.13 = (bf16[128,512]{0,1:T(8,128)(2,1)S(1)}, bf16[128,512]{0,1:T(8,128)(2,1)S(1)}, u32[]{:S(2)}, u32[]{:S(2)}) collective-permute-start(bf16[128,512]{0,1:T(8,128)(2,1)S(1)} %get-tuple-element.17), channel_id=1, source_target_pairs={{20,0},{24,4},{28,8},{32,12},{36,16},{40,20},{44,24},{48,28},{52,3... | collective-permute-start | bytes 393224 | tf_op jit(solution)/shard_map/ppermute | solution.py:17
  135.5 7.3 %collective-permute-start.12 = (bf16[128,512]{0,1:T(8,128)(2,1)S(1)}, bf16[128,512]{0,1:T(8,128)(2,1)S(1)}, u32[]{:S(2)}, u32[]{:S(2)}) collective-permute-start(bf16[128,512]{0,1:T(8,128)(2,1)S(1)} %get-tuple-element.18), channel_id=1, source_target_pairs={{24,0},{28,4},{32,8},{36,12},{40,16},{44,20},{48,24},{52,28},{56,3... | collective-permute-start | bytes 393224 | tf_op jit(solution)/shard_map/ppermute | solution.py:17
  142.8 1.9 %collective-permute-start.11 = (bf16[128,512]{0,1:T(8,128)(2,1)S(1)}, bf16[128,512]{0,1:T(8,128)(2,1)S(1)}, u32[]{:S(2)}, u32[]{:S(2)}) collective-permute-start(bf16[128,512]{0,1:T(8,128)(2,1)S(1)} %get-tuple-element.19), channel_id=1, source_target_pairs={{28,0},{32,4},{36,8},{40,12},{44,16},{48,20},{52,24},{56,28},{60,3... | collective-permute-start | bytes 393224 | tf_op jit(solution)/shard_map/ppermute | solution.py:17
  145.0 1.9 %collective-permute-done.12 = bf16[128,512]{0,1:T(8,128)(2,1)S(1)} collective-permute-done((bf16[128,512]{0,1:T(8,128)(2,1)S(1)}, bf16[128,512]{0,1:T(8,128)(2,1)S(1)}, u32[]{:S(2)}, u32[]{:S(2)}) %collective-permute-start.12) | collective-permute-done | bytes 131104 | tf_op jit(solution)/shard_map/ppermute | solution.py:17
  146.9 4.9 %collective-permute-done.11 = bf16[128,512]{0,1:T(8,128)(2,1)S(1)} collective-permute-done((bf16[128,512]{0,1:T(8,128)(2,1)S(1)}, bf16[128,512]{0,1:T(8,128)(2,1)S(1)}, u32[]{:S(2)}, u32[]{:S(2)}) %collective-permute-start.11) | collective-permute-done | bytes 131104 | tf_op jit(solution)/shard_map/ppermute | solution.py:17
  152.2 6.0 %collective-permute-start.18 = (bf16[48,1536]{0,1:T(8,128)(2,1)S(1)}, bf16[48,1536]{0,1:T(8,128)(2,1)S(1)}, u32[]{:S(2)}, u32[]{:S(2)}) collective-permute-start(bf16[48,1536]{0,1:T(8,128)(2,1)S(1)} %get-tuple-element.26), channel_id=1, source_target_pairs={{0,4},{4,8},{8,12},{12,16},{16,20},{20,24},{24,28},{28,32},{32,36}... | collective-permute-start | bytes 442376 | tf_op jit(solution)/shard_map/ppermute | solution.py:17
  158.2 1.9 %collective-permute-start.19 = (bf16[48,1536]{0,1:T(8,128)(2,1)S(1)}, bf16[48,1536]{0,1:T(8,128)(2,1)S(1)}, u32[]{:S(2)}, u32[]{:S(2)}) collective-permute-start(bf16[48,1536]{0,1:T(8,128)(2,1)S(1)} %get-tuple-element.27), channel_id=1, source_target_pairs={{4,0},{8,4},{12,8},{16,12},{20,16},{24,20},{28,24},{32,28},{36,32}... | collective-permute-start | bytes 442376 | tf_op jit(solution)/shard_map/ppermute | solution.py:17
  160.1 1.3 fusion.78
  161.4 2.1 %collective-permute-done.18 = bf16[48,1536]{0,1:T(8,128)(2,1)S(1)} collective-permute-done((bf16[48,1536]{0,1:T(8,128)(2,1)S(1)}, bf16[48,1536]{0,1:T(8,128)(2,1)S(1)}, u32[]{:S(2)}, u32[]{:S(2)}) %collective-permute-start.18) | collective-permute-done | bytes 147488 | tf_op jit(solution)/shard_map/ppermute | solution.py:17
  163.5 10.1 %collective-permute-done.19 = bf16[48,1536]{0,1:T(8,128)(2,1)S(1)} collective-permute-done((bf16[48,1536]{0,1:T(8,128)(2,1)S(1)}, bf16[48,1536]{0,1:T(8,128)(2,1)S(1)}, u32[]{:S(2)}, u32[]{:S(2)}) %collective-permute-start.19) | collective-permute-done | bytes 147488 | tf_op jit(solution)/shard_map/ppermute | solution.py:17
  174.3 1.2 gather_fusion.1
  175.7 0.7 fusion.93
  176.4 0.8 fusion.94
  (97 shorter events, 13.0 us)
Async XLA Ops:
  0.6 14.0 %copy-start = (bf16[56,2048]{1,0:T(8,128)(2,1)S(1)}, bf16[56,2048]{1,0:T(8,128)(2,1)}, u32[]{:S(2)}) copy-start(bf16[56,2048]{1,0:T(8,128)(2,1)} %param.9) | copy-start | bytes 688132
  2.2 13.1 %all-to-all-start.2 = ((bf16[56,4,256]{2,0,1:T(8,128)(2,1)}), bf16[56,4,256]{2,0,1:T(8,128)(2,1)S(1)}, u32[]{:S(2)}, u32[]{:S(2)}) async-start(bf16[56,4,256]{2,0,1:T(8,128)(2,1)} %bitcast.43), calls=%async_computation.2 | async-start | bytes 229376 | tf_op jit(solution)/shard_map/all_to_all | solution.py:148
  15.4 7.7 %all-to-all-start.3 = ((bf16[56,4,256]{2,0,1:T(8,128)(2,1)}), bf16[56,4,256]{2,0,1:T(8,128)(2,1)S(1)}, u32[]{:S(2)}, u32[]{:S(2)}) async-start(bf16[56,4,256]{2,0,1:T(8,128)(2,1)} %bitcast.42), calls=%async_computation.3 | async-start | bytes 229376 | tf_op jit(solution)/shard_map/all_to_all | solution.py:149
  23.1 9.0 %all-to-all-start = ((bf16[56,4,512]{2,0,1:T(8,128)(2,1)}), bf16[56,4,512]{2,0,1:T(8,128)(2,1)S(1)}, u32[]{:S(2)}, u32[]{:S(2)}) async-start(bf16[56,4,512]{2,0,1:T(8,128)(2,1)} %bitcast.41), calls=%async_computation | async-start | bytes 458752 | tf_op jit(solution)/shard_map/all_to_all | solution.py:146
  32.1 9.0 %all-to-all-start.1 = ((bf16[56,4,512]{2,0,1:T(8,128)(2,1)}), bf16[56,4,512]{2,0,1:T(8,128)(2,1)S(1)}, u32[]{:S(2)}, u32[]{:S(2)}) async-start(bf16[56,4,512]{2,0,1:T(8,128)(2,1)} %bitcast.40), calls=%async_computation.1 | async-start | bytes 458752 | tf_op jit(solution)/shard_map/all_to_all | solution.py:147
  41.2 7.8 %collective-permute-start = (bf16[48,1536]{1,0:T(8,128)(2,1)S(1)}, bf16[48,1536]{1,0:T(8,128)(2,1)S(1)}, u32[]{:S(2)}, u32[]{:S(2)}) collective-permute-start(bf16[48,1536]{1,0:T(8,128)(2,1)S(1)} %get-tuple-element.24), channel_id=1, source_target_pairs={{0,4},{4,8},{8,12},{12,16},{16,20},{20,24},{24,28},{28,32},{32,36}... | collective-permute-start | bytes 442376 | tf_op jit(solution)/shard_map/ppermute | solution.py:17
  45.9 12.8 %collective-permute-start.1 = (bf16[48,1536]{1,0:T(8,128)(2,1)S(1)}, bf16[48,1536]{1,0:T(8,128)(2,1)S(1)}, u32[]{:S(2)}, u32[]{:S(2)}) collective-permute-start(bf16[48,1536]{1,0:T(8,128)(2,1)S(1)} %get-tuple-element.25), channel_id=1, source_target_pairs={{4,0},{8,4},{12,8},{16,12},{20,16},{24,20},{28,24},{32,28},{36,32}... | collective-permute-start | bytes 442376 | tf_op jit(solution)/shard_map/ppermute | solution.py:17
  59.9 20.6 %collective-permute-start.2 = (bf16[128,512]{0,1:T(8,128)(2,1)S(1)}, bf16[128,512]{0,1:T(8,128)(2,1)S(1)}, u32[]{:S(2)}, u32[]{:S(2)}) collective-permute-start(bf16[128,512]{0,1:T(8,128)(2,1)S(1)} %slice.142), channel_id=1, source_target_pairs={{0,32},{4,36},{8,40},{12,44},{16,48},{20,52},{24,56},{28,60},{32,6... | collective-permute-start | bytes 393224 | tf_op jit(solution)/shard_map/ppermute | solution.py:17
  64.6 19.5 %collective-permute-start.3 = (bf16[128,512]{0,1:T(8,128)(2,1)S(1)}, bf16[128,512]{0,1:T(8,128)(2,1)S(1)}, u32[]{:S(2)}, u32[]{:S(2)}) collective-permute-start(bf16[128,512]{0,1:T(8,128)(2,1)S(1)} %slice.142), channel_id=1, source_target_pairs={{0,28},{4,32},{8,36},{12,40},{16,44},{20,48},{24,52},{28,56},{32,6... | collective-permute-start | bytes 393224 | tf_op jit(solution)/shard_map/ppermute | solution.py:17
  66.5 34.8 %collective-permute-start.9 = (bf16[128,512]{0,1:T(8,128)(2,1)S(1)}, bf16[128,512]{0,1:T(8,128)(2,1)S(1)}, u32[]{:S(2)}, u32[]{:S(2)}) collective-permute-start(bf16[128,512]{0,1:T(8,128)(2,1)S(1)} %slice.142), channel_id=1, source_target_pairs={{0,4},{4,8},{8,12},{12,16},{16,20},{20,24},{24,28},{28,32},{32,36}... | collective-permute-start | bytes 393224 | tf_op jit(solution)/shard_map/ppermute | solution.py:17
  74.3 26.9 %collective-permute-start.8 = (bf16[128,512]{0,1:T(8,128)(2,1)S(1)}, bf16[128,512]{0,1:T(8,128)(2,1)S(1)}, u32[]{:S(2)}, u32[]{:S(2)}) collective-permute-start(bf16[128,512]{0,1:T(8,128)(2,1)S(1)} %slice.142), channel_id=1, source_target_pairs={{0,8},{4,12},{8,16},{12,20},{16,24},{20,28},{24,32},{28,36},{32,40... | collective-permute-start | bytes 393224 | tf_op jit(solution)/shard_map/ppermute | solution.py:17
  76.2 24.9 %collective-permute-start.7 = (bf16[128,512]{0,1:T(8,128)(2,1)S(1)}, bf16[128,512]{0,1:T(8,128)(2,1)S(1)}, u32[]{:S(2)}, u32[]{:S(2)}) collective-permute-start(bf16[128,512]{0,1:T(8,128)(2,1)S(1)} %slice.142), channel_id=1, source_target_pairs={{0,12},{4,16},{8,20},{12,24},{16,28},{20,32},{24,36},{28,40},{32,4... | collective-permute-start | bytes 393224 | tf_op jit(solution)/shard_map/ppermute | solution.py:17
  80.6 12.2 %collective-permute-start.4 = (bf16[128,512]{0,1:T(8,128)(2,1)S(1)}, bf16[128,512]{0,1:T(8,128)(2,1)S(1)}, u32[]{:S(2)}, u32[]{:S(2)}) collective-permute-start(bf16[128,512]{0,1:T(8,128)(2,1)S(1)} %slice.142), channel_id=1, source_target_pairs={{0,24},{4,28},{8,32},{12,36},{16,40},{20,44},{24,48},{28,52},{32,5... | collective-permute-start | bytes 393224 | tf_op jit(solution)/shard_map/ppermute | solution.py:17
  84.1 13.4 %collective-permute-start.5 = (bf16[128,512]{0,1:T(8,128)(2,1)S(1)}, bf16[128,512]{0,1:T(8,128)(2,1)S(1)}, u32[]{:S(2)}, u32[]{:S(2)}) collective-permute-start(bf16[128,512]{0,1:T(8,128)(2,1)S(1)} %slice.142), channel_id=1, source_target_pairs={{0,20},{4,24},{8,28},{12,32},{16,36},{20,40},{24,44},{28,48},{32,5... | collective-permute-start | bytes 393224 | tf_op jit(solution)/shard_map/ppermute | solution.py:17
  92.7 8.4 %collective-permute-start.6 = (bf16[128,512]{0,1:T(8,128)(2,1)S(1)}, bf16[128,512]{0,1:T(8,128)(2,1)S(1)}, u32[]{:S(2)}, u32[]{:S(2)}) collective-permute-start(bf16[128,512]{0,1:T(8,128)(2,1)S(1)} %slice.142), channel_id=1, source_target_pairs={{0,16},{4,20},{8,24},{12,28},{16,32},{20,36},{24,40},{28,44},{32,4... | collective-permute-start | bytes 393224 | tf_op jit(solution)/shard_map/ppermute | solution.py:17
  110.6 19.7 %collective-permute-start.10 = (bf16[128,512]{0,1:T(8,128)(2,1)S(1)}, bf16[128,512]{0,1:T(8,128)(2,1)S(1)}, u32[]{:S(2)}, u32[]{:S(2)}) collective-permute-start(bf16[128,512]{0,1:T(8,128)(2,1)S(1)} %get-tuple-element.12), channel_id=1, source_target_pairs={{32,0},{36,4},{40,8},{44,12},{48,16},{52,20},{56,24},{60,28},{64,3... | collective-permute-start | bytes 393224 | tf_op jit(solution)/shard_map/ppermute | solution.py:17
  112.6 22.9 %collective-permute-start.17 = (bf16[128,512]{0,1:T(8,128)(2,1)S(1)}, bf16[128,512]{0,1:T(8,128)(2,1)S(1)}, u32[]{:S(2)}, u32[]{:S(2)}) collective-permute-start(bf16[128,512]{0,1:T(8,128)(2,1)S(1)} %get-tuple-element.13), channel_id=1, source_target_pairs={{4,0},{8,4},{12,8},{16,12},{20,16},{24,20},{28,24},{32,28},{36,32}... | collective-permute-start | bytes 393224 | tf_op jit(solution)/shard_map/ppermute | solution.py:17
  117.6 25.2 %collective-permute-start.16 = (bf16[128,512]{0,1:T(8,128)(2,1)S(1)}, bf16[128,512]{0,1:T(8,128)(2,1)S(1)}, u32[]{:S(2)}, u32[]{:S(2)}) collective-permute-start(bf16[128,512]{0,1:T(8,128)(2,1)S(1)} %get-tuple-element.14), channel_id=1, source_target_pairs={{8,0},{12,4},{16,8},{20,12},{24,16},{28,20},{32,24},{36,28},{40,32... | collective-permute-start | bytes 393224 | tf_op jit(solution)/shard_map/ppermute | solution.py:17
  119.5 25.4 %collective-permute-start.15 = (bf16[128,512]{0,1:T(8,128)(2,1)S(1)}, bf16[128,512]{0,1:T(8,128)(2,1)S(1)}, u32[]{:S(2)}, u32[]{:S(2)}) collective-permute-start(bf16[128,512]{0,1:T(8,128)(2,1)S(1)} %get-tuple-element.15), channel_id=1, source_target_pairs={{12,0},{16,4},{20,8},{24,12},{28,16},{32,20},{36,24},{40,28},{44,3... | collective-permute-start | bytes 393224 | tf_op jit(solution)/shard_map/ppermute | solution.py:17
  126.9 18.1 %collective-permute-start.14 = (bf16[128,512]{0,1:T(8,128)(2,1)S(1)}, bf16[128,512]{0,1:T(8,128)(2,1)S(1)}, u32[]{:S(2)}, u32[]{:S(2)}) collective-permute-start(bf16[128,512]{0,1:T(8,128)(2,1)S(1)} %get-tuple-element.16), channel_id=1, source_target_pairs={{16,0},{20,4},{24,8},{28,12},{32,16},{36,20},{40,24},{44,28},{48,3... | collective-permute-start | bytes 393224 | tf_op jit(solution)/shard_map/ppermute | solution.py:17
  130.4 14.6 %collective-permute-start.13 = (bf16[128,512]{0,1:T(8,128)(2,1)S(1)}, bf16[128,512]{0,1:T(8,128)(2,1)S(1)}, u32[]{:S(2)}, u32[]{:S(2)}) collective-permute-start(bf16[128,512]{0,1:T(8,128)(2,1)S(1)} %get-tuple-element.17), channel_id=1, source_target_pairs={{20,0},{24,4},{28,8},{32,12},{36,16},{40,20},{44,24},{48,28},{52,3... | collective-permute-start | bytes 393224 | tf_op jit(solution)/shard_map/ppermute | solution.py:17
  135.5 11.4 %collective-permute-start.12 = (bf16[128,512]{0,1:T(8,128)(2,1)S(1)}, bf16[128,512]{0,1:T(8,128)(2,1)S(1)}, u32[]{:S(2)}, u32[]{:S(2)}) collective-permute-start(bf16[128,512]{0,1:T(8,128)(2,1)S(1)} %get-tuple-element.18), channel_id=1, source_target_pairs={{24,0},{28,4},{32,8},{36,12},{40,16},{44,20},{48,24},{52,28},{56,3... | collective-permute-start | bytes 393224 | tf_op jit(solution)/shard_map/ppermute | solution.py:17
  142.8 9.1 %collective-permute-start.11 = (bf16[128,512]{0,1:T(8,128)(2,1)S(1)}, bf16[128,512]{0,1:T(8,128)(2,1)S(1)}, u32[]{:S(2)}, u32[]{:S(2)}) collective-permute-start(bf16[128,512]{0,1:T(8,128)(2,1)S(1)} %get-tuple-element.19), channel_id=1, source_target_pairs={{28,0},{32,4},{36,8},{40,12},{44,16},{48,20},{52,24},{56,28},{60,3... | collective-permute-start | bytes 393224 | tf_op jit(solution)/shard_map/ppermute | solution.py:17
  152.2 11.3 %collective-permute-start.18 = (bf16[48,1536]{0,1:T(8,128)(2,1)S(1)}, bf16[48,1536]{0,1:T(8,128)(2,1)S(1)}, u32[]{:S(2)}, u32[]{:S(2)}) collective-permute-start(bf16[48,1536]{0,1:T(8,128)(2,1)S(1)} %get-tuple-element.26), channel_id=1, source_target_pairs={{0,4},{4,8},{8,12},{12,16},{16,20},{20,24},{24,28},{28,32},{32,36}... | collective-permute-start | bytes 442376 | tf_op jit(solution)/shard_map/ppermute | solution.py:17
  158.2 15.4 %collective-permute-start.19 = (bf16[48,1536]{0,1:T(8,128)(2,1)S(1)}, bf16[48,1536]{0,1:T(8,128)(2,1)S(1)}, u32[]{:S(2)}, u32[]{:S(2)}) collective-permute-start(bf16[48,1536]{0,1:T(8,128)(2,1)S(1)} %get-tuple-element.27), channel_id=1, source_target_pairs={{4,0},{8,4},{12,8},{16,12},{20,16},{24,20},{28,24},{32,28},{36,32}... | collective-permute-start | bytes 442376 | tf_op jit(solution)/shard_map/ppermute | solution.py:17
where the time goes:
time: 178 us; the launch traced here: 177 us
  starting transfers between devices  96.3 us (54%)
  waiting for transfers between devices  47.1 us (26%)
  local copies, waits for them, and re-layouts  13.7 us (8%)
  matrix products  7.91 us (4%)
  other arithmetic  7.53 us (4%)
  between operations  4.65 us (3%)
    ppermute x20, starting transfers between devices, shifted(): lax.ppermute(value, axis, [(source, source + steps) for source in range(i...  82.8 us
    ppermute x20, waiting for transfers between devices, shifted(): lax.ppermute(value, axis, [(source, source + steps) for source in range(i...  32.2 us
    all_to_all x1, waiting for transfers between devices, on_device(): lax.all_to_all(dout_old, 'head', split_axis=1, concat_axis=0, tiled=True)  5.59 us
    all_to_all x1, waiting for transfers between devices, on_device(): lax.all_to_all(q_old, 'head', split_axis=1, concat_axis=0, tiled=True)  4.95 us
    all_to_all x1, waiting for transfers between devices, on_device(): lax.all_to_all(value_old_layout, 'head', split_axis=1, concat_axis=0, til...  4.38 us
  transfers between devices with their start and end apart: 24, of which 9 were waited for; matrix products, arithmetic and copies ran while one was open for 7% of the time, Pallas kernels for 0%

commit v1 on v0

v1 whole, which is shorter than its diff:
```python
import jax
import jax.numpy as jnp
from jax import lax
from jax.experimental import pallas as pl
from jax.experimental.pallas import tpu as pltpu
from jax.sharding import Mesh, PartitionSpec as P

PAIR = 256
SLOTS = 224
EDGE = 48
HEAD = 128
UNITS = 4
PAIRS = 64
SWAP = PAIR - 80
SCALE = 168.0 ** (-0.5)
LOG2E = 1.4426950408889634
OUTSIDE = -1e30

AXES = ("z", "xh", "yh", "yl", "xl", "c")
PAIR_AXES = ("z", "xh", "yh")
SEQ_AXES = ("z", "xh", "yh", "yl")
GROUP_AXES = ("yl", "xl", "c")
PLANE_AXES = ("xh", "yh")

NT = (((1,), (1,)), ((), ()))
NN = (((1,), (0,)), ((), ()))
TN = (((0,), (0,)), ((), ()))


def dot(a, b, dims):
    return lax.dot_general(a, b, dims, preferred_element_type=jnp.float32)


def pair_index():
    return (lax.axis_index("z") * 2 + lax.axis_index("xh")) * 2 + lax.axis_index("yh")


def vmem():
    return pl.BlockSpec(memory_space=pltpu.VMEM)


def smem():
    return pl.BlockSpec(memory_space=pltpu.SMEM)


def call(kernel, outs, specs, scratch=(), name=None, flops=0):
    many = isinstance(outs, (list, tuple))
    return pl.pallas_call(
        kernel,
        out_shape=outs,
        in_specs=specs,
        out_specs=[vmem() for _ in outs] if many else vmem(),
        scratch_shapes=list(scratch),
        name=name,
        cost_estimate=pl.CostEstimate(flops=flops, bytes_accessed=1 << 20, transcendentals=0),
    )


def shape(*dims, dtype=jnp.bfloat16):
    return jax.ShapeDtypeStruct(dims, dtype)


def picked(rows, source, candidates):
    count = candidates.shape[0]
    columns = lax.broadcasted_iota(jnp.int32, (rows, count), 1)
    chosen = (columns == source).astype(jnp.float32).astype(jnp.bfloat16)
    return dot(chosen, candidates, NN).astype(jnp.bfloat16)


def pack_kernel(first_ref, second_ref, out_ref):
    width = first_ref.shape[1] // 8
    for target in range(8):
        head = (target % 4) * 2 + target // 4
        out_ref[target, :, :width] = first_ref[:, head * width : (head + 1) * width]
        out_ref[target, :, width:] = second_ref[:, head * width : (head + 1) * width]


def pack(first, second, name):
    rows, cols = first.shape
    return call(pack_kernel, shape(8, rows, cols // 4), [vmem(), vmem()], name=name)(first, second)


def edges_kernel(offsets_ref, slots_ref, left_ref, right_ref):
    pair = pair_index()
    first = offsets_ref[2 * pair]
    middle = offsets_ref[2 * pair + 1]
    row = lax.broadcasted_iota(jnp.int32, (2 * EDGE, 1), 0)
    to_left = row + (pair * PAIR - EDGE - first)
    to_right = row + (SLOTS - EDGE + (pair + 1) * PAIR - middle)
    source = jnp.where(row < EDGE, to_left, to_right)
    both = picked(2 * EDGE, source, slots_ref[...])
    left_ref[...] = both[:EDGE]
    right_ref[...] = both[EDGE:]


def even_kernel(offsets_ref, slots_ref, left_ref, right_ref, out_ref):
    pair = pair_index()
    first = offsets_ref[2 * pair]
    middle = offsets_ref[2 * pair + 1]
    last = offsets_ref[2 * pair + 2]
    row = lax.broadcasted_iota(jnp.int32, (PAIR, 1), 0)
    place = row + pair * PAIR
    source = jnp.where(
        place < first,
        2 * SLOTS + row,
        jnp.where(
            place < middle,
            place - first,
            jnp.where(place < last, SLOTS + place - middle, 2 * SLOTS + 2 * EDGE - PAIR + row),
        ),
    )
    width = slots_ref.shape[1]
    candidates = jnp.concatenate(
        [slots_ref[...], left_ref[...], right_ref[...], jnp.zeros((96, width), jnp.bfloat16)], axis=0
    )
    out_ref[...] = picked(PAIR, source, candidates)


def even_rows(slots, offsets, name):
    width = slots.shape[1]
    left, right = call(
        edges_kernel,
        [shape(EDGE, width), shape(EDGE, width)],
        [smem(), vmem()],
        name=name + "_edges",
    )(offsets, slots)
    from_right = lax.ppermute(left, PAIR_AXES, [(i + 1, i) for i in range(PAIRS - 1)])
    from_left = lax.ppermute(right, PAIR_AXES, [(i, i + 1) for i in range(PAIRS - 1)])
    return call(
        even_kernel, shape(PAIR, width), [smem(), vmem(), vmem(), vmem()], name=name + "_even"
    )(offsets, slots, from_left, from_right)


def choose_kernel(own_ref, far_ref, out_ref):
    here = lax.axis_index("xh") * 2 + lax.axis_index("yh")
    for target in range(UNITS):

        @pl.when(here < target)
        def _():
            out_ref[target] = own_ref[...]

        @pl.when(here >= target)
        def _():
            out_ref[target] = far_ref[...]


def attend_kernel(
    rows_ref, own_ref, far_ref, others_ref, out_ref, swap_ref, step_ref, skip_ref,
    given_ref, kept_ref, back_ref, score_ref,
):
    here = lax.axis_index("xh") * 2 + lax.axis_index("yh")
    started = lax.axis_index("z") > 0
    width = 2 * PAIR
    queries = jnp.concatenate([rows_ref[:, :HEAD], rows_ref[:, HEAD : 2 * HEAD]], axis=0)
    grads = jnp.concatenate([rows_ref[:, 2 * HEAD : 3 * HEAD], rows_ref[:, 3 * HEAD :]], axis=0)
    key_row = lax.broadcasted_iota(jnp.int32, (PAIR, width), 0)
    query_row = lax.broadcasted_iota(jnp.int32, (PAIR, width), 1) & (PAIR - 1)
    near = key_row <= query_row
    unit_of = [(here + step) & (UNITS - 1) for step in range(1, UNITS)]
    top = jnp.full((1, width), OUTSIDE, jnp.float32)
    for step, unit in enumerate(unit_of):
        bias = jnp.where((unit < here) | started, 0.0, OUTSIDE)
        score = dot(others_ref[unit, :, :HEAD], queries, NT) * (SCALE * LOG2E) + bias
        score_ref[step * PAIR : (step + 1) * PAIR, :] = score
        top = jnp.maximum(top, jnp.max(score, axis=0, keepdims=True))
    bias = jnp.where(started, 0.0, OUTSIDE)
    score = jnp.where(
        near,
        dot(own_ref[:, :HEAD], queries, NT) * (SCALE * LOG2E),
        dot(far_ref[:, :HEAD], queries, NT) * (SCALE * LOG2E) + bias,
    )
    score_ref[3 * PAIR :, :] = score
    top = jnp.maximum(top, jnp.max(score, axis=0, keepdims=True))
    total = jnp.zeros((1, width), jnp.float32)
    for step in range(UNITS):
        weight = jnp.exp2(score_ref[step * PAIR : (step + 1) * PAIR, :] - top)
        score_ref[step * PAIR : (step + 1) * PAIR, :] = weight
        total = total + jnp.sum(weight, axis=0, keepdims=True)
    share = 1.0 / total
    zero = jnp.zeros((), jnp.bfloat16)
    attn = jnp.zeros((HEAD, width), jnp.float32)
    for step, unit in enumerate(unit_of):
        prob = (score_ref[step * PAIR : (step + 1) * PAIR, :] * share).astype(jnp.bfloat16)
        attn = attn + dot(others_ref[unit, :, HEAD:], prob, TN)
        given_ref[unit, :, HEAD:] = dot(prob, grads, NN).astype(jnp.bfloat16)
    prob = score_ref[3 * PAIR :, :] * share
    prob_own = jnp.where(near, prob, 0.0).astype(jnp.bfloat16)
    prob_far = jnp.where(near, 0.0, prob).astype(jnp.bfloat16)
    attn = attn + dot(own_ref[:, HEAD:], prob_own, TN) + dot(far_ref[:, HEAD:], prob_far, TN)
    kept_ref[:, HEAD:] = dot(prob_own, grads, NN)
    back_ref[:, HEAD:] = dot(prob_far, grads, NN)
    attn = attn.astype(jnp.bfloat16).astype(jnp.float32)
    grads_t = grads.astype(jnp.float32).T
    delta = jnp.sum(attn * grads_t, axis=0, keepdims=True)
    attn_rows = attn.T.astype(jnp.bfloat16)
    out_ref[:, :HEAD] = attn_rows[:PAIR]
    out_ref[:, HEAD : 2 * HEAD] = attn_rows[PAIR:]
    scaled = share * SCALE
    query_grad = jnp.zeros((HEAD, width), jnp.float32)
    for step, unit in enumerate(unit_of):
        prob = score_ref[step * PAIR : (step + 1) * PAIR, :] * scaled
        change = (prob * (dot(others_ref[unit, :, HEAD:], grads, NT) - delta)).astype(jnp.bfloat16)
        query_grad = query_grad + dot(others_ref[unit, :, :HEAD], change, TN)
        given_ref[unit, :, :HEAD] = dot(change, queries, NN).astype(jnp.bfloat16)
    prob = score_ref[3 * PAIR :, :] * scaled
    grad_own = dot(own_ref[:, HEAD:], grads, NT)
    grad_far = dot(far_ref[:, HEAD:], grads, NT)
    change = prob * (jnp.where(near, grad_own, grad_far) - delta)
    change_own = jnp.where(near, change, 0.0).astype(jnp.bfloat16)
    change_far = jnp.where(near, 0.0, change).astype(jnp.bfloat16)
    query_grad = query_grad + dot(own_ref[:, :HEAD], change_own, TN)
    query_grad = query_grad + dot(far_ref[:, :HEAD], change_far, TN)
    kept_ref[:, :HEAD] = dot(change_own, queries, NN)
    back_ref[:, :HEAD] = dot(change_far, queries, NN)
    given_ref[here] = jnp.zeros((PAIR, 2 * HEAD), jnp.bfloat16)
    grad_rows = query_grad.T.astype(jnp.bfloat16)
    out_ref[:, 2 * HEAD : 3 * HEAD] = grad_rows[:PAIR]
    out_ref[:, 3 * HEAD :] = grad_rows[PAIR:]
    parts(out_ref, swap_ref, step_ref, skip_ref)


def parts(rows_ref, swap_ref, step_ref, skip_ref):
    member = lax.axis_index("yl")
    start = pl.multiple_of(jnp.where(member == 0, PAIR - SWAP, 0), 16)
    low = pl.multiple_of(jnp.where(member == 0, 0, PAIR - EDGE), 16)
    high = pl.multiple_of(jnp.where(member == 0, PAIR - EDGE, 0), 16)
    swap_ref[...] = rows_ref[pl.ds(start, SWAP), :]
    step_ref[...] = rows_ref[pl.ds(low, EDGE), :]
    skip_ref[...] = rows_ref[pl.ds(high, EDGE), :]


def gather_kernel(arrived_ref, kept_ref, back_ref, own_ref, send_ref):
    here = lax.axis_index("xh") * 2 + lax.axis_index("yh")
    own_ref[...] = kept_ref[...]
    send = back_ref[...]
    own = kept_ref[...]
    for unit in range(UNITS):
        part = arrived_ref[unit].astype(jnp.float32)
        own = own + jnp.where(unit > here, part, 0.0)
        send = send + jnp.where(unit < here, part, 0.0)
    own_ref[...] = own
    send_ref[...] = send.astype(jnp.bfloat16)


def total_kernel(own_ref, back_ref, out_ref, swap_ref, step_ref, skip_ref):
    out_ref[...] = (own_ref[...] + back_ref[...].astype(jnp.float32)).astype(jnp.bfloat16)
    parts(out_ref, swap_ref, step_ref, skip_ref)


def place_kernel(offsets_ref, rows_ref, swap_ref, step_ref, skip_ref, first_ref, second_ref):
    pair = pair_index()
    member = lax.axis_index("yl")
    start = offsets_ref[2 * pair + member]
    end = offsets_ref[2 * pair + member + 1]
    slot = lax.broadcasted_iota(jnp.int32, (SLOTS, 1), 0)
    place = slot + (start - pair * PAIR)
    inside = (place >= 0) & (place < PAIR)
    edge = place + jnp.where(member == 0, EDGE, -PAIR)
    live = slot < end - start
    mine = jnp.where(live, jnp.where(inside, place, PAIR + edge), -1)
    theirs = place - jnp.where(member == 0, 0, PAIR - SWAP)
    theirs = jnp.where(live, jnp.where(inside, theirs, SWAP + edge), -1)
    full = rows_ref.shape[1]
    width = full // 2
    pad = jnp.zeros((80, full), jnp.bfloat16)
    own = picked(SLOTS, mine, jnp.concatenate([rows_ref[...], skip_ref[...], pad], axis=0))
    other = picked(
        SLOTS, theirs, jnp.concatenate([swap_ref[...], step_ref[...], pad[:32]], axis=0)
    )

    @pl.when(member == 0)
    def _():
        first_ref[:, :width] = own[:, :width]
        first_ref[:, width:] = other[:, :width]
        second_ref[:, :width] = own[:, width:]
        second_ref[:, width:] = other[:, width:]

    @pl.when(member == 1)
    def _():
        first_ref[:, :width] = other[:, :width]
        first_ref[:, width:] = own[:, :width]
        second_ref[:, :width] = other[:, width:]
        second_ref[:, width:] = own[:, width:]


def placed(rows, swap, step, skip, offsets, name):
    blocks = range(2 * PAIRS)
    swap = lax.ppermute(swap, SEQ_AXES, [(j, j ^ 1) for j in blocks])
    step = lax.ppermute(
        step,
        SEQ_AXES,
        [(j, j + 2 * (j % 2) - 1) for j in blocks if 0 <= j + 2 * (j % 2) - 1 < 2 * PAIRS],
    )
    skip = lax.ppermute(
        skip,
        SEQ_AXES,
        [(j, j + 2 - 4 * (j % 2)) for j in blocks if 0 <= j + 2 - 4 * (j % 2) < 2 * PAIRS],
    )
    width = rows.shape[1]
    return call(
        place_kernel,
        [shape(SLOTS, width), shape(SLOTS, width)],
        [smem(), vmem(), vmem(), vmem(), vmem()],
        name=name,
    )(offsets, rows, swap, step, skip)


def on_device(q_old, k_old, value_old_layout, dout_old, old_offsets, new_offsets):
    pair_rows = pack(k_old, value_old_layout, "pack_keys")
    pair_rows = lax.all_to_all(pair_rows, GROUP_AXES, 0, 0, tiled=True)
    query_rows = pack(q_old, dout_old, "pack_queries")
    query_rows = lax.all_to_all(query_rows, GROUP_AXES, 0, 0, tiled=True)
    own = even_rows(pair_rows.reshape(2 * SLOTS, 2 * HEAD), old_offsets, "keys")
    far = lax.ppermute(own, "z", [(i, i + 1) for i in range(15)])
    chosen = call(choose_kernel, shape(UNITS, PAIR, 2 * HEAD), [vmem(), vmem()], name="choose")(own, far)
    others = lax.all_to_all(chosen, PLANE_AXES, 0, 0, tiled=True)
    rows = even_rows(query_rows.reshape(2 * SLOTS, 4 * HEAD), old_offsets, "queries")
    wide = 4 * HEAD
    results, swap, step, skip, given, kept, back = call(
        attend_kernel,
        [
            shape(PAIR, wide),
            shape(SWAP, wide),
            shape(EDGE, wide),
            shape(EDGE, wide),
            shape(UNITS, PAIR, 2 * HEAD),
            shape(PAIR, 2 * HEAD, dtype=jnp.float32),
            shape(PAIR, 2 * HEAD, dtype=jnp.float32),
        ],
        [vmem(), vmem(), vmem(), vmem()],
        [pltpu.VMEM((UNITS * PAIR, 2 * PAIR), jnp.float32)],
        name="attend",
        flops=10**9,
    )(rows, own, far, others)
    arrived = lax.all_to_all(given, PLANE_AXES, 0, 0, tiled=True)
    own_grad, send = call(
        gather_kernel,
        [shape(PAIR, 2 * HEAD, dtype=jnp.float32), shape(PAIR, 2 * HEAD)],
        [vmem(), vmem(), vmem()],
        name="gather",
    )(arrived, kept, back)
    returned = lax.ppermute(send, "z", [(i + 1, i) for i in range(15)])
    attn_out, grad_query_out = placed(results, swap, step, skip, new_offsets, "place_rows")
    narrow = 2 * HEAD
    pair_grads = call(
        total_kernel,
        [shape(PAIR, narrow), shape(SWAP, narrow), shape(EDGE, narrow), shape(EDGE, narrow)],
        [vmem(), vmem()],
        name="total",
    )(own_grad, returned)
    grad_key_out, grad_value_out = placed(*pair_grads, new_offsets, "place_grads")
    return attn_out, grad_query_out, grad_key_out, grad_value_out


def solution(mesh):
    cut = Mesh(mesh.devices.reshape(16, 2, 2, 2, 2, 2), AXES)
    rows = P(AXES, None)
    return jax.shard_map(
        on_device,
        mesh=cut,
        in_specs=(rows, rows, rows, rows, P(), P()),
        out_specs=(P(SEQ_AXES, ("xl", "c")),) * 4,
        check_vma=False,
    )
```

time: 178 us -> 142 us (0.80)
  the two profiles are of different devices: /device:TPU:252 before, /device:TPU:96 now
where the time goes in v1:
time: 142 us; the launch traced here: 141 us
  starting transfers between devices  70.7 us (50%)
  Pallas kernels  26.1 us (18%)
  blocking collectives  19.8 us (14%)
  waiting for transfers between devices  17.2 us (12%)
  local copies, waits for them, and re-layouts  6.15 us (4%)
    all_to_all x1, blocking collectives, on_device(): arrived = lax.all_to_all(given, PLANE_AXES, 0, 0, tiled=True)  19.8 us
    ppermute x2, starting transfers between devices, even_rows(): lax.ppermute(left, PAIR_AXES, [(i + 1, i) for i in range(PAIRS - 1)])  11.1 us
    ppermute x2, starting transfers between devices, even_rows(): lax.ppermute(right, PAIR_AXES, [(i, i + 1) for i in range(PAIRS - 1)])  10.2 us
    all_to_all x1, starting transfers between devices, on_device(): others = lax.all_to_all(chosen, PLANE_AXES, 0, 0, tiled=True)  9.26 us
    ppermute x2, starting transfers between devices, placed(): lax.ppermute(skip, SEQ_AXES, [(j, j + 2 - 4 * (j % 2)) for j in blocks if...  8.88 us
    ppermute x2, starting transfers between devices, placed(): lax.ppermute(step, SEQ_AXES, [(j, j + 2 * (j % 2) - 1) for j in blocks if...  8.22 us
    ppermute x2, starting transfers between devices, placed(): swap = lax.ppermute(swap, SEQ_AXES, [(j, j ^ 1) for j in blocks])  7.67 us
    ppermute x1, starting transfers between devices, on_device(): far = lax.ppermute(own, 'z', [(i, i + 1) for i in range(15)])  6.23 us
  transfers between devices with their start and end apart: 15, of which 8 were waited for; matrix products, arithmetic and copies ran while one was open for 0% of the time, Pallas kernels for 11%

profile of v1, /device:TPU:96, one launch (start us, length us, event | category | flops | bytes accessed | tf_op | source)
XLA Modules:
  0.0 140.8 jit_solution(2987600070096750079)
XLA Ops:
  0.6 1.7 %pack_keys.1 = bf16[8,56,256]{2,1,0:T(8,128)(2,1)} custom-call(bf16[56,1024]{1,0:T(8,128)(2,1)} %first_ref.3, bf16[56,1024]{1,0:T(8,128)(2,1)} %second_ref.3), custom_call_target="tpu_custom_call" | custom-call | bytes 1048576 | tf_op jit(solution)/shard_map/pack_keys/pallas_call | solution.py:80
  2.3 3.8 %all-to-all-start.1 = ((bf16[8,56,256]{2,1,0:T(8,128)(2,1)}), bf16[8,56,256]{2,1,0:T(8,128)(2,1)S(1)}, u32[]{:S(2)}, u32[]{:S(2)}) async-start(bf16[8,56,256]{2,1,0:T(8,128)(2,1)} %pack_keys.1), calls=%async_computation.1 | async-start | bytes 458752 | tf_op jit(solution)/shard_map/all_to_all | solution.py:310
  6.1 1.9 %pack_queries.1 = bf16[8,56,512]{2,1,0:T(8,128)(2,1)} custom-call(bf16[56,2048]{1,0:T(8,128)(2,1)} %first_ref.2, bf16[56,2048]{1,0:T(8,128)(2,1)} %second_ref.2), custom_call_target="tpu_custom_call" | custom-call | bytes 1048576 | tf_op jit(solution)/shard_map/pack_queries/pallas_call | solution.py:80
  8.0 4.7 %all-to-all-done.1 = bf16[8,56,256]{2,1,0:T(8,128)(2,1)S(1)} async-done(((bf16[8,56,256]{2,1,0:T(8,128)(2,1)}), bf16[8,56,256]{2,1,0:T(8,128)(2,1)S(1)}, u32[]{:S(2)}, u32[]{:S(2)}) %all-to-all-start.1) | async-done | bytes 229408 | tf_op jit(solution)/shard_map/all_to_all | solution.py:310
  12.6 0.7 copy-done.1
  13.3 3.5 %all-to-all-start = ((bf16[8,56,512]{2,1,0:T(8,128)(2,1)}), bf16[8,56,512]{2,1,0:T(8,128)(2,1)S(1)}, u32[]{:S(2)}, u32[]{:S(2)}) async-start(bf16[8,56,512]{2,1,0:T(8,128)(2,1)} %pack_queries.1), calls=%async_computation | async-start | bytes 917504 | tf_op jit(solution)/shard_map/all_to_all | solution.py:312
  16.8 1.7 %keys_edges.1 = (bf16[48,256]{1,0:T(8,128)(2,1)}, bf16[48,256]{1,0:T(8,128)(2,1)}) custom-call(s32[129]{0:T(256)} %offsets_ref.9, bf16[448,256]{1,0:T(8,128)(2,1)} %bitcast.4), custom_call_target="tpu_custom_call" | custom-call | bytes 1048576 | tf_op jit(solution)/shard_map/keys_edges/pallas_call | solution.py:121
  18.6 4.8 %collective-permute-start.2 = (bf16[48,256]{1,0:T(8,128)(2,1)}, bf16[48,256]{1,0:T(8,128)(2,1)S(1)}, u32[]{:S(2)}, u32[]{:S(2)}) collective-permute-start(bf16[48,256]{1,0:T(8,128)(2,1)} %get-tuple-element.27), channel_id=1, source_target_pairs={{0,8},{8,16},{16,24},{24,32},{32,40},{40,48},{48,56},{56,64},{64,7... | collective-permute-start | bytes 73736 | tf_op jit(solution)/shard_map/ppermute | solution.py:128
  23.4 5.8 %collective-permute-start.3 = (bf16[48,256]{1,0:T(8,128)(2,1)}, bf16[48,256]{1,0:T(8,128)(2,1)S(1)}, u32[]{:S(2)}, u32[]{:S(2)}) collective-permute-start(bf16[48,256]{1,0:T(8,128)(2,1)} %get-tuple-element.28), channel_id=1, source_target_pairs={{8,0},{16,8},{24,16},{32,24},{40,32},{48,40},{56,48},{64,56},{72,6... | collective-permute-start | bytes 73736 | tf_op jit(solution)/shard_map/ppermute | solution.py:127
  29.2 0.1 collective-permute-done.2.left_ref
  29.3 1.6 %collective-permute-done.3.right_ref = bf16[48,256]{1,0:T(8,128)(2,1)S(1)} collective-permute-done((bf16[48,256]{1,0:T(8,128)(2,1)}, bf16[48,256]{1,0:T(8,128)(2,1)S(1)}, u32[]{:S(2)}, u32[]{:S(2)}) %collective-permute-start.3) | collective-permute-done | bytes 24608 | tf_op jit(solution)/shard_map/ppermute | solution.py:127
  30.9 0.6 copy-done.14
  31.5 1.9 %keys_even.1.own_ref = bf16[256,256]{1,0:T(8,128)(2,1)} custom-call(s32[129]{0:T(256)} %offsets_ref.9, bf16[448,256]{1,0:T(8,128)(2,1)} %bitcast.5, bf16[48,256]{1,0:T(8,128)(2,1)} %copy-done.13, bf16[48,256]{1,0:T(8,128)(2,1)} %copy-done.14), custom_call_target="tpu_custom_call" | custom-call | bytes 1048576 | tf_op jit(solution)/shard_map/keys_even/pallas_call | solution.py:129
  33.5 6.2 %collective-permute-start.4 = (bf16[256,256]{1,0:T(8,128)(2,1)}, bf16[256,256]{1,0:T(8,128)(2,1)S(1)}, u32[]{:S(2)}, u32[]{:S(2)}) collective-permute-start(bf16[256,256]{1,0:T(8,128)(2,1)} %keys_even.1.own_ref), channel_id=1, source_target_pairs={{0,32},{32,64},{64,96},{96,128},{128,160},{160,192},{192,224},{224... | collective-permute-start | bytes 393224 | tf_op jit(solution)/shard_map/ppermute | solution.py:314
  39.7 2.8 %collective-permute-done.4.far_ref = bf16[256,256]{1,0:T(8,128)(2,1)S(1)} collective-permute-done((bf16[256,256]{1,0:T(8,128)(2,1)}, bf16[256,256]{1,0:T(8,128)(2,1)S(1)}, u32[]{:S(2)}, u32[]{:S(2)}) %collective-permute-start.4) | collective-permute-done | bytes 131104 | tf_op jit(solution)/shard_map/ppermute | solution.py:314
  42.5 0.7 copy-done.5
  43.2 1.8 %choose.1 = bf16[4,256,256]{2,1,0:T(8,128)(2,1)} custom-call(bf16[256,256]{1,0:T(8,128)(2,1)} %keys_even.1.own_ref, bf16[256,256]{1,0:T(8,128)(2,1)} %copy-done.5), custom_call_target="tpu_custom_call" | custom-call | bytes 1048576 | tf_op jit(solution)/shard_map/choose/pallas_call | solution.py:315
  45.0 0.8 copy-done
  45.7 9.3 %all-to-all-start.2 = ((bf16[4,256,256]{2,1,0:T(8,128)(2,1)}), bf16[4,256,256]{2,1,0:T(8,128)(2,1)S(1)}, u32[]{:S(2)}, u32[]{:S(2)}) async-start(bf16[4,256,256]{2,1,0:T(8,128)(2,1)} %choose.1), calls=%async_computation.2 | async-start | bytes 1048576 | tf_op jit(solution)/shard_map/all_to_all | solution.py:316
  55.0 1.9 %queries_edges.1 = (bf16[48,512]{1,0:T(8,128)(2,1)}, bf16[48,512]{1,0:T(8,128)(2,1)}) custom-call(s32[129]{0:T(256)} %offsets_ref.9, bf16[448,512]{1,0:T(8,128)(2,1)} %bitcast.2), custom_call_target="tpu_custom_call" | custom-call | bytes 1048576 | tf_op jit(solution)/shard_map/queries_edges/pallas_call | solution.py:121
  56.9 5.4 %collective-permute-start = (bf16[48,512]{1,0:T(8,128)(2,1)}, bf16[48,512]{1,0:T(8,128)(2,1)S(1)}, u32[]{:S(2)}, u32[]{:S(2)}) collective-permute-start(bf16[48,512]{1,0:T(8,128)(2,1)} %get-tuple-element.25), channel_id=1, source_target_pairs={{0,8},{8,16},{16,24},{24,32},{32,40},{40,48},{48,56},{56,64},{64,7... | collective-permute-start | bytes 147464 | tf_op jit(solution)/shard_map/ppermute | solution.py:128
  62.3 5.2 %collective-permute-start.1 = (bf16[48,512]{1,0:T(8,128)(2,1)}, bf16[48,512]{1,0:T(8,128)(2,1)S(1)}, u32[]{:S(2)}, u32[]{:S(2)}) collective-permute-start(bf16[48,512]{1,0:T(8,128)(2,1)} %get-tuple-element.26), channel_id=1, source_target_pairs={{8,0},{16,8},{24,16},{32,24},{40,32},{48,40},{56,48},{64,56},{72,6... | collective-permute-start | bytes 147464 | tf_op jit(solution)/shard_map/ppermute | solution.py:127
  67.5 0.3 collective-permute-done.left_ref
  67.9 2.1 %collective-permute-done.1.right_ref = bf16[48,512]{1,0:T(8,128)(2,1)S(1)} collective-permute-done((bf16[48,512]{1,0:T(8,128)(2,1)}, bf16[48,512]{1,0:T(8,128)(2,1)S(1)}, u32[]{:S(2)}, u32[]{:S(2)}) %collective-permute-start.1) | collective-permute-done | bytes 49184 | tf_op jit(solution)/shard_map/ppermute | solution.py:127
  70.0 0.6 copy-done.10
  70.6 2.2 %queries_even.1.rows_ref = bf16[256,512]{1,0:T(8,128)(2,1)} custom-call(s32[129]{0:T(256)} %offsets_ref.9, bf16[448,512]{1,0:T(8,128)(2,1)} %bitcast.3, bf16[48,512]{1,0:T(8,128)(2,1)} %copy-done.9, bf16[48,512]{1,0:T(8,128)(2,1)} %copy-done.10), custom_call_target="tpu_custom_call" | custom-call | bytes 1048576 | tf_op jit(solution)/shard_map/queries_even/pallas_call | solution.py:129
  72.8 0.8 copy-done.2
  73.6 5.1 %attend.1 = (bf16[256,512]{1,0:T(8,128)(2,1)}, bf16[176,512]{1,0:T(8,128)(2,1)}, bf16[48,512]{1,0:T(8,128)(2,1)}, bf16[48,512]{1,0:T(8,128)(2,1)}, bf16[4,256,25...) custom-call(bf16[256,512]{1,0:T(8,128)(2,1)} %queries_even.1.rows_ref, ...), custom_call_target="tpu_custom_call" | custom-call | flops 1000000000 | bytes 1048576 | tf_op jit(solution)/shard_map/attend/pallas_call | solution.py:319
  78.8 19.8 %all_to_all.20.arrived_ref = bf16[4,256,256]{2,1,0:T(8,128)(2,1)} all-to-all(bf16[4,256,256]{2,1,0:T(8,128)(2,1)} %get-tuple-element.35), channel_id=1, replica_groups=mesh['z'=16,'xh'=2,'yh'=2,'yl'=2,'xl'=2,'c'=2] {'xh','yh'}, dimensions={0} | all-to-all | bytes 1048576 | tf_op jit(solution)/shard_map/all_to_all | solution.py:335
  98.5 2.1 %gather.1 = (f32[256,256]{1,0:T(8,128)}, bf16[256,256]{1,0:T(8,128)(2,1)}) custom-call(bf16[4,256,256]{2,1,0:T(8,128)(2,1)} %all_to_all.20.arrived_ref, f32[256,256]{1,0:T(8,128)} %get-tuple-element.36.kept_ref, f32[256,256]{1,0:T(8,128)} %get-tuple-element.37.back_ref), custom_call_target="tpu_custom_call" | custom-call | bytes 1048576 | tf_op jit(solution)/shard_map/gather/pallas_call | solution.py:336
  100.6 1.9 %collective-permute-start.8 = (bf16[256,256]{1,0:T(8,128)(2,1)}, bf16[256,256]{1,0:T(8,128)(2,1)S(1)}, u32[]{:S(2)}, u32[]{:S(2)}) collective-permute-start(bf16[256,256]{1,0:T(8,128)(2,1)} %get-tuple-element.39), channel_id=1, source_target_pairs={{32,0},{64,32},{96,64},{128,96},{160,128},{192,160},{224,192},{256... | collective-permute-start | bytes 393224 | tf_op jit(solution)/shard_map/ppermute | solution.py:342
  102.5 3.8 %collective-permute-start.5 = (bf16[176,512]{1,0:T(8,128)(2,1)S(1)}, bf16[176,512]{1,0:T(8,128)(2,1)S(1)}, u32[]{:S(2)}, u32[]{:S(2)}) collective-permute-start(bf16[176,512]{1,0:T(8,128)(2,1)S(1)} %copy-done.15), channel_id=1, source_target_pairs={{0,4},{4,0},{8,12},{12,8},{16,20},{20,16},{24,28},{28,24},{32,36},... | collective-permute-start | bytes 540680 | tf_op jit(solution)/shard_map/ppermute | solution.py:288
  106.4 2.5 %collective-permute-done.8.back_ref = bf16[256,256]{1,0:T(8,128)(2,1)S(1)} collective-permute-done((bf16[256,256]{1,0:T(8,128)(2,1)}, bf16[256,256]{1,0:T(8,128)(2,1)S(1)}, u32[]{:S(2)}, u32[]{:S(2)}) %collective-permute-start.8) | collective-permute-done | bytes 131104 | tf_op jit(solution)/shard_map/ppermute | solution.py:342
  108.9 0.7 copy-done.4
  109.6 1.7 %total.1 = (bf16[256,256]{1,0:T(8,128)(2,1)}, bf16[176,256]{1,0:T(8,128)(2,1)}, bf16[48,256]{1,0:T(8,128)(2,1)}, bf16[48,256]{1,0:T(8,128)(2,1)}) custom-call(f32[256,256]{1,0:T(8,128)} %get-tuple-element.38.own_ref, bf16[256,256]{1,0:T(8,128)(2,1)} %copy-done.4), custom_call_target="tpu_custom_call" | custom-call | bytes 1048576 | tf_op jit(solution)/shard_map/total/pallas_call | solution.py:345
  111.3 3.8 %collective-permute-start.9 = (bf16[176,256]{1,0:T(8,128)(2,1)}, bf16[176,256]{1,0:T(8,128)(2,1)S(1)}, u32[]{:S(2)}, u32[]{:S(2)}) collective-permute-start(bf16[176,256]{1,0:T(8,128)(2,1)} %get-tuple-element.41), channel_id=1, source_target_pairs={{0,4},{4,0},{8,12},{12,8},{16,20},{20,16},{24,28},{28,24},{32,36},... | collective-permute-start | bytes 270344 | tf_op jit(solution)/shard_map/ppermute | solution.py:288
  115.1 1.9 %collective-permute-start.6 = (bf16[48,512]{1,0:T(8,128)(2,1)S(1)}, bf16[48,512]{1,0:T(8,128)(2,1)S(1)}, u32[]{:S(2)}, u32[]{:S(2)}) collective-permute-start(bf16[48,512]{1,0:T(8,128)(2,1)S(1)} %copy-done.17), channel_id=1, source_target_pairs={{4,8},{8,4},{12,16},{16,12},{20,24},{24,20},{28,32},{32,28},{36,40... | collective-permute-start | bytes 147464 | tf_op jit(solution)/shard_map/ppermute | solution.py:289
  117.0 4.1 %collective-permute-start.7 = (bf16[48,512]{1,0:T(8,128)(2,1)S(1)}, bf16[48,512]{1,0:T(8,128)(2,1)S(1)}, u32[]{:S(2)}, u32[]{:S(2)}) collective-permute-start(bf16[48,512]{1,0:T(8,128)(2,1)S(1)} %copy-done.16), channel_id=1, source_target_pairs={{0,8},{8,16},{12,4},{16,24},{20,12},{24,32},{28,20},{32,40},{36,28... | collective-permute-start | bytes 147464 | tf_op jit(solution)/shard_map/ppermute | solution.py:294
  121.1 6.3 %collective-permute-start.10 = (bf16[48,256]{1,0:T(8,128)(2,1)}, bf16[48,256]{1,0:T(8,128)(2,1)S(1)}, u32[]{:S(2)}, u32[]{:S(2)}) collective-permute-start(bf16[48,256]{1,0:T(8,128)(2,1)} %get-tuple-element.42), channel_id=1, source_target_pairs={{4,8},{8,4},{12,16},{16,12},{20,24},{24,20},{28,32},{32,28},{36,40... | collective-permute-start | bytes 73736 | tf_op jit(solution)/shard_map/ppermute | solution.py:289
  127.4 0.0 copy-start.7
  127.4 4.8 %collective-permute-start.11 = (bf16[48,256]{1,0:T(8,128)(2,1)}, bf16[48,256]{1,0:T(8,128)(2,1)S(1)}, u32[]{:S(2)}, u32[]{:S(2)}) collective-permute-start(bf16[48,256]{1,0:T(8,128)(2,1)} %get-tuple-element.43), channel_id=1, source_target_pairs={{0,8},{8,16},{12,4},{16,24},{20,12},{24,32},{28,20},{32,40},{36,28... | collective-permute-start | bytes 73736 | tf_op jit(solution)/shard_map/ppermute | solution.py:294
  132.3 0.6 copy-done.8
  132.9 0.1 copy-done.3
  133.0 2.2 %place_rows.1 = (bf16[224,512]{1,0:T(8,128)(2,1)}, bf16[224,512]{1,0:T(8,128)(2,1)}) custom-call(s32[129]{0:T(256)} %offsets_ref.11, bf16[256,512]{1,0:T(8,128)(2,1)} %get-tuple-element.29.rows_ref, bf16[176,512]{1,0:T(8,128)(2,1)} %copy-done.3, bf16[48,512]{1,0:T(8,128)(2,1)} %copy-done.7, bf16[48,512]{1,0:T(8,128)(2,1)} %copy-done.8), custom_call_target="tpu_custom_call" | custom-call | bytes 1048576 | tf_op jit(solution)/shard_map/place_rows/pallas_call | solution.py:300
  135.2 3.0 %collective-permute-done.11.skip_ref = bf16[48,256]{1,0:T(8,128)(2,1)S(1)} collective-permute-done((bf16[48,256]{1,0:T(8,128)(2,1)}, bf16[48,256]{1,0:T(8,128)(2,1)S(1)}, u32[]{:S(2)}, u32[]{:S(2)}) %collective-permute-start.11) | collective-permute-done | bytes 24608 | tf_op jit(solution)/shard_map/ppermute | solution.py:294
  138.2 0.6 copy-done.12
  138.8 0.0 copy-done.6
  138.8 2.0 %place_grads.1 = (bf16[224,256]{1,0:T(8,128)(2,1)}, bf16[224,256]{1,0:T(8,128)(2,1)}) custom-call(s32[129]{0:T(256)} %offsets_ref.11, bf16[256,256]{1,0:T(8,128)(2,1)} %get-tuple-element.40.rows_ref, bf16[176,256]{1,0:T(8,128)(2,1)} %copy-done.6, bf16[48,256]{1,0:T(8,128)(2,1)} %copy-done.11, bf16[48,256]{1,0:T(8,128)(2,1)} %copy-done.12), custom_call_target="tpu_custom_call" | custom-call | bytes 1048576 | tf_op jit(solution)/shard_map/place_grads/pallas_call | solution.py:300
  (31 shorter events, 0.1 us)
Async XLA Ops:
  2.3 10.3 %all-to-all-start.1 = ((bf16[8,56,256]{2,1,0:T(8,128)(2,1)}), bf16[8,56,256]{2,1,0:T(8,128)(2,1)S(1)}, u32[]{:S(2)}, u32[]{:S(2)}) async-start(bf16[8,56,256]{2,1,0:T(8,128)(2,1)} %pack_keys.1), calls=%async_computation.1 | async-start | bytes 458752 | tf_op jit(solution)/shard_map/all_to_all | solution.py:310
  12.6 0.7 copy-start.1
  13.3 31.6 %all-to-all-start = ((bf16[8,56,512]{2,1,0:T(8,128)(2,1)}), bf16[8,56,512]{2,1,0:T(8,128)(2,1)S(1)}, u32[]{:S(2)}, u32[]{:S(2)}) async-start(bf16[8,56,512]{2,1,0:T(8,128)(2,1)} %pack_queries.1), calls=%async_computation | async-start | bytes 917504 | tf_op jit(solution)/shard_map/all_to_all | solution.py:312
  18.6 10.7 %collective-permute-start.2 = (bf16[48,256]{1,0:T(8,128)(2,1)}, bf16[48,256]{1,0:T(8,128)(2,1)S(1)}, u32[]{:S(2)}, u32[]{:S(2)}) collective-permute-start(bf16[48,256]{1,0:T(8,128)(2,1)} %get-tuple-element.27), channel_id=1, source_target_pairs={{0,8},{8,16},{16,24},{24,32},{32,40},{40,48},{48,56},{56,64},{64,7... | collective-permute-start | bytes 73736 | tf_op jit(solution)/shard_map/ppermute | solution.py:128
  23.4 7.6 %collective-permute-start.3 = (bf16[48,256]{1,0:T(8,128)(2,1)}, bf16[48,256]{1,0:T(8,128)(2,1)S(1)}, u32[]{:S(2)}, u32[]{:S(2)}) collective-permute-start(bf16[48,256]{1,0:T(8,128)(2,1)} %get-tuple-element.28), channel_id=1, source_target_pairs={{8,0},{16,8},{24,16},{32,24},{40,32},{48,40},{56,48},{64,56},{72,6... | collective-permute-start | bytes 73736 | tf_op jit(solution)/shard_map/ppermute | solution.py:127
  29.3 1.6 %copy-start.13 = (bf16[48,256]{1,0:T(8,128)(2,1)}, bf16[48,256]{1,0:T(8,128)(2,1)S(1)}, u32[]{:S(2)}) copy-start(bf16[48,256]{1,0:T(8,128)(2,1)S(1)} %collective-permute-done.2.left_ref) | copy-start | bytes 73732
  30.9 0.6 copy-start.14
  33.5 9.1 %collective-permute-start.4 = (bf16[256,256]{1,0:T(8,128)(2,1)}, bf16[256,256]{1,0:T(8,128)(2,1)S(1)}, u32[]{:S(2)}, u32[]{:S(2)}) collective-permute-start(bf16[256,256]{1,0:T(8,128)(2,1)} %keys_even.1.own_ref), channel_id=1, source_target_pairs={{0,32},{32,64},{64,96},{96,128},{128,160},{160,192},{192,224},{224... | collective-permute-start | bytes 393224 | tf_op jit(solution)/shard_map/ppermute | solution.py:314
  42.5 0.7 copy-start.5
  45.0 0.8 copy-start
  45.7 27.0 %all-to-all-start.2 = ((bf16[4,256,256]{2,1,0:T(8,128)(2,1)}), bf16[4,256,256]{2,1,0:T(8,128)(2,1)S(1)}, u32[]{:S(2)}, u32[]{:S(2)}) async-start(bf16[4,256,256]{2,1,0:T(8,128)(2,1)} %choose.1), calls=%async_computation.2 | async-start | bytes 1048576 | tf_op jit(solution)/shard_map/all_to_all | solution.py:316
  56.9 11.0 %collective-permute-start = (bf16[48,512]{1,0:T(8,128)(2,1)}, bf16[48,512]{1,0:T(8,128)(2,1)S(1)}, u32[]{:S(2)}, u32[]{:S(2)}) collective-permute-start(bf16[48,512]{1,0:T(8,128)(2,1)} %get-tuple-element.25), channel_id=1, source_target_pairs={{0,8},{8,16},{16,24},{24,32},{32,40},{40,48},{48,56},{56,64},{64,7... | collective-permute-start | bytes 147464 | tf_op jit(solution)/shard_map/ppermute | solution.py:128
  62.3 7.7 %collective-permute-start.1 = (bf16[48,512]{1,0:T(8,128)(2,1)}, bf16[48,512]{1,0:T(8,128)(2,1)S(1)}, u32[]{:S(2)}, u32[]{:S(2)}) collective-permute-start(bf16[48,512]{1,0:T(8,128)(2,1)} %get-tuple-element.26), channel_id=1, source_target_pairs={{8,0},{16,8},{24,16},{32,24},{40,32},{48,40},{56,48},{64,56},{72,6... | collective-permute-start | bytes 147464 | tf_op jit(solution)/shard_map/ppermute | solution.py:127
  67.9 2.1 %copy-start.9 = (bf16[48,512]{1,0:T(8,128)(2,1)}, bf16[48,512]{1,0:T(8,128)(2,1)S(1)}, u32[]{:S(2)}) copy-start(bf16[48,512]{1,0:T(8,128)(2,1)S(1)} %collective-permute-done.left_ref) | copy-start | bytes 147460
  70.0 0.6 copy-start.10
  72.8 0.8 copy-start.2
  98.5 4.0 %copy-start.15 = (bf16[176,512]{1,0:T(8,128)(2,1)S(1)}, bf16[176,512]{1,0:T(8,128)(2,1)}, u32[]{:S(2)}) copy-start(bf16[176,512]{1,0:T(8,128)(2,1)} %get-tuple-element.30) | copy-start | bytes 540676
  100.6 8.3 %collective-permute-start.8 = (bf16[256,256]{1,0:T(8,128)(2,1)}, bf16[256,256]{1,0:T(8,128)(2,1)S(1)}, u32[]{:S(2)}, u32[]{:S(2)}) collective-permute-start(bf16[256,256]{1,0:T(8,128)(2,1)} %get-tuple-element.39), channel_id=1, source_target_pairs={{32,0},{64,32},{96,64},{128,96},{160,128},{192,160},{224,192},{256... | collective-permute-start | bytes 393224 | tf_op jit(solution)/shard_map/ppermute | solution.py:342
  102.5 29.7 %collective-permute-start.5 = (bf16[176,512]{1,0:T(8,128)(2,1)S(1)}, bf16[176,512]{1,0:T(8,128)(2,1)S(1)}, u32[]{:S(2)}, u32[]{:S(2)}) collective-permute-start(bf16[176,512]{1,0:T(8,128)(2,1)S(1)} %copy-done.15), channel_id=1, source_target_pairs={{0,4},{4,0},{8,12},{12,8},{16,20},{20,16},{24,28},{28,24},{32,36},... | collective-permute-start | bytes 540680 | tf_op jit(solution)/shard_map/ppermute | solution.py:288
  108.9 0.7 copy-start.4
  109.5 5.6 %copy-start.17 = (bf16[48,512]{1,0:T(8,128)(2,1)S(1)}, bf16[48,512]{1,0:T(8,128)(2,1)}, u32[]{:S(2)}) copy-start(bf16[48,512]{1,0:T(8,128)(2,1)} %get-tuple-element.31) | copy-start | bytes 147460
  109.6 7.5 %copy-start.16 = (bf16[48,512]{1,0:T(8,128)(2,1)S(1)}, bf16[48,512]{1,0:T(8,128)(2,1)}, u32[]{:S(2)}) copy-start(bf16[48,512]{1,0:T(8,128)(2,1)} %get-tuple-element.32) | copy-start | bytes 147460
  111.3 26.9 %collective-permute-start.9 = (bf16[176,256]{1,0:T(8,128)(2,1)}, bf16[176,256]{1,0:T(8,128)(2,1)S(1)}, u32[]{:S(2)}, u32[]{:S(2)}) collective-permute-start(bf16[176,256]{1,0:T(8,128)(2,1)} %get-tuple-element.41), channel_id=1, source_target_pairs={{0,4},{4,0},{8,12},{12,8},{16,20},{20,16},{24,28},{28,24},{32,36},... | collective-permute-start | bytes 270344 | tf_op jit(solution)/shard_map/ppermute | solution.py:288
  115.1 12.3 %collective-permute-start.6 = (bf16[48,512]{1,0:T(8,128)(2,1)S(1)}, bf16[48,512]{1,0:T(8,128)(2,1)S(1)}, u32[]{:S(2)}, u32[]{:S(2)}) collective-permute-start(bf16[48,512]{1,0:T(8,128)(2,1)S(1)} %copy-done.17), channel_id=1, source_target_pairs={{4,8},{8,4},{12,16},{16,12},{20,24},{24,20},{28,32},{32,28},{36,40... | collective-permute-start | bytes 147464 | tf_op jit(solution)/shard_map/ppermute | solution.py:289
  117.0 15.2 %collective-permute-start.7 = (bf16[48,512]{1,0:T(8,128)(2,1)S(1)}, bf16[48,512]{1,0:T(8,128)(2,1)S(1)}, u32[]{:S(2)}, u32[]{:S(2)}) collective-permute-start(bf16[48,512]{1,0:T(8,128)(2,1)S(1)} %copy-done.16), channel_id=1, source_target_pairs={{0,8},{8,16},{12,4},{16,24},{20,12},{24,32},{28,20},{32,40},{36,28... | collective-permute-start | bytes 147464 | tf_op jit(solution)/shard_map/ppermute | solution.py:294
  121.1 14.1 %collective-permute-start.10 = (bf16[48,256]{1,0:T(8,128)(2,1)}, bf16[48,256]{1,0:T(8,128)(2,1)S(1)}, u32[]{:S(2)}, u32[]{:S(2)}) collective-permute-start(bf16[48,256]{1,0:T(8,128)(2,1)} %get-tuple-element.42), channel_id=1, source_target_pairs={{4,8},{8,4},{12,16},{16,12},{20,24},{24,20},{28,32},{32,28},{36,40... | collective-permute-start | bytes 73736 | tf_op jit(solution)/shard_map/ppermute | solution.py:289
  127.4 4.9 %copy-start.7 = (bf16[48,512]{1,0:T(8,128)(2,1)}, bf16[48,512]{1,0:T(8,128)(2,1)S(1)}, u32[]{:S(2)}) copy-start(bf16[48,512]{1,0:T(8,128)(2,1)S(1)} %collective-permute-done.6.step_ref) | copy-start | bytes 147460
  127.4 10.7 %collective-permute-start.11 = (bf16[48,256]{1,0:T(8,128)(2,1)}, bf16[48,256]{1,0:T(8,128)(2,1)S(1)}, u32[]{:S(2)}, u32[]{:S(2)}) collective-permute-start(bf16[48,256]{1,0:T(8,128)(2,1)} %get-tuple-element.43), channel_id=1, source_target_pairs={{0,8},{8,16},{12,4},{16,24},{20,12},{24,32},{28,20},{32,40},{36,28... | collective-permute-start | bytes 73736 | tf_op jit(solution)/shard_map/ppermute | solution.py:294
  132.3 0.6 copy-start.8
  132.3 0.7 copy-start.3
  135.2 3.0 %copy-start.11 = (bf16[48,256]{1,0:T(8,128)(2,1)}, bf16[48,256]{1,0:T(8,128)(2,1)S(1)}, u32[]{:S(2)}) copy-start(bf16[48,256]{1,0:T(8,128)(2,1)S(1)} %collective-permute-done.10.step_ref) | copy-start | bytes 73732
  138.2 0.6 copy-start.12
  138.2 0.6 copy-start.6

commit v2 on v1

v2 whole, which is shorter than its diff:
```python
import jax
import jax.numpy as jnp
from jax import lax
from jax.experimental import pallas as pl
from jax.experimental.pallas import tpu as pltpu
from jax.sharding import Mesh, PartitionSpec as P

PAIR = 256
SLOTS = 224
EDGE = 48
HEAD = 128
UNITS = 4
PAIRS = 64
SWAP = PAIR - 80
SCALE = 168.0 ** (-0.5)
LOG2E = 1.4426950408889634
OUTSIDE = -1e30

AXES = ("z", "xh", "yh", "yl", "xl", "c")
PAIR_AXES = ("z", "xh", "yh")
SEQ_AXES = ("z", "xh", "yh", "yl")
GROUP_AXES = ("yl", "xl", "c")

NT = (((1,), (1,)), ((), ()))
NN = (((1,), (0,)), ((), ()))
TN = (((0,), (0,)), ((), ()))


def dot(a, b, dims):
    return lax.dot_general(a, b, dims, preferred_element_type=jnp.float32)


def pair_index():
    return (lax.axis_index("z") * 2 + lax.axis_index("xh")) * 2 + lax.axis_index("yh")


def vmem():
    return pl.BlockSpec(memory_space=pltpu.VMEM)


def smem():
    return pl.BlockSpec(memory_space=pltpu.SMEM)


def call(kernel, outs, specs, scratch=(), name=None, flops=0, limit=4):
    many = isinstance(outs, (list, tuple))
    return pl.pallas_call(
        kernel,
        out_shape=outs,
        in_specs=specs,
        out_specs=[vmem() for _ in outs] if many else vmem(),
        scratch_shapes=list(scratch),
        name=name,
        compiler_params=pltpu.CompilerParams(vmem_limit_bytes=limit << 20),
        cost_estimate=pl.CostEstimate(flops=flops, bytes_accessed=1 << 20, transcendentals=0),
    )


def shape(*dims, dtype=jnp.bfloat16):
    return jax.ShapeDtypeStruct(dims, dtype)


def picked(rows, source, candidates):
    count = candidates.shape[0]
    columns = lax.broadcasted_iota(jnp.int32, (rows, count), 1)
    chosen = (columns == source).astype(jnp.float32).astype(jnp.bfloat16)
    return dot(chosen, candidates, NN).astype(jnp.bfloat16)


def pack_kernel(keys_ref, values_ref, queries_ref, grads_ref, out_ref):
    for target in range(8):
        head = (target % 4) * 2 + target // 4
        start = 0
        for ref in (keys_ref, values_ref, queries_ref, grads_ref):
            width = ref.shape[1] // 8
            out_ref[target, :, start : start + width] = ref[:, head * width : (head + 1) * width]
            start += width


def edges_kernel(offsets_ref, slots_ref, left_ref, right_ref):
    pair = pair_index()
    first = offsets_ref[2 * pair]
    middle = offsets_ref[2 * pair + 1]
    row = lax.broadcasted_iota(jnp.int32, (2 * EDGE, 1), 0)
    to_left = row + (pair * PAIR - EDGE - first)
    to_right = row + (SLOTS - EDGE + (pair + 1) * PAIR - middle)
    source = jnp.where(row < EDGE, to_left, to_right)
    both = picked(2 * EDGE, source, slots_ref[...])
    left_ref[...] = both[:EDGE]
    right_ref[...] = both[EDGE:]


def even_kernel(offsets_ref, slots_ref, left_ref, right_ref, keys_ref, rows_ref):
    pair = pair_index()
    first = offsets_ref[2 * pair]
    middle = offsets_ref[2 * pair + 1]
    last = offsets_ref[2 * pair + 2]
    row = lax.broadcasted_iota(jnp.int32, (PAIR, 1), 0)
    place = row + pair * PAIR
    source = jnp.where(
        place < first,
        2 * SLOTS + row,
        jnp.where(
            place < middle,
            place - first,
            jnp.where(place < last, SLOTS + place - middle, 2 * SLOTS + 2 * EDGE - PAIR + row),
        ),
    )
    width = slots_ref.shape[1]
    candidates = jnp.concatenate(
        [slots_ref[...], left_ref[...], right_ref[...], jnp.zeros((96, width), jnp.bfloat16)], axis=0
    )
    rows = picked(PAIR, source, candidates)
    keys_ref[...] = rows[:, : 2 * HEAD]
    rows_ref[...] = rows[:, 2 * HEAD :]


def shifted(value, steps):
    pairs = range(max(0, -steps), min(PAIRS, PAIRS - steps))
    return lax.ppermute(value, PAIR_AXES, [(i, i + steps) for i in pairs])


def even_rows(slots, offsets):
    width = slots.shape[1]
    left, right = call(
        edges_kernel, [shape(EDGE, width), shape(EDGE, width)], [smem(), vmem()], name="edges"
    )(offsets, slots)
    return call(
        even_kernel,
        [shape(PAIR, 2 * HEAD), shape(PAIR, 4 * HEAD)],
        [smem(), vmem(), vmem(), vmem()],
        name="even",
    )(offsets, slots, shifted(right, 1), shifted(left, -1))


def attend_kernel(
    rows_ref, own_ref, first_ref, second_ref, third_ref, far_ref,
    out_ref, kept_ref, given1_ref, given2_ref, given3_ref, back_ref, score_ref,
):
    pair = pair_index()
    others = (first_ref, second_ref, third_ref)
    given = (given1_ref, given2_ref, given3_ref)
    width = 2 * PAIR
    queries = jnp.concatenate([rows_ref[:, :HEAD], rows_ref[:, HEAD : 2 * HEAD]], axis=0)
    grads = jnp.concatenate([rows_ref[:, 2 * HEAD : 3 * HEAD], rows_ref[:, 3 * HEAD :]], axis=0)
    key_row = lax.broadcasted_iota(jnp.int32, (PAIR, width), 0)
    query_row = lax.broadcasted_iota(jnp.int32, (PAIR, width), 1) & (PAIR - 1)
    near = key_row <= query_row
    top = jnp.full((1, width), OUTSIDE, jnp.float32)
    for step, ref in enumerate(others):
        bias = jnp.where(pair > step, 0.0, OUTSIDE)
        score = dot(ref[:, :HEAD], queries, NT) * (SCALE * LOG2E) + bias
        score_ref[step * PAIR : (step + 1) * PAIR, :] = score
        top = jnp.maximum(top, jnp.max(score, axis=0, keepdims=True))
    bias = jnp.where(pair >= UNITS, 0.0, OUTSIDE)
    score = jnp.where(
        near,
        dot(own_ref[:, :HEAD], queries, NT) * (SCALE * LOG2E),
        dot(far_ref[:, :HEAD], queries, NT) * (SCALE * LOG2E) + bias,
    )
    score_ref[3 * PAIR :, :] = score
    top = jnp.maximum(top, jnp.max(score, axis=0, keepdims=True))
    total = jnp.zeros((1, width), jnp.float32)
    for step in range(UNITS):
        weight = jnp.exp2(score_ref[step * PAIR : (step + 1) * PAIR, :] - top)
        score_ref[step * PAIR : (step + 1) * PAIR, :] = weight
        total = total + jnp.sum(weight, axis=0, keepdims=True)
    share = 1.0 / total
    zero = jnp.zeros((), jnp.bfloat16)
    attn = jnp.zeros((HEAD, width), jnp.float32)
    for step, ref in enumerate(others):
        prob = (score_ref[step * PAIR : (step + 1) * PAIR, :] * share).astype(jnp.bfloat16)
        attn = attn + dot(ref[:, HEAD:], prob, TN)
        given[step][:, HEAD:] = dot(prob, grads, NN).astype(jnp.bfloat16)
    prob = score_ref[3 * PAIR :, :] * share
    prob_own = jnp.where(near, prob, 0.0).astype(jnp.bfloat16)
    prob_far = jnp.where(near, 0.0, prob).astype(jnp.bfloat16)
    attn = attn + dot(own_ref[:, HEAD:], prob_own, TN) + dot(far_ref[:, HEAD:], prob_far, TN)
    kept_ref[:, HEAD:] = dot(prob_own, grads, NN)
    back_ref[:, HEAD:] = dot(prob_far, grads, NN).astype(jnp.bfloat16)
    attn = attn.astype(jnp.bfloat16).astype(jnp.float32)
    grads_t = grads.astype(jnp.float32).T
    delta = jnp.sum(attn * grads_t, axis=0, keepdims=True)
    attn_rows = attn.T.astype(jnp.bfloat16)
    out_ref[:, :HEAD] = attn_rows[:PAIR]
    out_ref[:, HEAD : 2 * HEAD] = attn_rows[PAIR:]
    scaled = share * SCALE
    query_grad = jnp.zeros((HEAD, width), jnp.float32)
    for step, ref in enumerate(others):
        prob = score_ref[step * PAIR : (step + 1) * PAIR, :] * scaled
        change = (prob * (dot(ref[:, HEAD:], grads, NT) - delta)).astype(jnp.bfloat16)
        query_grad = query_grad + dot(ref[:, :HEAD], change, TN)
        given[step][:, :HEAD] = dot(change, queries, NN).astype(jnp.bfloat16)
    prob = score_ref[3 * PAIR :, :] * scaled
    grad_own = dot(own_ref[:, HEAD:], grads, NT)
    grad_far = dot(far_ref[:, HEAD:], grads, NT)
    change = prob * (jnp.where(near, grad_own, grad_far) - delta)
    change_own = jnp.where(near, change, 0.0).astype(jnp.bfloat16)
    change_far = jnp.where(near, 0.0, change).astype(jnp.bfloat16)
    query_grad = query_grad + dot(own_ref[:, :HEAD], change_own, TN)
    query_grad = query_grad + dot(far_ref[:, :HEAD], change_far, TN)
    kept_ref[:, :HEAD] = dot(change_own, queries, NN)
    back_ref[:, :HEAD] = dot(change_far, queries, NN).astype(jnp.bfloat16)
    grad_rows = query_grad.T.astype(jnp.bfloat16)
    out_ref[:, 2 * HEAD : 3 * HEAD] = grad_rows[:PAIR]
    out_ref[:, 3 * HEAD :] = grad_rows[PAIR:]


def parts(rows_ref, swap_ref, step_ref, skip_ref):
    member = lax.axis_index("yl")
    start = pl.multiple_of(jnp.where(member == 0, PAIR - SWAP, 0), 16)
    low = pl.multiple_of(jnp.where(member == 0, 0, PAIR - EDGE), 16)
    high = pl.multiple_of(jnp.where(member == 0, PAIR - EDGE, 0), 16)
    swap_ref[...] = rows_ref[pl.ds(start, SWAP), :]
    step_ref[...] = rows_ref[pl.ds(low, EDGE), :]
    skip_ref[...] = rows_ref[pl.ds(high, EDGE), :]


def total_kernel(rows_ref, own_ref, back1_ref, back2_ref, back3_ref, back4_ref, out_ref, swap_ref, step_ref, skip_ref):
    total = own_ref[...]
    for ref in (back1_ref, back2_ref, back3_ref, back4_ref):
        total = total + ref[...].astype(jnp.float32)
    out_ref[:, : 4 * HEAD] = rows_ref[...]
    out_ref[:, 4 * HEAD :] = total.astype(jnp.bfloat16)
    parts(out_ref, swap_ref, step_ref, skip_ref)


def place_kernel(offsets_ref, rows_ref, swap_ref, step_ref, skip_ref, *out_refs):
    pair = pair_index()
    member = lax.axis_index("yl")
    start = offsets_ref[2 * pair + member]
    end = offsets_ref[2 * pair + member + 1]
    slot = lax.broadcasted_iota(jnp.int32, (SLOTS, 1), 0)
    place = slot + (start - pair * PAIR)
    inside = (place >= 0) & (place < PAIR)
    edge = place + jnp.where(member == 0, EDGE, -PAIR)
    live = slot < end - start
    mine = jnp.where(live, jnp.where(inside, place, PAIR + edge), -1)
    theirs = place - jnp.where(member == 0, 0, PAIR - SWAP)
    theirs = jnp.where(live, jnp.where(inside, theirs, SWAP + edge), -1)
    pad = jnp.zeros((80, rows_ref.shape[1]), jnp.bfloat16)
    own = picked(SLOTS, mine, jnp.concatenate([rows_ref[...], skip_ref[...], pad], axis=0))
    other = picked(
        SLOTS, theirs, jnp.concatenate([swap_ref[...], step_ref[...], pad[:32]], axis=0)
    )

    def store(low, high):
        column = 0
        for ref in out_refs:
            width = ref.shape[1] // 2
            ref[:, :width] = low[:, column : column + width]
            ref[:, width:] = high[:, column : column + width]
            column += width

    @pl.when(member == 0)
    def _():
        store(own, other)

    @pl.when(member == 1)
    def _():
        store(other, own)


def placed(rows, swap, step, skip, offsets):
    blocks = range(2 * PAIRS)
    swap = lax.ppermute(swap, SEQ_AXES, [(j, j ^ 1) for j in blocks])
    step = lax.ppermute(
        step,
        SEQ_AXES,
        [(j, j + 2 * (j % 2) - 1) for j in blocks if 0 <= j + 2 * (j % 2) - 1 < 2 * PAIRS],
    )
    skip = lax.ppermute(
        skip,
        SEQ_AXES,
        [(j, j + 2 - 4 * (j % 2)) for j in blocks if 0 <= j + 2 - 4 * (j % 2) < 2 * PAIRS],
    )
    return call(
        place_kernel,
        [shape(SLOTS, 4 * HEAD)] * 2 + [shape(SLOTS, 2 * HEAD)] * 2,
        [smem(), vmem(), vmem(), vmem(), vmem()],
        name="place",
        limit=6,
    )(offsets, rows, swap, step, skip)


def on_device(q_old, k_old, value_old_layout, dout_old, old_offsets, new_offsets):
    packed = call(pack_kernel, shape(8, 56, 6 * HEAD), [vmem()] * 4, name="pack")(
        k_old, value_old_layout, q_old, dout_old
    )
    slots = lax.all_to_all(packed, GROUP_AXES, 0, 0, tiled=True)
    own, rows = even_rows(slots.reshape(2 * SLOTS, 6 * HEAD), old_offsets)
    others = [shifted(own, step + 1) for step in range(UNITS)]
    wide, narrow = 4 * HEAD, 2 * HEAD
    results, kept, *given = call(
        attend_kernel,
        [shape(PAIR, wide), shape(PAIR, narrow, dtype=jnp.float32)] + [shape(PAIR, narrow)] * UNITS,
        [vmem()] * 6,
        [pltpu.VMEM((UNITS * PAIR, 2 * PAIR), jnp.float32)],
        name="attend",
        flops=10**9,
        limit=24,
    )(rows, own, *others)
    back = [shifted(value, -step - 1) for step, value in enumerate(given)]
    full = wide + narrow
    parts_of = call(
        total_kernel,
        [shape(PAIR, full), shape(SWAP, full), shape(EDGE, full), shape(EDGE, full)],
        [vmem()] * 6,
        name="total",
    )(results, kept, *back)
    return tuple(placed(*parts_of, new_offsets))


def solution(mesh):
    cut = Mesh(mesh.devices.reshape(16, 2, 2, 2, 2, 2), AXES)
    rows = P(AXES, None)
    return jax.shard_map(
        on_device,
        mesh=cut,
        in_specs=(rows, rows, rows, rows, P(), P()),
        out_specs=(P(SEQ_AXES, ("xl", "c")),) * 4,
        check_vma=False,
    )
```

time: 142 us -> 108 us (0.76)
  the two profiles are of different devices: /device:TPU:96 before, /device:TPU:128 now
where the time goes in v2:
time: 108 us; the launch traced here: 107 us
  starting transfers between devices  53.3 us (49%)
  waiting for transfers between devices  26.8 us (25%)
  blocking collectives  15 us (14%)
  Pallas kernels  6.78 us (6%)
  local copies, waits for them, and re-layouts  4.35 us (4%)
    ppermute x10, starting transfers between devices, shifted(): return lax.ppermute(value, PAIR_AXES, [(i, i + steps) for i in pairs])  43.4 us
    ppermute x10, waiting for transfers between devices, shifted(): return lax.ppermute(value, PAIR_AXES, [(i, i + steps) for i in pairs])  16.5 us
    all_to_all x1, blocking collectives, on_device(): slots = lax.all_to_all(packed, GROUP_AXES, 0, 0, tiled=True)  15 us
    ppermute x1, waiting for transfers between devices, placed(): lax.ppermute(skip, SEQ_AXES, [(j, j + 2 - 4 * (j % 2)) for j in blocks if...  5.85 us
    ppermute x1, starting transfers between devices, placed(): lax.ppermute(step, SEQ_AXES, [(j, j + 2 * (j % 2) - 1) for j in blocks if...  5.54 us
    ppermute x1, waiting for transfers between devices, placed(): lax.ppermute(step, SEQ_AXES, [(j, j + 2 * (j % 2) - 1) for j in blocks if...  4.48 us
    unnamed x12, local copies, waits for them, and re-layouts  4.35 us
    pallas_call x1, Pallas kernels, on_device(): call(attend_kernel, [shape(PAIR, wide), shape(PAIR, narrow, dtype=jnp.flo...  2.78 us
  transfers between devices with their start and end apart: 13, of which 8 were waited for; matrix products, arithmetic and copies ran while one was open for 0% of the time, Pallas kernels for 0%

profile of v2, /device:TPU:128, one launch (start us, length us, event | category | flops | bytes accessed | tf_op | source)
XLA Modules:
  0.0 107.2 jit_solution(17218611637218919266)
XLA Ops:
  0.6 0.0 copy-start
  0.6 0.9 copy-done
  1.6 0.0 copy-start.1
  1.6 0.9 copy-done.1
  2.5 0.0 copy-start.2
  2.5 0.9 copy-done.2
  3.4 0.0 copy-start.3
  3.4 0.9 copy-done.3
  4.3 0.1 pack.1
  4.4 15.0 %all_to_all.5 = bf16[8,56,768]{2,1,0:T(8,128)(2,1)S(1)} all-to-all(bf16[8,56,768]{2,1,0:T(8,128)(2,1)S(1)} %pack.1), channel_id=1, replica_groups=mesh['z'=16,'xh'=2,'yh'=2,'yl'=2,'xl'=2,'c'=2] {'yl','xl','c'}, dimensions={0} | all-to-all | bytes 1376256 | tf_op jit(solution)/shard_map/all_to_all | solution.py:290
  19.4 0.0 copy-start.4
  19.4 0.7 copy-done.4
  20.1 0.8 edges.1
  20.9 4.8 %collective-permute-start = (bf16[48,768]{1,0:T(8,128)(2,1)S(1)}, bf16[48,768]{1,0:T(8,128)(2,1)S(1)}, u32[]{:S(2)}, u32[]{:S(2)}) collective-permute-start(bf16[48,768]{1,0:T(8,128)(2,1)S(1)} %get-tuple-element.18), channel_id=1, source_target_pairs={{0,8},{8,16},{16,24},{24,32},{32,40},{40,48},{48,56},{56,64},{64,7... | collective-permute-start | bytes 221192 | tf_op jit(solution)/shard_map/ppermute | solution.py:120
  25.7 7.1 %collective-permute-start.1 = (bf16[48,768]{1,0:T(8,128)(2,1)S(1)}, bf16[48,768]{1,0:T(8,128)(2,1)S(1)}, u32[]{:S(2)}, u32[]{:S(2)}) collective-permute-start(bf16[48,768]{1,0:T(8,128)(2,1)S(1)} %get-tuple-element.19), channel_id=1, source_target_pairs={{8,0},{16,8},{24,16},{32,24},{40,32},{48,40},{56,48},{64,56},{72,6... | collective-permute-start | bytes 221192 | tf_op jit(solution)/shard_map/ppermute | solution.py:120
  32.8 0.5 collective-permute-done.left_ref
  33.3 1.5 %collective-permute-done.1.right_ref = bf16[48,768]{1,0:T(8,128)(2,1)S(1)} collective-permute-done((bf16[48,768]{1,0:T(8,128)(2,1)S(1)}, bf16[48,768]{1,0:T(8,128)(2,1)S(1)}, u32[]{:S(2)}, u32[]{:S(2)}) %collective-permute-start.1) | collective-permute-done | bytes 73760 | tf_op jit(solution)/shard_map/ppermute | solution.py:120
  34.7 1.1 even.1
  35.8 2.6 %collective-permute-start.5 = (bf16[256,256]{1,0:T(8,128)(2,1)S(1)}, bf16[256,256]{1,0:T(8,128)(2,1)S(1)}, u32[]{:S(2)}, u32[]{:S(2)}) collective-permute-start(bf16[256,256]{1,0:T(8,128)(2,1)S(1)} %get-tuple-element.21.own_ref), channel_id=1, source_target_pairs={{0,32},{8,40},{16,48},{24,56},{32,64},{40,72},{48,80},{56,88},{64,... | collective-permute-start | bytes 393224 | tf_op jit(solution)/shard_map/ppermute | solution.py:120
  38.4 9.5 %collective-permute-start.4 = (bf16[256,256]{1,0:T(8,128)(2,1)S(1)}, bf16[256,256]{1,0:T(8,128)(2,1)S(1)}, u32[]{:S(2)}, u32[]{:S(2)}) collective-permute-start(bf16[256,256]{1,0:T(8,128)(2,1)S(1)} %get-tuple-element.21.own_ref), channel_id=1, source_target_pairs={{0,24},{8,32},{16,40},{24,48},{32,56},{40,64},{48,72},{56,80},{64,... | collective-permute-start | bytes 393224 | tf_op jit(solution)/shard_map/ppermute | solution.py:120
  48.0 3.7 %collective-permute-start.3 = (bf16[256,256]{1,0:T(8,128)(2,1)S(1)}, bf16[256,256]{1,0:T(8,128)(2,1)S(1)}, u32[]{:S(2)}, u32[]{:S(2)}) collective-permute-start(bf16[256,256]{1,0:T(8,128)(2,1)S(1)} %get-tuple-element.21.own_ref), channel_id=1, source_target_pairs={{0,16},{8,24},{16,32},{24,40},{32,48},{40,56},{48,64},{56,72},{64,... | collective-permute-start | bytes 393224 | tf_op jit(solution)/shard_map/ppermute | solution.py:120
  51.7 1.9 %collective-permute-start.2 = (bf16[256,256]{1,0:T(8,128)(2,1)S(1)}, bf16[256,256]{1,0:T(8,128)(2,1)S(1)}, u32[]{:S(2)}, u32[]{:S(2)}) collective-permute-start(bf16[256,256]{1,0:T(8,128)(2,1)S(1)} %get-tuple-element.21.own_ref), channel_id=1, source_target_pairs={{0,8},{8,16},{16,24},{24,32},{32,40},{40,48},{48,56},{56,64},{64,7... | collective-permute-start | bytes 393224 | tf_op jit(solution)/shard_map/ppermute | solution.py:120
  53.7 0.0 collective-permute-done.5.far_ref
  53.7 0.0 collective-permute-done.4.third_ref
  53.7 4.8 %collective-permute-done.3.second_ref = bf16[256,256]{1,0:T(8,128)(2,1)S(1)} collective-permute-done((bf16[256,256]{1,0:T(8,128)(2,1)S(1)}, bf16[256,256]{1,0:T(8,128)(2,1)S(1)}, u32[]{:S(2)}, u32[]{:S(2)}) %collective-permute-start.3) | collective-permute-done | bytes 131104 | tf_op jit(solution)/shard_map/ppermute | solution.py:120
  58.5 6.1 %collective-permute-done.2.first_ref = bf16[256,256]{1,0:T(8,128)(2,1)S(1)} collective-permute-done((bf16[256,256]{1,0:T(8,128)(2,1)S(1)}, bf16[256,256]{1,0:T(8,128)(2,1)S(1)}, u32[]{:S(2)}, u32[]{:S(2)}) %collective-permute-start.2) | collective-permute-done | bytes 131104 | tf_op jit(solution)/shard_map/ppermute | solution.py:120
  64.6 2.8 %attend.1 = (bf16[256,512]{1,0:T(8,128)(2,1)S(1)}, f32[256,256]{1,0:T(8,128)S(1)}, bf16[256,256]{1,0:T(8,128)(2,1)S(1)}, bf16[256,256]{1,0:T(8,128)(2,1)S(1)}, b...) custom-call(bf16[256,512]{1,0:T(8,128)(2,1)S(1)} %get-tuple-element.20.rows_ref, ...), custom_call_target="tpu_custom_call" | custom-call | flops 1000000000 | bytes 1048576 | tf_op jit(solution)/shard_map/attend/pallas_call | solution.py:294
  67.4 1.9 %collective-permute-start.6 = (bf16[256,256]{1,0:T(8,128)(2,1)S(1)}, bf16[256,256]{1,0:T(8,128)(2,1)S(1)}, u32[]{:S(2)}, u32[]{:S(2)}) collective-permute-start(bf16[256,256]{1,0:T(8,128)(2,1)S(1)} %get-tuple-element.24), channel_id=1, source_target_pairs={{8,0},{16,8},{24,16},{32,24},{40,32},{48,40},{56,48},{64,56},{72,6... | collective-permute-start | bytes 393224 | tf_op jit(solution)/shard_map/ppermute | solution.py:120
  69.3 3.6 %collective-permute-start.7 = (bf16[256,256]{1,0:T(8,128)(2,1)S(1)}, bf16[256,256]{1,0:T(8,128)(2,1)S(1)}, u32[]{:S(2)}, u32[]{:S(2)}) collective-permute-start(bf16[256,256]{1,0:T(8,128)(2,1)S(1)} %get-tuple-element.25), channel_id=1, source_target_pairs={{16,0},{24,8},{32,16},{40,24},{48,32},{56,40},{64,48},{72,56},{80,... | collective-permute-start | bytes 393224 | tf_op jit(solution)/shard_map/ppermute | solution.py:120
  72.9 5.0 %collective-permute-start.8 = (bf16[256,256]{1,0:T(8,128)(2,1)S(1)}, bf16[256,256]{1,0:T(8,128)(2,1)S(1)}, u32[]{:S(2)}, u32[]{:S(2)}) collective-permute-start(bf16[256,256]{1,0:T(8,128)(2,1)S(1)} %get-tuple-element.26), channel_id=1, source_target_pairs={{24,0},{32,8},{40,16},{48,24},{56,32},{64,40},{72,48},{80,56},{88,... | collective-permute-start | bytes 393224 | tf_op jit(solution)/shard_map/ppermute | solution.py:120
  77.9 3.2 %collective-permute-start.9 = (bf16[256,256]{1,0:T(8,128)(2,1)S(1)}, bf16[256,256]{1,0:T(8,128)(2,1)S(1)}, u32[]{:S(2)}, u32[]{:S(2)}) collective-permute-start(bf16[256,256]{1,0:T(8,128)(2,1)S(1)} %get-tuple-element.27), channel_id=1, source_target_pairs={{32,0},{40,8},{48,16},{56,24},{64,32},{72,40},{80,48},{88,56},{96,... | collective-permute-start | bytes 393224 | tf_op jit(solution)/shard_map/ppermute | solution.py:120
  81.2 0.0 collective-permute-done.6.back1_ref
  81.2 0.0 collective-permute-done.7.back2_ref
  81.2 2.5 %collective-permute-done.8.back3_ref = bf16[256,256]{1,0:T(8,128)(2,1)S(1)} collective-permute-done((bf16[256,256]{1,0:T(8,128)(2,1)S(1)}, bf16[256,256]{1,0:T(8,128)(2,1)S(1)}, u32[]{:S(2)}, u32[]{:S(2)}) %collective-permute-start.8) | collective-permute-done | bytes 131104 | tf_op jit(solution)/shard_map/ppermute | solution.py:120
  83.7 1.1 %collective-permute-done.9.back4_ref = bf16[256,256]{1,0:T(8,128)(2,1)S(1)} collective-permute-done((bf16[256,256]{1,0:T(8,128)(2,1)S(1)}, bf16[256,256]{1,0:T(8,128)(2,1)S(1)}, u32[]{:S(2)}, u32[]{:S(2)}) %collective-permute-start.9) | collective-permute-done | bytes 131104 | tf_op jit(solution)/shard_map/ppermute | solution.py:120
  84.8 0.1 total.1
  84.9 2.5 %collective-permute-start.10 = (bf16[176,768]{1,0:T(8,128)(2,1)S(1)}, bf16[176,768]{1,0:T(8,128)(2,1)S(1)}, u32[]{:S(2)}, u32[]{:S(2)}) collective-permute-start(bf16[176,768]{1,0:T(8,128)(2,1)S(1)} %get-tuple-element.29), channel_id=1, source_target_pairs={{0,4},{4,0},{8,12},{12,8},{16,20},{20,16},{24,28},{28,24},{32,36},... | collective-permute-start | bytes 811016 | tf_op jit(solution)/shard_map/ppermute | solution.py:266
  87.4 5.5 %collective-permute-start.11 = (bf16[48,768]{1,0:T(8,128)(2,1)S(1)}, bf16[48,768]{1,0:T(8,128)(2,1)S(1)}, u32[]{:S(2)}, u32[]{:S(2)}) collective-permute-start(bf16[48,768]{1,0:T(8,128)(2,1)S(1)} %get-tuple-element.30), channel_id=1, source_target_pairs={{4,8},{8,4},{12,16},{16,12},{20,24},{24,20},{28,32},{32,28},{36,40... | collective-permute-start | bytes 221192 | tf_op jit(solution)/shard_map/ppermute | solution.py:267
  92.9 0.0 copy-start.5
  93.0 1.9 %collective-permute-start.12 = (bf16[48,768]{1,0:T(8,128)(2,1)S(1)}, bf16[48,768]{1,0:T(8,128)(2,1)S(1)}, u32[]{:S(2)}, u32[]{:S(2)}) collective-permute-start(bf16[48,768]{1,0:T(8,128)(2,1)S(1)} %get-tuple-element.31), channel_id=1, source_target_pairs={{0,8},{8,16},{12,4},{16,24},{20,12},{24,32},{28,20},{32,40},{36,28... | collective-permute-start | bytes 221192 | tf_op jit(solution)/shard_map/ppermute | solution.py:272
  94.9 4.5 %collective-permute-done.11.step_ref = bf16[48,768]{1,0:T(8,128)(2,1)S(1)} collective-permute-done((bf16[48,768]{1,0:T(8,128)(2,1)S(1)}, bf16[48,768]{1,0:T(8,128)(2,1)S(1)}, u32[]{:S(2)}, u32[]{:S(2)}) %collective-permute-start.11) | collective-permute-done | bytes 73760 | tf_op jit(solution)/shard_map/ppermute | solution.py:267
  99.4 5.9 %collective-permute-done.12.skip_ref = bf16[48,768]{1,0:T(8,128)(2,1)S(1)} collective-permute-done((bf16[48,768]{1,0:T(8,128)(2,1)S(1)}, bf16[48,768]{1,0:T(8,128)(2,1)S(1)}, u32[]{:S(2)}, u32[]{:S(2)}) %collective-permute-start.12) | collective-permute-done | bytes 73760 | tf_op jit(solution)/shard_map/ppermute | solution.py:272
  105.2 0.0 collective-permute-done.10.swap_ref
  105.2 0.0 copy-done.5
  105.2 1.9 %place.1 = (bf16[224,512]{1,0:T(8,128)(2,1)}, bf16[224,512]{1,0:T(8,128)(2,1)}, bf16[224,256]{1,0:T(8,128)(2,1)}, bf16[224,256]{1,0:T(8,128)(2,1)}) custom-call(s32[129]{0:T(256)S(1)} %copy-done.5, bf16[256,768]{1,0:T(8,128)(2,1)S(1)} %get-tuple-element.28.rows_ref, bf16[176,768]{1,0:T(8,128)(2,1)S(1)} %collective-permute-done.10.swap_ref, ...), custom_call_target="tpu_custom_call" | custom-call | bytes 1048576 | tf_op jit(solution)/shard_map/place/pallas_call | solution.py:277
Async XLA Ops:
  0.6 0.9 copy-start
  1.6 0.9 copy-start.1
  2.5 0.9 copy-start.2
  3.4 0.9 copy-start.3
  19.4 0.7 copy-start.4
  20.9 12.4 %collective-permute-start = (bf16[48,768]{1,0:T(8,128)(2,1)S(1)}, bf16[48,768]{1,0:T(8,128)(2,1)S(1)}, u32[]{:S(2)}, u32[]{:S(2)}) collective-permute-start(bf16[48,768]{1,0:T(8,128)(2,1)S(1)} %get-tuple-element.18), channel_id=1, source_target_pairs={{0,8},{8,16},{16,24},{24,32},{32,40},{40,48},{48,56},{56,64},{64,7... | collective-permute-start | bytes 221192 | tf_op jit(solution)/shard_map/ppermute | solution.py:120
  25.7 9.0 %collective-permute-start.1 = (bf16[48,768]{1,0:T(8,128)(2,1)S(1)}, bf16[48,768]{1,0:T(8,128)(2,1)S(1)}, u32[]{:S(2)}, u32[]{:S(2)}) collective-permute-start(bf16[48,768]{1,0:T(8,128)(2,1)S(1)} %get-tuple-element.19), channel_id=1, source_target_pairs={{8,0},{16,8},{24,16},{32,24},{40,32},{48,40},{56,48},{64,56},{72,6... | collective-permute-start | bytes 221192 | tf_op jit(solution)/shard_map/ppermute | solution.py:120
  35.8 17.8 %collective-permute-start.5 = (bf16[256,256]{1,0:T(8,128)(2,1)S(1)}, bf16[256,256]{1,0:T(8,128)(2,1)S(1)}, u32[]{:S(2)}, u32[]{:S(2)}) collective-permute-start(bf16[256,256]{1,0:T(8,128)(2,1)S(1)} %get-tuple-element.21.own_ref), channel_id=1, source_target_pairs={{0,32},{8,40},{16,48},{24,56},{32,64},{40,72},{48,80},{56,88},{64,... | collective-permute-start | bytes 393224 | tf_op jit(solution)/shard_map/ppermute | solution.py:120
  38.4 15.2 %collective-permute-start.4 = (bf16[256,256]{1,0:T(8,128)(2,1)S(1)}, bf16[256,256]{1,0:T(8,128)(2,1)S(1)}, u32[]{:S(2)}, u32[]{:S(2)}) collective-permute-start(bf16[256,256]{1,0:T(8,128)(2,1)S(1)} %get-tuple-element.21.own_ref), channel_id=1, source_target_pairs={{0,24},{8,32},{16,40},{24,48},{32,56},{40,64},{48,72},{56,80},{64,... | collective-permute-start | bytes 393224 | tf_op jit(solution)/shard_map/ppermute | solution.py:120
  48.0 10.5 %collective-permute-start.3 = (bf16[256,256]{1,0:T(8,128)(2,1)S(1)}, bf16[256,256]{1,0:T(8,128)(2,1)S(1)}, u32[]{:S(2)}, u32[]{:S(2)}) collective-permute-start(bf16[256,256]{1,0:T(8,128)(2,1)S(1)} %get-tuple-element.21.own_ref), channel_id=1, source_target_pairs={{0,16},{8,24},{16,32},{24,40},{32,48},{40,56},{48,64},{56,72},{64,... | collective-permute-start | bytes 393224 | tf_op jit(solution)/shard_map/ppermute | solution.py:120
  51.7 12.9 %collective-permute-start.2 = (bf16[256,256]{1,0:T(8,128)(2,1)S(1)}, bf16[256,256]{1,0:T(8,128)(2,1)S(1)}, u32[]{:S(2)}, u32[]{:S(2)}) collective-permute-start(bf16[256,256]{1,0:T(8,128)(2,1)S(1)} %get-tuple-element.21.own_ref), channel_id=1, source_target_pairs={{0,8},{8,16},{16,24},{24,32},{32,40},{40,48},{48,56},{56,64},{64,7... | collective-permute-start | bytes 393224 | tf_op jit(solution)/shard_map/ppermute | solution.py:120
  67.4 13.8 %collective-permute-start.6 = (bf16[256,256]{1,0:T(8,128)(2,1)S(1)}, bf16[256,256]{1,0:T(8,128)(2,1)S(1)}, u32[]{:S(2)}, u32[]{:S(2)}) collective-permute-start(bf16[256,256]{1,0:T(8,128)(2,1)S(1)} %get-tuple-element.24), channel_id=1, source_target_pairs={{8,0},{16,8},{24,16},{32,24},{40,32},{48,40},{56,48},{64,56},{72,6... | collective-permute-start | bytes 393224 | tf_op jit(solution)/shard_map/ppermute | solution.py:120
  69.3 11.8 %collective-permute-start.7 = (bf16[256,256]{1,0:T(8,128)(2,1)S(1)}, bf16[256,256]{1,0:T(8,128)(2,1)S(1)}, u32[]{:S(2)}, u32[]{:S(2)}) collective-permute-start(bf16[256,256]{1,0:T(8,128)(2,1)S(1)} %get-tuple-element.25), channel_id=1, source_target_pairs={{16,0},{24,8},{32,16},{40,24},{48,32},{56,40},{64,48},{72,56},{80,... | collective-permute-start | bytes 393224 | tf_op jit(solution)/shard_map/ppermute | solution.py:120
  72.9 10.8 %collective-permute-start.8 = (bf16[256,256]{1,0:T(8,128)(2,1)S(1)}, bf16[256,256]{1,0:T(8,128)(2,1)S(1)}, u32[]{:S(2)}, u32[]{:S(2)}) collective-permute-start(bf16[256,256]{1,0:T(8,128)(2,1)S(1)} %get-tuple-element.26), channel_id=1, source_target_pairs={{24,0},{32,8},{40,16},{48,24},{56,32},{64,40},{72,48},{80,56},{88,... | collective-permute-start | bytes 393224 | tf_op jit(solution)/shard_map/ppermute | solution.py:120
  77.9 6.9 %collective-permute-start.9 = (bf16[256,256]{1,0:T(8,128)(2,1)S(1)}, bf16[256,256]{1,0:T(8,128)(2,1)S(1)}, u32[]{:S(2)}, u32[]{:S(2)}) collective-permute-start(bf16[256,256]{1,0:T(8,128)(2,1)S(1)} %get-tuple-element.27), channel_id=1, source_target_pairs={{32,0},{40,8},{48,16},{56,24},{64,32},{72,40},{80,48},{88,56},{96,... | collective-permute-start | bytes 393224 | tf_op jit(solution)/shard_map/ppermute | solution.py:120
  84.9 20.3 %collective-permute-start.10 = (bf16[176,768]{1,0:T(8,128)(2,1)S(1)}, bf16[176,768]{1,0:T(8,128)(2,1)S(1)}, u32[]{:S(2)}, u32[]{:S(2)}) collective-permute-start(bf16[176,768]{1,0:T(8,128)(2,1)S(1)} %get-tuple-element.29), channel_id=1, source_target_pairs={{0,4},{4,0},{8,12},{12,8},{16,20},{20,16},{24,28},{28,24},{32,36},... | collective-permute-start | bytes 811016 | tf_op jit(solution)/shard_map/ppermute | solution.py:266
  87.4 12.0 %collective-permute-start.11 = (bf16[48,768]{1,0:T(8,128)(2,1)S(1)}, bf16[48,768]{1,0:T(8,128)(2,1)S(1)}, u32[]{:S(2)}, u32[]{:S(2)}) collective-permute-start(bf16[48,768]{1,0:T(8,128)(2,1)S(1)} %get-tuple-element.30), channel_id=1, source_target_pairs={{4,8},{8,4},{12,16},{16,12},{20,24},{24,20},{28,32},{32,28},{36,40... | collective-permute-start | bytes 221192 | tf_op jit(solution)/shard_map/ppermute | solution.py:267
  92.9 12.3 %copy-start.5 = (s32[129]{0:T(256)S(1)}, s32[129]{0:T(256)}, u32[]{:S(2)}) copy-start(s32[129]{0:T(256)} %offsets_ref.5) | copy-start | bytes 1552
  93.0 12.3 %collective-permute-start.12 = (bf16[48,768]{1,0:T(8,128)(2,1)S(1)}, bf16[48,768]{1,0:T(8,128)(2,1)S(1)}, u32[]{:S(2)}, u32[]{:S(2)}) collective-permute-start(bf16[48,768]{1,0:T(8,128)(2,1)S(1)} %get-tuple-element.31), channel_id=1, source_target_pairs={{0,8},{8,16},{12,4},{16,24},{20,12},{24,32},{28,20},{32,40},{36,28... | collective-permute-start | bytes 221192 | tf_op jit(solution)/shard_map/ppermute | solution.py:272

commit v3 on v2

v3 whole, which is shorter than its diff:
```python
import jax
import jax.numpy as jnp
from jax import lax
from jax.experimental import pallas as pl
from jax.experimental.pallas import tpu as pltpu
from jax.sharding import Mesh, PartitionSpec as P


PAIR = 256
SLOTS = 224
LEAD = 48
EDGE = 96
SPAN = PAIR + EDGE
HEAD = 128
UNITS = 4
PAIRS = 64
SCALE = 168.0 ** (-0.5)
LOG2E = 1.4426950408889634
OUTSIDE = -1e30

AXES = ("z", "xh", "yh", "yl", "xl", "c")
SEQ_AXES = ("z", "xh", "yh", "yl")
GROUP_AXES = ("yl", "xl", "c")

NT = (((1,), (1,)), ((), ()))
NN = (((1,), (0,)), ((), ()))
TN = (((0,), (0,)), ((), ()))


def dot(a, b, dims):
    return lax.dot_general(a, b, dims, preferred_element_type=jnp.float32)


def pair_index():
    return (lax.axis_index("z") * 2 + lax.axis_index("xh")) * 2 + lax.axis_index("yh")


def vmem():
    return pl.BlockSpec(memory_space=pltpu.VMEM)


def call(kernel, outs, specs, scratch=(), flops=0, limit=4):
    many = isinstance(outs, (list, tuple))
    return pl.pallas_call(
        kernel,
        out_shape=outs,
        in_specs=specs,
        out_specs=[vmem() for _ in outs] if many else vmem(),
        scratch_shapes=list(scratch),
        compiler_params=pltpu.CompilerParams(vmem_limit_bytes=limit << 20),
        cost_estimate=pl.CostEstimate(flops=flops, bytes_accessed=1 << 20, transcendentals=0),
    )


def shape(*dims, dtype=jnp.bfloat16):
    return jax.ShapeDtypeStruct(dims, dtype)


def picked(rows, source, candidates):
    count = candidates.shape[0]
    columns = lax.broadcasted_iota(jnp.int32, (rows, count), 1)
    chosen = (columns == source).astype(jnp.float32).astype(jnp.bfloat16)
    return dot(chosen, candidates, NN).astype(jnp.bfloat16)


def compute_member():
    return lax.axis_index("yl") ^ lax.axis_index("yh")


def pack_kernel(
    keys_ref, values_ref, queries_ref, grads_ref, old_ref, new_ref, out_ref, facts_ref,
    offsets_ref, sems, offset_sems,
):
    old_copy = pltpu.make_async_copy(old_ref, offsets_ref.at[0], offset_sems.at[0])
    new_copy = pltpu.make_async_copy(new_ref, offsets_ref.at[1], offset_sems.at[1])
    old_copy.start()
    new_copy.start()
    mirrored = lax.axis_index("yh")
    copies = []
    for target in range(8):
        head = (target % 4) * 2 + ((target // 4) ^ mirrored)
        begin = 0
        for ref in (keys_ref, values_ref, queries_ref, grads_ref):
            width = ref.shape[1] // 8
            source = ref.at[:, pl.ds(pl.multiple_of(head * width, HEAD), width)]
            copy = pltpu.make_async_copy(
                source, out_ref.at[target, :, pl.ds(begin, width)], sems.at[len(copies)]
            )
            copy.start()
            copies.append(copy)
            begin += width
    old_copy.wait()
    new_copy.wait()
    pair = pair_index()
    block = 2 * pair + lax.axis_index("yl")
    facts = (
        offsets_ref[0, 2 * pair],
        offsets_ref[0, 2 * pair + 1],
        offsets_ref[0, 2 * pair + 2],
        offsets_ref[1, block],
        offsets_ref[1, block + 1],
    )
    for row, fact in enumerate(facts):
        facts_ref[row : row + 1, :] = jnp.full((1, HEAD), fact, jnp.int32)
    facts_ref[len(facts) :, :] = jnp.zeros((8 - len(facts), HEAD), jnp.int32)
    for copy in copies:
        copy.wait()


def raw_kernel(facts_ref, slots_ref, first_ref, edge_ref, rows_ref):
    start = pair_index() * PAIR - LEAD
    place = lax.broadcasted_iota(jnp.int32, (SPAN, 1), 0) + start
    first = facts_ref[0:1, 0:1]
    middle = facts_ref[1:2, 0:1]
    last = facts_ref[2:3, 0:1]
    source = jnp.where(place < middle, place - first, SLOTS + place - middle)
    source = jnp.where((place >= first) & (place < last), source, -1)
    rows = picked(SPAN, source, slots_ref[...])
    first_ref[...] = rows[:, : 2 * HEAD]
    edge_ref[...] = rows[PAIR:, 2 * HEAD :]
    rows_ref[...] = rows[:PAIR, 2 * HEAD :]


def joined(rows, edge):
    return jnp.concatenate([rows[:EDGE] + edge, rows[EDGE:]], axis=0)


def relay_kernel(mine_ref, first_ref, second_ref, fourth_ref):
    whole = joined(mine_ref[:PAIR], first_ref[PAIR:SPAN])
    edge = mine_ref[PAIR:SPAN]
    second_ref[:PAIR] = whole
    second_ref[PAIR:SPAN] = edge
    second_ref[SPAN:] = first_ref[:PAIR]
    fourth_ref[:PAIR] = whole
    fourth_ref[PAIR:] = edge


def attend_kernel(
    rows_ref, edge_ref, mine_ref, first_ref, second_ref, fourth_ref,
    out_ref, edge_out_ref, kept_ref, near_ref, give2_ref, give4_ref, score_ref,
):
    start = pair_index() * PAIR - LEAD
    width = 2 * PAIR
    own = mine_ref[:PAIR]
    far = fourth_ref[:PAIR]
    others = (
        joined(first_ref[:PAIR], second_ref[PAIR:SPAN]),
        second_ref[:PAIR],
        joined(second_ref[SPAN:], fourth_ref[PAIR:]),
    )

    def stacked(column):
        parts = []
        for head in range(2):
            columns = slice(column + head * HEAD, column + (head + 1) * HEAD)
            parts.append(joined(rows_ref[:, columns], edge_ref[:, columns]))
        return jnp.concatenate(parts, axis=0)

    queries = stacked(0)
    grads = stacked(2 * HEAD)
    key_row = lax.broadcasted_iota(jnp.int32, (PAIR, width), 0)
    query_row = lax.broadcasted_iota(jnp.int32, (PAIR, width), 1) & (PAIR - 1)
    near = key_row <= query_row
    column = lax.broadcasted_iota(jnp.int32, (1, width), 1) & (PAIR - 1)
    positive = (column + start >= 0).astype(jnp.float32)
    place = lax.broadcasted_iota(jnp.int32, (PAIR, 1), 0) + start

    def scores(keys, distance):
        bias = jnp.where(place - distance * PAIR >= 0, 0.0, OUTSIDE)
        return dot(keys[:, :HEAD], queries, NT) * (SCALE * LOG2E) + bias * positive

    top = jnp.full((1, width), OUTSIDE, jnp.float32)
    for step, keys in enumerate(others):
        score = scores(keys, step + 1)
        score_ref[step * PAIR : (step + 1) * PAIR, :] = score
        top = jnp.maximum(top, jnp.max(score, axis=0, keepdims=True))
    score = jnp.where(near, scores(own, 0), scores(far, UNITS))
    score_ref[3 * PAIR :, :] = score
    top = jnp.maximum(top, jnp.max(score, axis=0, keepdims=True))
    total = jnp.zeros((1, width), jnp.float32)
    for step in range(UNITS):
        weight = jnp.exp2(score_ref[step * PAIR : (step + 1) * PAIR, :] - top)
        score_ref[step * PAIR : (step + 1) * PAIR, :] = weight
        total = total + jnp.sum(weight, axis=0, keepdims=True)
    share = 1.0 / total

    def keep(step, columns, value):
        rounded = value.astype(jnp.bfloat16)
        if step == 0:
            kept_ref[:, columns] = value
        elif step == 1:
            near_ref[:, columns] = value
            give2_ref[PAIR:SPAN, columns] = rounded[:EDGE]
        elif step == 2:
            give2_ref[:PAIR, columns] = rounded
        elif step == 3:
            give2_ref[SPAN:, columns] = rounded
            give4_ref[PAIR:, columns] = rounded[:EDGE]
        else:
            give4_ref[:PAIR, columns] = rounded

    key_columns = slice(0, HEAD)
    value_columns = slice(HEAD, 2 * HEAD)
    attn = jnp.zeros((HEAD, width), jnp.float32)
    for step, keys in enumerate(others):
        prob = (score_ref[step * PAIR : (step + 1) * PAIR, :] * share).astype(jnp.bfloat16)
        attn = attn + dot(keys[:, HEAD:], prob, TN)
        keep(step + 1, value_columns, dot(prob, grads, NN))
    prob = score_ref[3 * PAIR :, :] * share
    prob_own = jnp.where(near, prob, 0.0).astype(jnp.bfloat16)
    prob_far = jnp.where(near, 0.0, prob).astype(jnp.bfloat16)
    attn = attn + dot(own[:, HEAD:], prob_own, TN) + dot(far[:, HEAD:], prob_far, TN)
    keep(0, value_columns, dot(prob_own, grads, NN))
    keep(UNITS, value_columns, dot(prob_far, grads, NN))
    attn = attn.astype(jnp.bfloat16).astype(jnp.float32)
    delta = jnp.sum(attn * grads.astype(jnp.float32).T, axis=0, keepdims=True)
    attn_rows = attn.T.astype(jnp.bfloat16)
    out_ref[:, :HEAD] = attn_rows[:PAIR]
    out_ref[:, HEAD : 2 * HEAD] = attn_rows[PAIR:]
    scaled = share * SCALE
    query_grad = jnp.zeros((HEAD, width), jnp.float32)
    for step, keys in enumerate(others):
        prob = score_ref[step * PAIR : (step + 1) * PAIR, :] * scaled
        change = (prob * (dot(keys[:, HEAD:], grads, NT) - delta)).astype(jnp.bfloat16)
        query_grad = query_grad + dot(keys[:, :HEAD], change, TN)
        keep(step + 1, key_columns, dot(change, queries, NN))
    prob = score_ref[3 * PAIR :, :] * scaled
    grad_prob = jnp.where(near, dot(own[:, HEAD:], grads, NT), dot(far[:, HEAD:], grads, NT))
    change = prob * (grad_prob - delta)
    change_own = jnp.where(near, change, 0.0).astype(jnp.bfloat16)
    change_far = jnp.where(near, 0.0, change).astype(jnp.bfloat16)
    query_grad = query_grad + dot(own[:, :HEAD], change_own, TN)
    query_grad = query_grad + dot(far[:, :HEAD], change_far, TN)
    keep(0, key_columns, dot(change_own, queries, NN))
    keep(UNITS, key_columns, dot(change_far, queries, NN))
    grad_rows = query_grad.T.astype(jnp.bfloat16)
    out_ref[:, 2 * HEAD : 3 * HEAD] = grad_rows[:PAIR]
    out_ref[:, 3 * HEAD :] = grad_rows[PAIR:]
    edge_out_ref[...] = out_ref[:EDGE, :]


def merge_kernel(kept_ref, near_ref, back2_ref, back4_ref, sum_ref, give_ref):
    def read(ref, start, rows):
        return ref[start : start + rows].astype(jnp.float32)

    sum_ref[:PAIR] = kept_ref[...] + read(back2_ref, 0, PAIR) + read(back4_ref, 0, PAIR)
    sum_ref[PAIR:] = read(back2_ref, PAIR, EDGE) + read(back4_ref, PAIR, EDGE)
    give_ref[:PAIR] = (near_ref[...] + read(back2_ref, SPAN, PAIR)).astype(jnp.bfloat16)
    edge = kept_ref[:EDGE] + read(back2_ref, 0, EDGE) + read(back4_ref, 0, EDGE)
    give_ref[PAIR:] = edge.astype(jnp.bfloat16)


def swap_rows(out_ref, swap_ref):
    start = pl.multiple_of(jnp.where(lax.axis_index("yl") == 0, SPAN - SLOTS, 0), 16)
    swap_ref[...] = out_ref[pl.ds(start, SLOTS), :]


def span_kernel(rows_ref, edge_ref, out_ref, swap_ref):
    out_ref[:PAIR] = rows_ref[...]
    out_ref[PAIR:] = edge_ref[...]
    swap_rows(out_ref, swap_ref)


def total_kernel(sum_ref, back_ref, out_ref, swap_ref):
    out_ref[...] = (sum_ref[...] + back_ref[...].astype(jnp.float32)).astype(jnp.bfloat16)
    swap_rows(out_ref, swap_ref)


def place_kernel(facts_ref, rows_ref, swap_ref, first_ref, second_ref):
    start = facts_ref[3:4, 0:1]
    end = facts_ref[4:5, 0:1]
    slot = lax.broadcasted_iota(jnp.int32, (SLOTS, 1), 0)
    place = slot + (start - (pair_index() * PAIR - LEAD))
    live = slot < end - start
    partner_start = jnp.where(lax.axis_index("yl") == 0, 0, SPAN - SLOTS)
    own = picked(SLOTS, jnp.where(live, place, -1), rows_ref[...])
    other = picked(SLOTS, jnp.where(live, place - partner_start, -1), swap_ref[...])
    width = first_ref.shape[1] // 2

    def store(low, high):
        first_ref[:, :width] = low[:, :width]
        first_ref[:, width:] = high[:, :width]
        second_ref[:, :width] = low[:, width:]
        second_ref[:, width:] = high[:, width:]

    @pl.when(compute_member() == 0)
    def _():
        store(own, other)

    @pl.when(compute_member() == 1)
    def _():
        store(other, own)


def placed(facts, rows, swapped):
    width = rows.shape[1]
    return call(place_kernel, [shape(SLOTS, width)] * 2, [vmem()] * 3)(facts, rows, swapped)


def swapped(value):
    return lax.ppermute(value, "yl", [(0, 1), (1, 0)])


def shifted(value, steps):
    route = [
        (2 * pair + member, 2 * ((pair + steps) % PAIRS) + (member ^ (steps & 1)))
        for pair in range(PAIRS)
        for member in range(2)
    ]
    return lax.ppermute(value, SEQ_AXES, route)


def layer(q_old, k_old, value_old_layout, dout_old, old_offsets, new_offsets):
    wide, narrow, full = 4 * HEAD, 2 * HEAD, 6 * HEAD
    packed, facts = call(
        pack_kernel,
        [shape(8, 56, full), shape(8, HEAD, dtype=jnp.int32)],
        [pl.BlockSpec(memory_space=pltpu.HBM)] * 6,
        [
            pltpu.SMEM((2, old_offsets.shape[0]), jnp.int32),
            pltpu.SemaphoreType.DMA((32,)),
            pltpu.SemaphoreType.DMA((2,)),
        ],
        limit=60,
    )(k_old, value_old_layout, q_old, dout_old, old_offsets, new_offsets)
    slots = lax.all_to_all(packed, GROUP_AXES, 0, 0, tiled=True).reshape(2 * SLOTS, full)
    first, edge, rows = call(
        raw_kernel, [shape(SPAN, narrow), shape(EDGE, wide), shape(PAIR, wide)], [vmem()] * 2
    )(facts, slots)
    from_first = shifted(first, 1)
    from_edge = shifted(edge, 1)
    second, fourth = call(
        relay_kernel, [shape(SPAN + PAIR, narrow), shape(SPAN, narrow)], [vmem()] * 2
    )(first, from_first)
    from_second = shifted(second, 2)
    from_fourth = shifted(fourth, 4)
    results, result_edge, kept, near, give2, give4 = call(
        attend_kernel,
        [
            shape(PAIR, wide),
            shape(EDGE, wide),
            shape(PAIR, narrow, dtype=jnp.float32),
            shape(PAIR, narrow, dtype=jnp.float32),
            shape(SPAN + PAIR, narrow),
            shape(SPAN, narrow),
        ],
        [vmem()] * 6,
        [pltpu.VMEM((UNITS * PAIR, 2 * PAIR), jnp.float32)],
        flops=10**9,
        limit=24,
    )(rows, from_edge, second, from_first, from_second, from_fourth)
    back2 = shifted(give2, -2)
    back4 = shifted(give4, -4)
    back_edge = shifted(result_edge, -1)
    sums, give = call(
        merge_kernel, [shape(SPAN, narrow, dtype=jnp.float32), shape(SPAN, narrow)], [vmem()] * 4
    )(kept, near, back2, back4)
    back = shifted(give, -1)
    span_rows, row_swap = call(
        span_kernel, [shape(SPAN, wide), shape(SLOTS, wide)], [vmem()] * 2
    )(results, back_edge)
    other_rows = swapped(row_swap)
    totals, total_swap = call(
        total_kernel, [shape(SPAN, narrow), shape(SLOTS, narrow)], [vmem()] * 2
    )(sums, back)
    other_totals = swapped(total_swap)
    attn_out, grad_query_out = placed(facts, span_rows, other_rows)
    grad_key_out, grad_value_out = placed(facts, totals, other_totals)
    return attn_out, grad_query_out, grad_key_out, grad_value_out


def solution(mesh):
    cut = Mesh(mesh.devices.reshape(16, 2, 2, 2, 2, 2), AXES)
    rows = P(AXES, None)
    return jax.shard_map(
        layer,
        mesh=cut,
        in_specs=(rows, rows, rows, rows, P(), P()),
        out_specs=(P(SEQ_AXES, ("xl", "c")),) * 4,
        check_vma=False,
    )
```

time: 108 us -> 89.4 us (0.83)
  the two profiles are of different devices: /device:TPU:128 before, /device:TPU:8 now
where the time goes in v3:
time: 89.4 us; the launch traced here: 88.8 us
  waiting for transfers between devices  35.9 us (40%)
  starting transfers between devices  24.9 us (28%)
  blocking collectives  19.2 us (21%)
  Pallas kernels  8.08 us (9%)
    ppermute x8, waiting for transfers between devices, shifted(): return lax.ppermute(value, SEQ_AXES, route)  33 us
    ppermute x8, starting transfers between devices, shifted(): return lax.ppermute(value, SEQ_AXES, route)  19.9 us
    all_to_all x1, blocking collectives, layer(): lax.all_to_all(packed, GROUP_AXES, 0, 0, tiled=True)  19.2 us
    ppermute x2, starting transfers between devices, swapped(): return lax.ppermute(value, 'yl', [(0, 1), (1, 0)])  4.93 us
    ppermute x2, waiting for transfers between devices, swapped(): return lax.ppermute(value, 'yl', [(0, 1), (1, 0)])  2.9 us
    pallas_call x1, Pallas kernels, layer(): call(attend_kernel, [shape(PAIR, wide), shape(EDGE, wide), shape(PAIR, na...  2.84 us
    pallas_call x1, Pallas kernels, layer(): call(pack_kernel, [shape(8, 56, full), shape(8, HEAD, dtype=jnp.int32)],...  2.27 us
    pallas_call x2, Pallas kernels, placed(): call(place_kernel, [shape(SLOTS, width)] * 2, [vmem()] * 3)  2.24 us
  transfers between devices with their start and end apart: 10, of which 5 were waited for; matrix products, arithmetic and copies ran while one was open for 0% of the time, Pallas kernels for 2%

profile of v3, /device:TPU:8, one launch (start us, length us, event | category | flops | bytes accessed | tf_op | source)
XLA Modules:
  0.0 88.8 jit_solution(16556948036566379246)
XLA Ops:
  0.6 2.3 %shard_map.93 = (bf16[8,56,768]{2,1,0:T(8,128)(2,1)}, s32[8,128]{1,0:T(8,128)}) custom-call(bf16[56,1024]{1,0:T(8,128)(2,1)} %keys_ref.1, bf16[56,1024]{1,0:T(8,128)(2,1)} %values_ref.1, bf16[56,2048]{1,0:T(8,128)(2,1)} %queries_ref.1, bf16[56,2048]{1,0:T(8,128)(2,1)} %grads_ref.1, s32[129]{0:T(256)} %old_ref.1, s32[129]{0:T(256)} %new_ref.1), custom_call_target="tpu_custom_call" | custom-call | bytes 1048576 | tf_op jit(solution)/shard_map/pallas_call | solution.py:315
  2.9 0.0 copy-start
  2.9 19.2 %all_to_all.5 = bf16[8,56,768]{2,1,0:T(8,128)(2,1)S(1)} all-to-all(bf16[8,56,768]{2,1,0:T(8,128)(2,1)} %get-tuple-element.28), channel_id=1, replica_groups=mesh['z'=16,'xh'=2,'yh'=2,'yl'=2,'xl'=2,'c'=2] {'yl','xl','c'}, dimensions={0} | all-to-all | bytes 1376256 | tf_op jit(solution)/shard_map/all_to_all | solution.py:326
  22.2 0.0 copy-done
  22.2 0.5 shard_map.94
  22.7 1.9 %collective-permute-start.1 = (bf16[352,256]{1,0:T(8,128)(2,1)S(1)}, bf16[352,256]{1,0:T(8,128)(2,1)S(1)}, u32[]{:S(2)}, u32[]{:S(2)}) collective-permute-start(bf16[352,256]{1,0:T(8,128)(2,1)S(1)} %get-tuple-element.31.mine_ref), channel_id=1, source_target_pairs={{0,12},{4,8},{8,20},{12,16},{16,28},{20,24},{24,36},{28,32},{32,44... | collective-permute-start | bytes 540680 | tf_op jit(solution)/shard_map/ppermute | solution.py:310
  24.6 12.9 %collective-permute-done.1.first_ref = bf16[352,256]{1,0:T(8,128)(2,1)S(1)} collective-permute-done((bf16[352,256]{1,0:T(8,128)(2,1)S(1)}, bf16[352,256]{1,0:T(8,128)(2,1)S(1)}, u32[]{:S(2)}, u32[]{:S(2)}) %collective-permute-start.1) | collective-permute-done | bytes 180256 | tf_op jit(solution)/shard_map/ppermute | solution.py:310
  37.5 1.9 %collective-permute-start.2 = (bf16[608,256]{1,0:T(8,128)(2,1)S(1)}, bf16[608,256]{1,0:T(8,128)(2,1)S(1)}, u32[]{:S(2)}, u32[]{:S(2)}) collective-permute-start(bf16[608,256]{1,0:T(8,128)(2,1)S(1)} %get-tuple-element.32.mine_ref), channel_id=1, source_target_pairs={{0,16},{4,20},{8,24},{12,28},{16,32},{20,36},{24,40},{28,44},{32,4... | collective-permute-start | bytes 933896 | tf_op jit(solution)/shard_map/ppermute | solution.py:310
  39.5 1.9 %collective-permute-start.3 = (bf16[352,256]{1,0:T(8,128)(2,1)S(1)}, bf16[352,256]{1,0:T(8,128)(2,1)S(1)}, u32[]{:S(2)}, u32[]{:S(2)}) collective-permute-start(bf16[352,256]{1,0:T(8,128)(2,1)S(1)} %get-tuple-element.33), channel_id=1, source_target_pairs={{0,32},{4,36},{8,40},{12,44},{16,48},{20,52},{24,56},{28,60},{32,6... | collective-permute-start | bytes 540680 | tf_op jit(solution)/shard_map/ppermute | solution.py:310
  41.4 1.9 %collective-permute-start = (bf16[96,512]{1,0:T(8,128)(2,1)S(1)}, bf16[96,512]{1,0:T(8,128)(2,1)S(1)}, u32[]{:S(2)}, u32[]{:S(2)}) collective-permute-start(bf16[96,512]{1,0:T(8,128)(2,1)S(1)} %get-tuple-element.30), channel_id=1, source_target_pairs={{0,12},{4,8},{8,20},{12,16},{16,28},{20,24},{24,36},{28,32},{32,44... | collective-permute-start | bytes 294920 | tf_op jit(solution)/shard_map/ppermute | solution.py:310
  43.3 10.0 %collective-permute-done.edge_ref = bf16[96,512]{1,0:T(8,128)(2,1)S(1)} collective-permute-done((bf16[96,512]{1,0:T(8,128)(2,1)S(1)}, bf16[96,512]{1,0:T(8,128)(2,1)S(1)}, u32[]{:S(2)}, u32[]{:S(2)}) %collective-permute-start) | collective-permute-done | bytes 98336 | tf_op jit(solution)/shard_map/ppermute | solution.py:310
  53.3 0.0 collective-permute-done.3.fourth_ref
  53.3 0.0 collective-permute-done.2.second_ref
  53.3 2.8 %shard_map.96 = (bf16[256,512]{1,0:T(8,128)(2,1)S(1)}, bf16[96,512]{1,0:T(8,128)(2,1)S(1)}, f32[256,256]{1,0:T(8,128)S(1)}, f32[256,256]{1,0:T(8,128)S(1)}, bf16...) custom-call(bf16[256,512]{1,0:T(8,128)(2,1)S(1)} %get-tuple-element.29.rows_ref, ...), custom_call_target="tpu_custom_call" | custom-call | flops 1000000000 | bytes 1048576 | tf_op jit(solution)/shard_map/pallas_call | solution.py:337
  56.2 4.5 %collective-permute-start.6 = (bf16[608,256]{1,0:T(8,128)(2,1)S(1)}, bf16[608,256]{1,0:T(8,128)(2,1)S(1)}, u32[]{:S(2)}, u32[]{:S(2)}) collective-permute-start(bf16[608,256]{1,0:T(8,128)(2,1)S(1)} %get-tuple-element.42), channel_id=1, source_target_pairs={{0,496},{4,500},{8,504},{12,508},{16,0},{20,4},{24,8},{28,12},{32,... | collective-permute-start | bytes 933896 | tf_op jit(solution)/shard_map/ppermute | solution.py:310
  60.7 3.9 %collective-permute-start.7 = (bf16[352,256]{1,0:T(8,128)(2,1)S(1)}, bf16[352,256]{1,0:T(8,128)(2,1)S(1)}, u32[]{:S(2)}, u32[]{:S(2)}) collective-permute-start(bf16[352,256]{1,0:T(8,128)(2,1)S(1)} %get-tuple-element.43), channel_id=1, source_target_pairs={{0,480},{4,484},{8,488},{12,492},{16,496},{20,500},{24,504},{28,50... | collective-permute-start | bytes 540680 | tf_op jit(solution)/shard_map/ppermute | solution.py:310
  64.6 1.9 %collective-permute-start.4 = (bf16[96,512]{1,0:T(8,128)(2,1)S(1)}, bf16[96,512]{1,0:T(8,128)(2,1)S(1)}, u32[]{:S(2)}, u32[]{:S(2)}) collective-permute-start(bf16[96,512]{1,0:T(8,128)(2,1)S(1)} %get-tuple-element.35), channel_id=1, source_target_pairs={{0,508},{4,504},{8,4},{12,0},{16,12},{20,8},{24,20},{28,16},{32,28... | collective-permute-start | bytes 294920 | tf_op jit(solution)/shard_map/ppermute | solution.py:310
  66.6 7.0 %collective-permute-done.7.back4_ref = bf16[352,256]{1,0:T(8,128)(2,1)S(1)} collective-permute-done((bf16[352,256]{1,0:T(8,128)(2,1)S(1)}, bf16[352,256]{1,0:T(8,128)(2,1)S(1)}, u32[]{:S(2)}, u32[]{:S(2)}) %collective-permute-start.7) | collective-permute-done | bytes 180256 | tf_op jit(solution)/shard_map/ppermute | solution.py:310
  73.6 0.0 collective-permute-done.6.back2_ref
  73.6 0.1 shard_map.99
  73.7 1.9 %collective-permute-start.8 = (bf16[352,256]{1,0:T(8,128)(2,1)S(1)}, bf16[352,256]{1,0:T(8,128)(2,1)S(1)}, u32[]{:S(2)}, u32[]{:S(2)}) collective-permute-start(bf16[352,256]{1,0:T(8,128)(2,1)S(1)} %get-tuple-element.45), channel_id=1, source_target_pairs={{0,508},{4,504},{8,4},{12,0},{16,12},{20,8},{24,20},{28,16},{32,28... | collective-permute-start | bytes 540680 | tf_op jit(solution)/shard_map/ppermute | solution.py:310
  75.6 0.0 collective-permute-done.4.edge_ref
  75.7 2.4 %collective-permute-start.5 = (bf16[224,512]{1,0:T(8,128)(2,1)S(1)}, bf16[224,512]{1,0:T(8,128)(2,1)S(1)}, u32[]{:S(2)}, u32[]{:S(2)}) collective-permute-start(bf16[224,512]{1,0:T(8,128)(2,1)S(1)} %get-tuple-element.37), channel_id=1, source_target_pairs={{0,4},{4,0},{1,5},{5,1},{2,6},{6,2},{3,7},{7,3},{8,12},{12,8},{9,1... | collective-permute-start | bytes 688136 | tf_op jit(solution)/shard_map/ppermute | solution.py:301
  78.0 3.0 %collective-permute-done.8.back_ref = bf16[352,256]{1,0:T(8,128)(2,1)S(1)} collective-permute-done((bf16[352,256]{1,0:T(8,128)(2,1)S(1)}, bf16[352,256]{1,0:T(8,128)(2,1)S(1)}, u32[]{:S(2)}, u32[]{:S(2)}) %collective-permute-start.8) | collective-permute-done | bytes 180256 | tf_op jit(solution)/shard_map/ppermute | solution.py:310
  81.1 0.1 shard_map.100
  81.1 2.6 %collective-permute-start.9 = (bf16[224,256]{1,0:T(8,128)(2,1)S(1)}, bf16[224,256]{1,0:T(8,128)(2,1)S(1)}, u32[]{:S(2)}, u32[]{:S(2)}) collective-permute-start(bf16[224,256]{1,0:T(8,128)(2,1)S(1)} %get-tuple-element.47), channel_id=1, source_target_pairs={{0,4},{4,0},{1,5},{5,1},{2,6},{6,2},{3,7},{7,3},{8,12},{12,8},{9,1... | collective-permute-start | bytes 344072 | tf_op jit(solution)/shard_map/ppermute | solution.py:301
  83.7 0.0 collective-permute-done.5.swap_ref
  83.7 1.2 %shard_map.98 = (bf16[224,512]{1,0:T(8,128)(2,1)}, bf16[224,512]{1,0:T(8,128)(2,1)}) custom-call(s32[8,128]{1,0:T(8,128)S(1)} %copy-done, bf16[352,512]{1,0:T(8,128)(2,1)S(1)} %get-tuple-element.36.rows_ref, bf16[224,512]{1,0:T(8,128)(2,1)S(1)} %collective-permute-done.5.swap_ref), custom_call_target="tpu_custom_call" | custom-call | bytes 1048576 | tf_op jit(solution)/shard_map/pallas_call | solution.py:297
  84.9 2.9 %collective-permute-done.9.swap_ref = bf16[224,256]{1,0:T(8,128)(2,1)S(1)} collective-permute-done((bf16[224,256]{1,0:T(8,128)(2,1)S(1)}, bf16[224,256]{1,0:T(8,128)(2,1)S(1)}, u32[]{:S(2)}, u32[]{:S(2)}) %collective-permute-start.9) | collective-permute-done | bytes 114720 | tf_op jit(solution)/shard_map/ppermute | solution.py:301
  87.8 1.0 %shard_map.101 = (bf16[224,256]{1,0:T(8,128)(2,1)}, bf16[224,256]{1,0:T(8,128)(2,1)}) custom-call(s32[8,128]{1,0:T(8,128)S(1)} %copy-done, bf16[352,256]{1,0:T(8,128)(2,1)S(1)} %get-tuple-element.46.rows_ref, bf16[224,256]{1,0:T(8,128)(2,1)S(1)} %collective-permute-done.9.swap_ref), custom_call_target="tpu_custom_call" | custom-call | bytes 1048576 | tf_op jit(solution)/shard_map/pallas_call | solution.py:297
  (2 shorter events, 0.1 us)
Async XLA Ops:
  2.9 19.3 %copy-start = (s32[8,128]{1,0:T(8,128)S(1)}, s32[8,128]{1,0:T(8,128)}, u32[]{:S(2)}) copy-start(s32[8,128]{1,0:T(8,128)} %get-tuple-element.27.facts_ref) | copy-start | bytes 12292
  22.7 14.8 %collective-permute-start.1 = (bf16[352,256]{1,0:T(8,128)(2,1)S(1)}, bf16[352,256]{1,0:T(8,128)(2,1)S(1)}, u32[]{:S(2)}, u32[]{:S(2)}) collective-permute-start(bf16[352,256]{1,0:T(8,128)(2,1)S(1)} %get-tuple-element.31.mine_ref), channel_id=1, source_target_pairs={{0,12},{4,8},{8,20},{12,16},{16,28},{20,24},{24,36},{28,32},{32,44... | collective-permute-start | bytes 540680 | tf_op jit(solution)/shard_map/ppermute | solution.py:310
  37.5 15.8 %collective-permute-start.2 = (bf16[608,256]{1,0:T(8,128)(2,1)S(1)}, bf16[608,256]{1,0:T(8,128)(2,1)S(1)}, u32[]{:S(2)}, u32[]{:S(2)}) collective-permute-start(bf16[608,256]{1,0:T(8,128)(2,1)S(1)} %get-tuple-element.32.mine_ref), channel_id=1, source_target_pairs={{0,16},{4,20},{8,24},{12,28},{16,32},{20,36},{24,40},{28,44},{32,4... | collective-permute-start | bytes 933896 | tf_op jit(solution)/shard_map/ppermute | solution.py:310
  39.5 13.9 %collective-permute-start.3 = (bf16[352,256]{1,0:T(8,128)(2,1)S(1)}, bf16[352,256]{1,0:T(8,128)(2,1)S(1)}, u32[]{:S(2)}, u32[]{:S(2)}) collective-permute-start(bf16[352,256]{1,0:T(8,128)(2,1)S(1)} %get-tuple-element.33), channel_id=1, source_target_pairs={{0,32},{4,36},{8,40},{12,44},{16,48},{20,52},{24,56},{28,60},{32,6... | collective-permute-start | bytes 540680 | tf_op jit(solution)/shard_map/ppermute | solution.py:310
  41.4 12.0 %collective-permute-start = (bf16[96,512]{1,0:T(8,128)(2,1)S(1)}, bf16[96,512]{1,0:T(8,128)(2,1)S(1)}, u32[]{:S(2)}, u32[]{:S(2)}) collective-permute-start(bf16[96,512]{1,0:T(8,128)(2,1)S(1)} %get-tuple-element.30), channel_id=1, source_target_pairs={{0,12},{4,8},{8,20},{12,16},{16,28},{20,24},{24,36},{28,32},{32,44... | collective-permute-start | bytes 294920 | tf_op jit(solution)/shard_map/ppermute | solution.py:310
  56.2 17.4 %collective-permute-start.6 = (bf16[608,256]{1,0:T(8,128)(2,1)S(1)}, bf16[608,256]{1,0:T(8,128)(2,1)S(1)}, u32[]{:S(2)}, u32[]{:S(2)}) collective-permute-start(bf16[608,256]{1,0:T(8,128)(2,1)S(1)} %get-tuple-element.42), channel_id=1, source_target_pairs={{0,496},{4,500},{8,504},{12,508},{16,0},{20,4},{24,8},{28,12},{32,... | collective-permute-start | bytes 933896 | tf_op jit(solution)/shard_map/ppermute | solution.py:310
  60.7 12.9 %collective-permute-start.7 = (bf16[352,256]{1,0:T(8,128)(2,1)S(1)}, bf16[352,256]{1,0:T(8,128)(2,1)S(1)}, u32[]{:S(2)}, u32[]{:S(2)}) collective-permute-start(bf16[352,256]{1,0:T(8,128)(2,1)S(1)} %get-tuple-element.43), channel_id=1, source_target_pairs={{0,480},{4,484},{8,488},{12,492},{16,496},{20,500},{24,504},{28,50... | collective-permute-start | bytes 540680 | tf_op jit(solution)/shard_map/ppermute | solution.py:310
  64.6 11.0 %collective-permute-start.4 = (bf16[96,512]{1,0:T(8,128)(2,1)S(1)}, bf16[96,512]{1,0:T(8,128)(2,1)S(1)}, u32[]{:S(2)}, u32[]{:S(2)}) collective-permute-start(bf16[96,512]{1,0:T(8,128)(2,1)S(1)} %get-tuple-element.35), channel_id=1, source_target_pairs={{0,508},{4,504},{8,4},{12,0},{16,12},{20,8},{24,20},{28,16},{32,28... | collective-permute-start | bytes 294920 | tf_op jit(solution)/shard_map/ppermute | solution.py:310
  73.7 7.4 %collective-permute-start.8 = (bf16[352,256]{1,0:T(8,128)(2,1)S(1)}, bf16[352,256]{1,0:T(8,128)(2,1)S(1)}, u32[]{:S(2)}, u32[]{:S(2)}) collective-permute-start(bf16[352,256]{1,0:T(8,128)(2,1)S(1)} %get-tuple-element.45), channel_id=1, source_target_pairs={{0,508},{4,504},{8,4},{12,0},{16,12},{20,8},{24,20},{28,16},{32,28... | collective-permute-start | bytes 540680 | tf_op jit(solution)/shard_map/ppermute | solution.py:310
  75.7 8.0 %collective-permute-start.5 = (bf16[224,512]{1,0:T(8,128)(2,1)S(1)}, bf16[224,512]{1,0:T(8,128)(2,1)S(1)}, u32[]{:S(2)}, u32[]{:S(2)}) collective-permute-start(bf16[224,512]{1,0:T(8,128)(2,1)S(1)} %get-tuple-element.37), channel_id=1, source_target_pairs={{0,4},{4,0},{1,5},{5,1},{2,6},{6,2},{3,7},{7,3},{8,12},{12,8},{9,1... | collective-permute-start | bytes 688136 | tf_op jit(solution)/shard_map/ppermute | solution.py:301
  81.1 6.7 %collective-permute-start.9 = (bf16[224,256]{1,0:T(8,128)(2,1)S(1)}, bf16[224,256]{1,0:T(8,128)(2,1)S(1)}, u32[]{:S(2)}, u32[]{:S(2)}) collective-permute-start(bf16[224,256]{1,0:T(8,128)(2,1)S(1)} %get-tuple-element.47), channel_id=1, source_target_pairs={{0,4},{4,0},{1,5},{5,1},{2,6},{6,2},{3,7},{7,3},{8,12},{12,8},{9,1... | collective-permute-start | bytes 344072 | tf_op jit(solution)/shard_map/ppermute | solution.py:301

commit v4 on v3

--- a/solution.py
+++ b/solution.py
@@ -9,6 +9,7 @@
 PAIR = 256
 SLOTS = 224
 LEAD = 48
+EXTRA = 64
 EDGE = 96
 SPAN = PAIR + EDGE
 HEAD = 128
@@ -67,20 +68,13 @@
     return lax.axis_index("yl") ^ lax.axis_index("yh")
 
 
-def pack_kernel(
-    keys_ref, values_ref, queries_ref, grads_ref, old_ref, new_ref, out_ref, facts_ref,
-    offsets_ref, sems, offset_sems,
-):
-    old_copy = pltpu.make_async_copy(old_ref, offsets_ref.at[0], offset_sems.at[0])
-    new_copy = pltpu.make_async_copy(new_ref, offsets_ref.at[1], offset_sems.at[1])
-    old_copy.start()
-    new_copy.start()
+def start_packing(refs, out_ref, sems):
     mirrored = lax.axis_index("yh")
     copies = []
     for target in range(8):
         head = (target % 4) * 2 + ((target // 4) ^ mirrored)
         begin = 0
-        for ref in (keys_ref, values_ref, queries_ref, grads_ref):
+        for ref in refs:
             width = ref.shape[1] // 8
             source = ref.at[:, pl.ds(pl.multiple_of(head * width, HEAD), width)]
             copy = pltpu.make_async_copy(
@@ -89,8 +83,23 @@
             copy.start()
             copies.append(copy)
             begin += width
-    old_copy.wait()
-    new_copy.wait()
+    return copies
+
+
+def pack_kernel(first_ref, second_ref, out_ref, sems):
+    for copy in start_packing((first_ref, second_ref), out_ref, sems):
+        copy.wait()
+
+
+def facts_kernel(old_ref, new_ref, facts_ref, offsets_ref, sems):
+    copies = [
+        pltpu.make_async_copy(ref, offsets_ref.at[row], sems.at[row])
+        for row, ref in enumerate((old_ref, new_ref))
+    ]
+    for copy in copies:
+        copy.start()
+    for copy in copies:
+        copy.wait()
     pair = pair_index()
     block = 2 * pair + lax.axis_index("yl")
     facts = (
@@ -103,22 +112,26 @@
     for row, fact in enumerate(facts):
         facts_ref[row : row + 1, :] = jnp.full((1, HEAD), fact, jnp.int32)
     facts_ref[len(facts) :, :] = jnp.zeros((8 - len(facts), HEAD), jnp.int32)
-    for copy in copies:
-        copy.wait()
-
-
-def raw_kernel(facts_ref, slots_ref, first_ref, edge_ref, rows_ref):
-    start = pair_index() * PAIR - LEAD
-    place = lax.broadcasted_iota(jnp.int32, (SPAN, 1), 0) + start
+
+
+def raw_rows(facts_ref, slots_ref):
+    place = lax.broadcasted_iota(jnp.int32, (SPAN, 1), 0) + (pair_index() * PAIR - LEAD)
     first = facts_ref[0:1, 0:1]
     middle = facts_ref[1:2, 0:1]
     last = facts_ref[2:3, 0:1]
     source = jnp.where(place < middle, place - first, SLOTS + place - middle)
     source = jnp.where((place >= first) & (place < last), source, -1)
-    rows = picked(SPAN, source, slots_ref[...])
-    first_ref[...] = rows[:, : 2 * HEAD]
-    edge_ref[...] = rows[PAIR:, 2 * HEAD :]
-    rows_ref[...] = rows[:PAIR, 2 * HEAD :]
+    return picked(SPAN, source, slots_ref[...])
+
+
+def raw_keys_kernel(facts_ref, slots_ref, out_ref):
+    out_ref[...] = raw_rows(facts_ref, slots_ref)
+
+
+def raw_queries_kernel(facts_ref, slots_ref, edge_ref, rows_ref):
+    rows = raw_rows(facts_ref, slots_ref)
+    edge_ref[...] = rows[PAIR:]
+    rows_ref[...] = rows[:PAIR]
 
 
 def joined(rows, edge):
@@ -136,47 +149,55 @@
 
 
 def attend_kernel(
-    rows_ref, edge_ref, mine_ref, first_ref, second_ref, fourth_ref,
-    out_ref, edge_out_ref, kept_ref, near_ref, give2_ref, give4_ref, score_ref,
+    rows_ref, edge_ref, extra_ref, mine_ref, first_ref, second_ref, fourth_ref,
+    out_ref, edge_out_ref, extra_out_ref, kept_ref, near_ref, past_ref, give2_ref, give4_ref,
+    score_ref,
 ):
-    start = pair_index() * PAIR - LEAD
-    width = 2 * PAIR
+    pair = pair_index()
+    main = 2 * PAIR
+    width = main + 2 * EXTRA
     own = mine_ref[:PAIR]
+    past = mine_ref[PAIR : PAIR + EXTRA]
     far = fourth_ref[:PAIR]
     others = (
         joined(first_ref[:PAIR], second_ref[PAIR:SPAN]),
         second_ref[:PAIR],
         joined(second_ref[SPAN:], fourth_ref[PAIR:]),
     )
+    used = jnp.where(pair == PAIRS - 1, 1.0, 0.0).astype(jnp.bfloat16)
 
     def stacked(column):
-        parts = []
+        parts, extras = [], []
         for head in range(2):
             columns = slice(column + head * HEAD, column + (head + 1) * HEAD)
             parts.append(joined(rows_ref[:, columns], edge_ref[:, columns]))
-        return jnp.concatenate(parts, axis=0)
+            extras.append(extra_ref[:EXTRA, columns] * used)
+        return jnp.concatenate(parts + extras, axis=0)
 
     queries = stacked(0)
     grads = stacked(2 * HEAD)
     key_row = lax.broadcasted_iota(jnp.int32, (PAIR, width), 0)
-    query_row = lax.broadcasted_iota(jnp.int32, (PAIR, width), 1) & (PAIR - 1)
-    near = key_row <= query_row
-    column = lax.broadcasted_iota(jnp.int32, (1, width), 1) & (PAIR - 1)
-    positive = (column + start >= 0).astype(jnp.float32)
-    place = lax.broadcasted_iota(jnp.int32, (PAIR, 1), 0) + start
+    lane = lax.broadcasted_iota(jnp.int32, (PAIR, width), 1)
+    near = key_row <= jnp.where(lane < main, lane & (PAIR - 1), PAIR)
+    past_row = lax.broadcasted_iota(jnp.int32, (EXTRA, 2 * EXTRA), 0)
+    past_lane = lax.broadcasted_iota(jnp.int32, (EXTRA, 2 * EXTRA), 1)
+    beyond = past_row <= (past_lane & (EXTRA - 1))
+    place = lax.broadcasted_iota(jnp.int32, (PAIR, 1), 0) + (pair * PAIR - LEAD)
 
     def scores(keys, distance):
         bias = jnp.where(place - distance * PAIR >= 0, 0.0, OUTSIDE)
-        return dot(keys[:, :HEAD], queries, NT) * (SCALE * LOG2E) + bias * positive
-
+        return dot(keys[:, :HEAD], queries, NT) * (SCALE * LOG2E) + bias
+
+    corner = (slice(2 * PAIR, 2 * PAIR + EXTRA), slice(main, width))
+    for step, keys in enumerate(others):
+        score_ref[step * PAIR : (step + 1) * PAIR, :] = scores(keys, step + 1)
+    past_score = dot(past[:, :HEAD], queries[main:], NT) * (SCALE * LOG2E)
+    score_ref[corner] = jnp.where(beyond, past_score, score_ref[corner])
+    score_ref[3 * PAIR :, :] = jnp.where(near, scores(own, 0), scores(far, UNITS))
     top = jnp.full((1, width), OUTSIDE, jnp.float32)
-    for step, keys in enumerate(others):
-        score = scores(keys, step + 1)
-        score_ref[step * PAIR : (step + 1) * PAIR, :] = score
+    for step in range(UNITS):
+        score = score_ref[step * PAIR : (step + 1) * PAIR, :]
         top = jnp.maximum(top, jnp.max(score, axis=0, keepdims=True))
-    score = jnp.where(near, scores(own, 0), scores(far, UNITS))
-    score_ref[3 * PAIR :, :] = score
-    top = jnp.maximum(top, jnp.max(score, axis=0, keepdims=True))
     total = jnp.zeros((1, width), jnp.float32)
     for step in range(UNITS):
         weight = jnp.exp2(score_ref[step * PAIR : (step + 1) * PAIR, :] - top)
@@ -199,29 +220,57 @@
         else:
             give4_ref[:PAIR, columns] = rounded
 
+    def without_corner(value):
+        left = value[:EXTRA, :main]
+        right = jnp.where(beyond, 0.0, value[:EXTRA, main:])
+        return jnp.concatenate(
+            [jnp.concatenate([left, right], axis=1), value[EXTRA:]], axis=0
+        )
+
+    def widened(value):
+        return jnp.concatenate([jnp.zeros((HEAD, main), jnp.float32), value], axis=1)
+
     key_columns = slice(0, HEAD)
     value_columns = slice(HEAD, 2 * HEAD)
     attn = jnp.zeros((HEAD, width), jnp.float32)
     for step, keys in enumerate(others):
-        prob = (score_ref[step * PAIR : (step + 1) * PAIR, :] * share).astype(jnp.bfloat16)
+        prob = score_ref[step * PAIR : (step + 1) * PAIR, :] * share
+        if step == 2:
+            prob = without_corner(prob)
+        prob = prob.astype(jnp.bfloat16)
         attn = attn + dot(keys[:, HEAD:], prob, TN)
         keep(step + 1, value_columns, dot(prob, grads, NN))
     prob = score_ref[3 * PAIR :, :] * share
     prob_own = jnp.where(near, prob, 0.0).astype(jnp.bfloat16)
     prob_far = jnp.where(near, 0.0, prob).astype(jnp.bfloat16)
+    prob_past = score_ref[corner] * share[:, main:]
+    prob_past = jnp.where(beyond, prob_past, 0.0).astype(jnp.bfloat16)
     attn = attn + dot(own[:, HEAD:], prob_own, TN) + dot(far[:, HEAD:], prob_far, TN)
+    attn = attn + widened(dot(past[:, HEAD:], prob_past, TN))
     keep(0, value_columns, dot(prob_own, grads, NN))
     keep(UNITS, value_columns, dot(prob_far, grads, NN))
+    past_ref[:, value_columns] = dot(prob_past, grads[main:], NN)
     attn = attn.astype(jnp.bfloat16).astype(jnp.float32)
     delta = jnp.sum(attn * grads.astype(jnp.float32).T, axis=0, keepdims=True)
-    attn_rows = attn.T.astype(jnp.bfloat16)
-    out_ref[:, :HEAD] = attn_rows[:PAIR]
-    out_ref[:, HEAD : 2 * HEAD] = attn_rows[PAIR:]
+
+    def store(value, column):
+        rows = value.T.astype(jnp.bfloat16)
+        for head in range(2):
+            columns = slice(column + head * HEAD, column + (head + 1) * HEAD)
+            out_ref[:, columns] = rows[head * PAIR : (head + 1) * PAIR]
+            edge_out_ref[:, columns] = rows[head * PAIR : head * PAIR + EDGE]
+            start = main + head * EXTRA
+            extra_out_ref[:, columns] = rows[start : start + EXTRA]
+
+    store(attn, 0)
     scaled = share * SCALE
     query_grad = jnp.zeros((HEAD, width), jnp.float32)
     for step, keys in enumerate(others):
         prob = score_ref[step * PAIR : (step + 1) * PAIR, :] * scaled
-        change = (prob * (dot(keys[:, HEAD:], grads, NT) - delta)).astype(jnp.bfloat16)
+        change = prob * (dot(keys[:, HEAD:], grads, NT) - delta)
+        if step == 2:
+            change = without_corner(change)
+        change = change.astype(jnp.bfloat16)
         query_grad = query_grad + dot(keys[:, :HEAD], change, TN)
         keep(step + 1, key_columns, dot(change, queries, NN))
     prob = score_ref[3 * PAIR :, :] * scaled
@@ -229,22 +278,25 @@
     change = prob * (grad_prob - delta)
     change_own = jnp.where(near, change, 0.0).astype(jnp.bfloat16)
     change_far = jnp.where(near, 0.0, change).astype(jnp.bfloat16)
+    change = dot(past[:, HEAD:], grads[main:], NT) - delta[:, main:]
+    change = jnp.where(beyond, score_ref[corner] * scaled[:, main:] * change, 0.0)
+    change_past = change.astype(jnp.bfloat16)
     query_grad = query_grad + dot(own[:, :HEAD], change_own, TN)
     query_grad = query_grad + dot(far[:, :HEAD], change_far, TN)
+    query_grad = query_grad + widened(dot(past[:, :HEAD], change_past, TN))
     keep(0, key_columns, dot(change_own, queries, NN))
     keep(UNITS, key_columns, dot(change_far, queries, NN))
-    grad_rows = query_grad.T.astype(jnp.bfloat16)
-    out_ref[:, 2 * HEAD : 3 * HEAD] = grad_rows[:PAIR]
-    out_ref[:, 3 * HEAD :] = grad_rows[PAIR:]
-    edge_out_ref[...] = out_ref[:EDGE, :]
-
-
-def merge_kernel(kept_ref, near_ref, back2_ref, back4_ref, sum_ref, give_ref):
+    past_ref[:, key_columns] = dot(change_past, queries[main:], NN)
+    store(query_grad, 2 * HEAD)
+
+
+def merge_kernel(kept_ref, near_ref, past_ref, back2_ref, back4_ref, sum_ref, give_ref):
     def read(ref, start, rows):
         return ref[start : start + rows].astype(jnp.float32)
 
     sum_ref[:PAIR] = kept_ref[...] + read(back2_ref, 0, PAIR) + read(back4_ref, 0, PAIR)
     sum_ref[PAIR:] = read(back2_ref, PAIR, EDGE) + read(back4_ref, PAIR, EDGE)
+    sum_ref[PAIR : PAIR + EXTRA] = sum_ref[PAIR : PAIR + EXTRA] + past_ref[...]
     give_ref[:PAIR] = (near_ref[...] + read(back2_ref, SPAN, PAIR)).astype(jnp.bfloat16)
     edge = kept_ref[:EDGE] + read(back2_ref, 0, EDGE) + read(back4_ref, 0, EDGE)
     give_ref[PAIR:] = edge.astype(jnp.bfloat16)
@@ -255,9 +307,11 @@
     swap_ref[...] = out_ref[pl.ds(start, SLOTS), :]
 
 
-def span_kernel(rows_ref, edge_ref, out_ref, swap_ref):
+def span_kernel(rows_ref, edge_ref, extra_ref, out_ref, swap_ref):
+    last = pair_index() == PAIRS - 1
     out_ref[:PAIR] = rows_ref[...]
-    out_ref[PAIR:] = edge_ref[...]
+    out_ref[PAIR : PAIR + EXTRA] = jnp.where(last, extra_ref[...], edge_ref[:EXTRA])
+    out_ref[PAIR + EXTRA :] = edge_ref[EXTRA:]
     swap_rows(out_ref, swap_ref)
 
 
@@ -303,30 +357,40 @@
 
 def shifted(value, steps):
     route = [
-        (2 * pair + member, 2 * ((pair + steps) % PAIRS) + (member ^ (steps & 1)))
-        for pair in range(PAIRS)
+        (2 * pair + member, 2 * (pair + steps) + (member ^ (steps & 1)))
+        for pair in range(max(0, -steps), min(PAIRS, PAIRS - steps))
         for member in range(2)
     ]
     return lax.ppermute(value, SEQ_AXES, route)
 
 
 def layer(q_old, k_old, value_old_layout, dout_old, old_offsets, new_offsets):
-    wide, narrow, full = 4 * HEAD, 2 * HEAD, 6 * HEAD
-    packed, facts = call(
-        pack_kernel,
-        [shape(8, 56, full), shape(8, HEAD, dtype=jnp.int32)],
-        [pl.BlockSpec(memory_space=pltpu.HBM)] * 6,
+    wide, narrow = 4 * HEAD, 2 * HEAD
+    hbm = pl.BlockSpec(memory_space=pltpu.HBM)
+    copies = [pltpu.SemaphoreType.DMA((16,))]
+    packed_keys = call(
+        pack_kernel, shape(8, 56, narrow), [hbm] * 2, copies, limit=60
+    )(k_old, value_old_layout)
+    packed_queries = call(
+        pack_kernel, shape(8, 56, wide), [hbm] * 2, copies, limit=60
+    )(q_old, dout_old)
+    facts = call(
+        facts_kernel,
+        shape(8, HEAD, dtype=jnp.int32),
+        [hbm] * 2,
         [
             pltpu.SMEM((2, old_offsets.shape[0]), jnp.int32),
-            pltpu.SemaphoreType.DMA((32,)),
             pltpu.SemaphoreType.DMA((2,)),
         ],
-        limit=60,
-    )(k_old, value_old_layout, q_old, dout_old, old_offsets, new_offsets)
-    slots = lax.all_to_all(packed, GROUP_AXES, 0, 0, tiled=True).reshape(2 * SLOTS, full)
-    first, edge, rows = call(
-        raw_kernel, [shape(SPAN, narrow), shape(EDGE, wide), shape(PAIR, wide)], [vmem()] * 2
-    )(facts, slots)
+    )(old_offsets, new_offsets)
+    key_slots = lax.all_to_all(packed_keys, GROUP_AXES, 0, 0, tiled=True)
+    query_slots = lax.all_to_all(packed_queries, GROUP_AXES, 0, 0, tiled=True)
+    first = call(raw_keys_kernel, shape(SPAN, narrow), [vmem()] * 2)(
+        facts, key_slots.reshape(2 * SLOTS, narrow)
+    )
+    edge, rows = call(
+        raw_queries_kernel, [shape(EDGE, wide), shape(PAIR, wide)], [vmem()] * 2
+    )(facts, query_slots.reshape(2 * SLOTS, wide))
     from_first = shifted(first, 1)
     from_edge = shifted(edge, 1)
     second, fourth = call(
@@ -334,31 +398,33 @@
     )(first, from_first)
     from_second = shifted(second, 2)
     from_fourth = shifted(fourth, 4)
-    results, result_edge, kept, near, give2, give4 = call(
+    results, result_edge, result_extra, kept, near, past, give2, give4 = call(
         attend_kernel,
         [
             shape(PAIR, wide),
             shape(EDGE, wide),
+            shape(EXTRA, wide),
             shape(PAIR, narrow, dtype=jnp.float32),
             shape(PAIR, narrow, dtype=jnp.float32),
+            shape(EXTRA, narrow, dtype=jnp.float32),
             shape(SPAN + PAIR, narrow),
             shape(SPAN, narrow),
         ],
-        [vmem()] * 6,
-        [pltpu.VMEM((UNITS * PAIR, 2 * PAIR), jnp.float32)],
+        [vmem()] * 7,
+        [pltpu.VMEM((UNITS * PAIR, 2 * (PAIR + EXTRA)), jnp.float32)],
         flops=10**9,
         limit=24,
-    )(rows, from_edge, second, from_first, from_second, from_fourth)
+    )(rows, from_edge, edge, second, from_first, from_second, from_fourth)
     back2 = shifted(give2, -2)
     back4 = shifted(give4, -4)
     back_edge = shifted(result_edge, -1)
     sums, give = call(
-        merge_kernel, [shape(SPAN, narrow, dtype=jnp.float32), shape(SPAN, narrow)], [vmem()] * 4
-    )(kept, near, back2, back4)
+        merge_kernel, [shape(SPAN, narrow, dtype=jnp.float32), shape(SPAN, narrow)], [vmem()] * 5
+    )(kept, near, past, back2, back4)
     back = shifted(give, -1)
     span_rows, row_swap = call(
-        span_kernel, [shape(SPAN, wide), shape(SLOTS, wide)], [vmem()] * 2
-    )(results, back_edge)
+        span_kernel, [shape(SPAN, wide), shape(SLOTS, wide)], [vmem()] * 3
+    )(results, back_edge, result_extra)
     other_rows = swapped(row_swap)
     totals, total_swap = call(
         total_kernel, [shape(SPAN, narrow), shape(SLOTS, narrow)], [vmem()] * 2

time: 89.4 us -> 88.8 us (level)
  the two profiles are of different devices: /device:TPU:8 before, /device:TPU:98 now
where the time goes in v4:
time: 88.8 us; the launch traced here: 88.1 us
  starting transfers between devices  39 us (44%)
  waiting for transfers between devices  37.4 us (42%)
  Pallas kernels  10.9 us (12%)
    ppermute x8, waiting for transfers between devices, shifted(): return lax.ppermute(value, SEQ_AXES, route)  30.7 us
    ppermute x8, starting transfers between devices, shifted(): return lax.ppermute(value, SEQ_AXES, route)  26 us
    all_to_all x1, starting transfers between devices, layer(): query_slots = lax.all_to_all(packed_queries, GROUP_AXES, 0, 0, tiled=True)  4.84 us
    all_to_all x1, starting transfers between devices, layer(): key_slots = lax.all_to_all(packed_keys, GROUP_AXES, 0, 0, tiled=True)  4.32 us
    ppermute x2, starting transfers between devices, swapped(): return lax.ppermute(value, 'yl', [(0, 1), (1, 0)])  3.84 us
    ppermute x2, waiting for transfers between devices, swapped(): return lax.ppermute(value, 'yl', [(0, 1), (1, 0)])  3.54 us
    pallas_call x1, Pallas kernels, layer(): call(attend_kernel, [shape(PAIR, wide), shape(EDGE, wide), shape(EXTRA, w...  3.49 us
    all_to_all x1, waiting for transfers between devices, layer(): key_slots = lax.all_to_all(packed_keys, GROUP_AXES, 0, 0, tiled=True)  3.17 us
  transfers between devices with their start and end apart: 12, of which 6 were waited for; matrix products, arithmetic and copies ran while one was open for 0% of the time, Pallas kernels for 5%

profile of v4, /device:TPU:98, one launch (start us, length us, event | category | flops | bytes accessed | tf_op | source)
XLA Modules:
  0.0 88.1 jit_solution(10300836427765544679)
XLA Ops:
  0.6 1.7 %shard_map.96 = bf16[8,56,256]{2,1,0:T(8,128)(2,1)} custom-call(bf16[56,1024]{1,0:T(8,128)(2,1)} %first_ref.3, bf16[56,1024]{1,0:T(8,128)(2,1)} %second_ref.3), custom_call_target="tpu_custom_call" | custom-call | bytes 1048576 | tf_op jit(solution)/shard_map/pallas_call | solution.py:371
  2.4 4.3 %all-to-all-start.1 = ((bf16[8,56,256]{2,1,0:T(8,128)(2,1)}), bf16[8,56,256]{2,1,0:T(8,128)(2,1)S(1)}, u32[]{:S(2)}, u32[]{:S(2)}) async-start(bf16[8,56,256]{2,1,0:T(8,128)(2,1)} %shard_map.96), calls=%async_computation.1 | async-start | bytes 458752 | tf_op jit(solution)/shard_map/all_to_all | solution.py:386
  6.7 1.9 %shard_map.94 = bf16[8,56,512]{2,1,0:T(8,128)(2,1)} custom-call(bf16[56,2048]{1,0:T(8,128)(2,1)} %first_ref.2, bf16[56,2048]{1,0:T(8,128)(2,1)} %second_ref.2), custom_call_target="tpu_custom_call" | custom-call | bytes 1048576 | tf_op jit(solution)/shard_map/pallas_call | solution.py:374
  8.6 0.0 copy-start
  8.6 0.0 copy-start.1
  8.6 3.2 %all-to-all-done.1 = bf16[8,56,256]{2,1,0:T(8,128)(2,1)S(1)} async-done(((bf16[8,56,256]{2,1,0:T(8,128)(2,1)}), bf16[8,56,256]{2,1,0:T(8,128)(2,1)S(1)}, u32[]{:S(2)}, u32[]{:S(2)}) %all-to-all-start.1) | async-done | bytes 229408 | tf_op jit(solution)/shard_map/all_to_all | solution.py:386
  11.8 4.8 %all-to-all-start = ((bf16[8,56,512]{2,1,0:T(8,128)(2,1)}), bf16[8,56,512]{2,1,0:T(8,128)(2,1)S(1)}, u32[]{:S(2)}, u32[]{:S(2)}) async-start(bf16[8,56,512]{2,1,0:T(8,128)(2,1)} %shard_map.94), calls=%async_computation | async-start | bytes 917504 | tf_op jit(solution)/shard_map/all_to_all | solution.py:387
  16.6 0.0 copy-done
  16.6 0.0 copy-done.1
  16.6 0.6 shard_map.93.facts_ref
  17.2 0.3 shard_map.97.mine_ref
  17.6 4.8 %collective-permute-start.1 = (bf16[352,256]{1,0:T(8,128)(2,1)S(1)}, bf16[352,256]{1,0:T(8,128)(2,1)S(1)}, u32[]{:S(2)}, u32[]{:S(2)}) collective-permute-start(bf16[352,256]{1,0:T(8,128)(2,1)S(1)} %shard_map.97.mine_ref), channel_id=1, source_target_pairs={{0,12},{4,8},{8,20},{12,16},{16,28},{20,24},{24,36},{28,32},{32,44... | collective-permute-start | bytes 540680 | tf_op jit(solution)/shard_map/ppermute | solution.py:364
  22.4 8.2 %collective-permute-done.1.first_ref = bf16[352,256]{1,0:T(8,128)(2,1)S(1)} collective-permute-done((bf16[352,256]{1,0:T(8,128)(2,1)S(1)}, bf16[352,256]{1,0:T(8,128)(2,1)S(1)}, u32[]{:S(2)}, u32[]{:S(2)}) %collective-permute-start.1) | collective-permute-done | bytes 180256 | tf_op jit(solution)/shard_map/ppermute | solution.py:364
  30.7 3.7 %collective-permute-start.2 = (bf16[608,256]{1,0:T(8,128)(2,1)S(1)}, bf16[608,256]{1,0:T(8,128)(2,1)S(1)}, u32[]{:S(2)}, u32[]{:S(2)}) collective-permute-start(bf16[608,256]{1,0:T(8,128)(2,1)S(1)} %get-tuple-element.28.mine_ref), channel_id=1, source_target_pairs={{0,16},{4,20},{8,24},{12,28},{16,32},{20,36},{24,40},{28,44},{32,4... | collective-permute-start | bytes 933896 | tf_op jit(solution)/shard_map/ppermute | solution.py:364
  34.4 5.0 %collective-permute-start.3 = (bf16[352,256]{1,0:T(8,128)(2,1)S(1)}, bf16[352,256]{1,0:T(8,128)(2,1)S(1)}, u32[]{:S(2)}, u32[]{:S(2)}) collective-permute-start(bf16[352,256]{1,0:T(8,128)(2,1)S(1)} %get-tuple-element.29), channel_id=1, source_target_pairs={{0,32},{4,36},{8,40},{12,44},{16,48},{20,52},{24,56},{28,60},{32,6... | collective-permute-start | bytes 540680 | tf_op jit(solution)/shard_map/ppermute | solution.py:364
  39.5 0.0 all-to-all-done
  39.5 0.4 shard_map.95
  39.9 1.9 %collective-permute-start = (bf16[96,512]{1,0:T(8,128)(2,1)S(1)}, bf16[96,512]{1,0:T(8,128)(2,1)S(1)}, u32[]{:S(2)}, u32[]{:S(2)}) collective-permute-start(bf16[96,512]{1,0:T(8,128)(2,1)S(1)} %get-tuple-element.27.extra_ref), channel_id=1, source_target_pairs={{0,12},{4,8},{8,20},{12,16},{16,28},{20,24},{24,36},{28,32},{32,44... | collective-permute-start | bytes 294920 | tf_op jit(solution)/shard_map/ppermute | solution.py:364
  41.8 9.1 %collective-permute-done.edge_ref = bf16[96,512]{1,0:T(8,128)(2,1)S(1)} collective-permute-done((bf16[96,512]{1,0:T(8,128)(2,1)S(1)}, bf16[96,512]{1,0:T(8,128)(2,1)S(1)}, u32[]{:S(2)}, u32[]{:S(2)}) %collective-permute-start) | collective-permute-done | bytes 98336 | tf_op jit(solution)/shard_map/ppermute | solution.py:364
  50.9 0.0 collective-permute-done.3.fourth_ref
  50.9 0.0 collective-permute-done.2.second_ref
  50.9 3.5 %shard_map.99 = (bf16[256,512]{1,0:T(8,128)(2,1)S(1)}, bf16[96,512]{1,0:T(8,128)(2,1)S(1)}, bf16[64,512]{1,0:T(8,128)(2,1)S(1)}, f32[256,256]{1,0:T(8,128)S(1)},...) custom-call(bf16[256,512]{1,0:T(8,128)(2,1)S(1)} %get-tuple-element., ...), custom_call_target="tpu_custom_call" | custom-call | flops 1000000000 | bytes 1048576 | tf_op jit(solution)/shard_map/pallas_call | solution.py:401
  54.4 4.7 %collective-permute-start.6 = (bf16[608,256]{1,0:T(8,128)(2,1)S(1)}, bf16[608,256]{1,0:T(8,128)(2,1)S(1)}, u32[]{:S(2)}, u32[]{:S(2)}) collective-permute-start(bf16[608,256]{1,0:T(8,128)(2,1)S(1)} %get-tuple-element.40), channel_id=1, source_target_pairs={{16,0},{20,4},{24,8},{28,12},{32,16},{36,20},{40,24},{44,28},{48,3... | collective-permute-start | bytes 933896 | tf_op jit(solution)/shard_map/ppermute | solution.py:364
  59.2 1.9 %collective-permute-start.7 = (bf16[352,256]{1,0:T(8,128)(2,1)S(1)}, bf16[352,256]{1,0:T(8,128)(2,1)S(1)}, u32[]{:S(2)}, u32[]{:S(2)}) collective-permute-start(bf16[352,256]{1,0:T(8,128)(2,1)S(1)} %get-tuple-element.41), channel_id=1, source_target_pairs={{32,0},{36,4},{40,8},{44,12},{48,16},{52,20},{56,24},{60,28},{64,3... | collective-permute-start | bytes 540680 | tf_op jit(solution)/shard_map/ppermute | solution.py:364
  61.1 1.9 %collective-permute-start.4 = (bf16[96,512]{1,0:T(8,128)(2,1)S(1)}, bf16[96,512]{1,0:T(8,128)(2,1)S(1)}, u32[]{:S(2)}, u32[]{:S(2)}) collective-permute-start(bf16[96,512]{1,0:T(8,128)(2,1)S(1)} %get-tuple-element.31), channel_id=1, source_target_pairs={{8,4},{12,0},{16,12},{20,8},{24,20},{28,16},{32,28},{36,24},{40,36... | collective-permute-start | bytes 294920 | tf_op jit(solution)/shard_map/ppermute | solution.py:364
  63.0 8.6 %collective-permute-done.7.back4_ref = bf16[352,256]{1,0:T(8,128)(2,1)S(1)} collective-permute-done((bf16[352,256]{1,0:T(8,128)(2,1)S(1)}, bf16[352,256]{1,0:T(8,128)(2,1)S(1)}, u32[]{:S(2)}, u32[]{:S(2)}) %collective-permute-start.7) | collective-permute-done | bytes 180256 | tf_op jit(solution)/shard_map/ppermute | solution.py:364
  71.7 0.0 collective-permute-done.6.back2_ref
  71.7 0.1 shard_map.102
  71.8 1.9 %collective-permute-start.8 = (bf16[352,256]{1,0:T(8,128)(2,1)S(1)}, bf16[352,256]{1,0:T(8,128)(2,1)S(1)}, u32[]{:S(2)}, u32[]{:S(2)}) collective-permute-start(bf16[352,256]{1,0:T(8,128)(2,1)S(1)} %get-tuple-element.43), channel_id=1, source_target_pairs={{8,4},{12,0},{16,12},{20,8},{24,20},{28,16},{32,28},{36,24},{40,36... | collective-permute-start | bytes 540680 | tf_op jit(solution)/shard_map/ppermute | solution.py:364
  73.7 0.0 collective-permute-done.4.edge_ref
  73.8 1.9 %collective-permute-start.5 = (bf16[224,512]{1,0:T(8,128)(2,1)S(1)}, bf16[224,512]{1,0:T(8,128)(2,1)S(1)}, u32[]{:S(2)}, u32[]{:S(2)}) collective-permute-start(bf16[224,512]{1,0:T(8,128)(2,1)S(1)} %get-tuple-element.34), channel_id=1, source_target_pairs={{0,4},{4,0},{1,5},{5,1},{2,6},{6,2},{3,7},{7,3},{8,12},{12,8},{9,1... | collective-permute-start | bytes 688136 | tf_op jit(solution)/shard_map/ppermute | solution.py:355
  75.7 4.7 %collective-permute-done.8.back_ref = bf16[352,256]{1,0:T(8,128)(2,1)S(1)} collective-permute-done((bf16[352,256]{1,0:T(8,128)(2,1)S(1)}, bf16[352,256]{1,0:T(8,128)(2,1)S(1)}, u32[]{:S(2)}, u32[]{:S(2)}) %collective-permute-start.8) | collective-permute-done | bytes 180256 | tf_op jit(solution)/shard_map/ppermute | solution.py:364
  80.4 0.1 shard_map.103
  80.4 1.9 %collective-permute-start.9 = (bf16[224,256]{1,0:T(8,128)(2,1)S(1)}, bf16[224,256]{1,0:T(8,128)(2,1)S(1)}, u32[]{:S(2)}, u32[]{:S(2)}) collective-permute-start(bf16[224,256]{1,0:T(8,128)(2,1)S(1)} %get-tuple-element.45), channel_id=1, source_target_pairs={{0,4},{4,0},{1,5},{5,1},{2,6},{6,2},{3,7},{7,3},{8,12},{12,8},{9,1... | collective-permute-start | bytes 344072 | tf_op jit(solution)/shard_map/ppermute | solution.py:355
  82.4 0.0 collective-permute-done.5.swap_ref
  82.4 1.2 %shard_map.101 = (bf16[224,512]{1,0:T(8,128)(2,1)}, bf16[224,512]{1,0:T(8,128)(2,1)}) custom-call(s32[8,128]{1,0:T(8,128)S(1)} %shard_map.93.facts_ref, bf16[352,512]{1,0:T(8,128)(2,1)S(1)} %get-tuple-element.33.rows_ref, bf16[224,512]{1,0:T(8,128)(2,1)S(1)} %collective-permute-done.5.swap_ref), custom_call_target="tpu_custom_call" | custom-call | bytes 1048576 | tf_op jit(solution)/shard_map/pallas_call | solution.py:351
  83.6 3.5 %collective-permute-done.9.swap_ref = bf16[224,256]{1,0:T(8,128)(2,1)S(1)} collective-permute-done((bf16[224,256]{1,0:T(8,128)(2,1)S(1)}, bf16[224,256]{1,0:T(8,128)(2,1)S(1)}, u32[]{:S(2)}, u32[]{:S(2)}) %collective-permute-start.9) | collective-permute-done | bytes 114720 | tf_op jit(solution)/shard_map/ppermute | solution.py:355
  87.1 1.0 %shard_map.104 = (bf16[224,256]{1,0:T(8,128)(2,1)}, bf16[224,256]{1,0:T(8,128)(2,1)}) custom-call(s32[8,128]{1,0:T(8,128)S(1)} %shard_map.93.facts_ref, bf16[352,256]{1,0:T(8,128)(2,1)S(1)} %get-tuple-element.44.rows_ref, bf16[224,256]{1,0:T(8,128)(2,1)S(1)} %collective-permute-done.9.swap_ref), custom_call_target="tpu_custom_call" | custom-call | bytes 1048576 | tf_op jit(solution)/shard_map/pallas_call | solution.py:351
  (2 shorter events, 0.1 us)
Async XLA Ops:
  2.4 9.4 %all-to-all-start.1 = ((bf16[8,56,256]{2,1,0:T(8,128)(2,1)}), bf16[8,56,256]{2,1,0:T(8,128)(2,1)S(1)}, u32[]{:S(2)}, u32[]{:S(2)}) async-start(bf16[8,56,256]{2,1,0:T(8,128)(2,1)} %shard_map.96), calls=%async_computation.1 | async-start | bytes 458752 | tf_op jit(solution)/shard_map/all_to_all | solution.py:386
  8.6 8.0 %copy-start = (s32[129]{0:T(256)S(1)}, s32[129]{0:T(256)}, u32[]{:S(2)}) copy-start(s32[129]{0:T(256)} %old_ref.1) | copy-start | bytes 1552
  8.6 8.0 %copy-start.1 = (s32[129]{0:T(256)S(1)}, s32[129]{0:T(256)}, u32[]{:S(2)}) copy-start(s32[129]{0:T(256)} %new_ref.1) | copy-start | bytes 1552
  11.8 27.7 %all-to-all-start = ((bf16[8,56,512]{2,1,0:T(8,128)(2,1)}), bf16[8,56,512]{2,1,0:T(8,128)(2,1)S(1)}, u32[]{:S(2)}, u32[]{:S(2)}) async-start(bf16[8,56,512]{2,1,0:T(8,128)(2,1)} %shard_map.94), calls=%async_computation | async-start | bytes 917504 | tf_op jit(solution)/shard_map/all_to_all | solution.py:387
  17.6 13.1 %collective-permute-start.1 = (bf16[352,256]{1,0:T(8,128)(2,1)S(1)}, bf16[352,256]{1,0:T(8,128)(2,1)S(1)}, u32[]{:S(2)}, u32[]{:S(2)}) collective-permute-start(bf16[352,256]{1,0:T(8,128)(2,1)S(1)} %shard_map.97.mine_ref), channel_id=1, source_target_pairs={{0,12},{4,8},{8,20},{12,16},{16,28},{20,24},{24,36},{28,32},{32,44... | collective-permute-start | bytes 540680 | tf_op jit(solution)/shard_map/ppermute | solution.py:364
  30.7 20.2 %collective-permute-start.2 = (bf16[608,256]{1,0:T(8,128)(2,1)S(1)}, bf16[608,256]{1,0:T(8,128)(2,1)S(1)}, u32[]{:S(2)}, u32[]{:S(2)}) collective-permute-start(bf16[608,256]{1,0:T(8,128)(2,1)S(1)} %get-tuple-element.28.mine_ref), channel_id=1, source_target_pairs={{0,16},{4,20},{8,24},{12,28},{16,32},{20,36},{24,40},{28,44},{32,4... | collective-permute-start | bytes 933896 | tf_op jit(solution)/shard_map/ppermute | solution.py:364
  34.4 16.5 %collective-permute-start.3 = (bf16[352,256]{1,0:T(8,128)(2,1)S(1)}, bf16[352,256]{1,0:T(8,128)(2,1)S(1)}, u32[]{:S(2)}, u32[]{:S(2)}) collective-permute-start(bf16[352,256]{1,0:T(8,128)(2,1)S(1)} %get-tuple-element.29), channel_id=1, source_target_pairs={{0,32},{4,36},{8,40},{12,44},{16,48},{20,52},{24,56},{28,60},{32,6... | collective-permute-start | bytes 540680 | tf_op jit(solution)/shard_map/ppermute | solution.py:364
  39.9 11.0 %collective-permute-start = (bf16[96,512]{1,0:T(8,128)(2,1)S(1)}, bf16[96,512]{1,0:T(8,128)(2,1)S(1)}, u32[]{:S(2)}, u32[]{:S(2)}) collective-permute-start(bf16[96,512]{1,0:T(8,128)(2,1)S(1)} %get-tuple-element.27.extra_ref), channel_id=1, source_target_pairs={{0,12},{4,8},{8,20},{12,16},{16,28},{20,24},{24,36},{28,32},{32,44... | collective-permute-start | bytes 294920 | tf_op jit(solution)/shard_map/ppermute | solution.py:364
  54.4 17.2 %collective-permute-start.6 = (bf16[608,256]{1,0:T(8,128)(2,1)S(1)}, bf16[608,256]{1,0:T(8,128)(2,1)S(1)}, u32[]{:S(2)}, u32[]{:S(2)}) collective-permute-start(bf16[608,256]{1,0:T(8,128)(2,1)S(1)} %get-tuple-element.40), channel_id=1, source_target_pairs={{16,0},{20,4},{24,8},{28,12},{32,16},{36,20},{40,24},{44,28},{48,3... | collective-permute-start | bytes 933896 | tf_op jit(solution)/shard_map/ppermute | solution.py:364
  59.2 12.5 %collective-permute-start.7 = (bf16[352,256]{1,0:T(8,128)(2,1)S(1)}, bf16[352,256]{1,0:T(8,128)(2,1)S(1)}, u32[]{:S(2)}, u32[]{:S(2)}) collective-permute-start(bf16[352,256]{1,0:T(8,128)(2,1)S(1)} %get-tuple-element.41), channel_id=1, source_target_pairs={{32,0},{36,4},{40,8},{44,12},{48,16},{52,20},{56,24},{60,28},{64,3... | collective-permute-start | bytes 540680 | tf_op jit(solution)/shard_map/ppermute | solution.py:364
  61.1 12.6 %collective-permute-start.4 = (bf16[96,512]{1,0:T(8,128)(2,1)S(1)}, bf16[96,512]{1,0:T(8,128)(2,1)S(1)}, u32[]{:S(2)}, u32[]{:S(2)}) collective-permute-start(bf16[96,512]{1,0:T(8,128)(2,1)S(1)} %get-tuple-element.31), channel_id=1, source_target_pairs={{8,4},{12,0},{16,12},{20,8},{24,20},{28,16},{32,28},{36,24},{40,36... | collective-permute-start | bytes 294920 | tf_op jit(solution)/shard_map/ppermute | solution.py:364
  71.8 8.6 %collective-permute-start.8 = (bf16[352,256]{1,0:T(8,128)(2,1)S(1)}, bf16[352,256]{1,0:T(8,128)(2,1)S(1)}, u32[]{:S(2)}, u32[]{:S(2)}) collective-permute-start(bf16[352,256]{1,0:T(8,128)(2,1)S(1)} %get-tuple-element.43), channel_id=1, source_target_pairs={{8,4},{12,0},{16,12},{20,8},{24,20},{28,16},{32,28},{36,24},{40,36... | collective-permute-start | bytes 540680 | tf_op jit(solution)/shard_map/ppermute | solution.py:364
  73.8 8.6 %collective-permute-start.5 = (bf16[224,512]{1,0:T(8,128)(2,1)S(1)}, bf16[224,512]{1,0:T(8,128)(2,1)S(1)}, u32[]{:S(2)}, u32[]{:S(2)}) collective-permute-start(bf16[224,512]{1,0:T(8,128)(2,1)S(1)} %get-tuple-element.34), channel_id=1, source_target_pairs={{0,4},{4,0},{1,5},{5,1},{2,6},{6,2},{3,7},{7,3},{8,12},{12,8},{9,1... | collective-permute-start | bytes 688136 | tf_op jit(solution)/shard_map/ppermute | solution.py:355
  80.4 6.7 %collective-permute-start.9 = (bf16[224,256]{1,0:T(8,128)(2,1)S(1)}, bf16[224,256]{1,0:T(8,128)(2,1)S(1)}, u32[]{:S(2)}, u32[]{:S(2)}) collective-permute-start(bf16[224,256]{1,0:T(8,128)(2,1)S(1)} %get-tuple-element.45), channel_id=1, source_target_pairs={{0,4},{4,0},{1,5},{5,1},{2,6},{6,2},{3,7},{7,3},{8,12},{12,8},{9,1... | collective-permute-start | bytes 344072 | tf_op jit(solution)/shard_map/ppermute | solution.py:355

commit v5 on v4

--- a/solution.py
+++ b/solution.py
@@ -10,6 +10,7 @@
 SLOTS = 224
 LEAD = 48
 EXTRA = 64
+HALF = PAIR // 2
 EDGE = 96
 SPAN = PAIR + EDGE
 HEAD = 128
@@ -148,146 +149,213 @@
     fourth_ref[PAIR:] = edge
 
 
-def attend_kernel(
-    rows_ref, edge_ref, extra_ref, mine_ref, first_ref, second_ref, fourth_ref,
-    out_ref, edge_out_ref, extra_out_ref, kept_ref, near_ref, past_ref, give2_ref, give4_ref,
-    score_ref,
-):
-    pair = pair_index()
-    main = 2 * PAIR
-    width = main + 2 * EXTRA
-    own = mine_ref[:PAIR]
-    past = mine_ref[PAIR : PAIR + EXTRA]
-    far = fourth_ref[:PAIR]
-    others = (
+def attend(queries, grads, full, near_block, far_block, past, score_ref, give):
+    width = queries.shape[0]
+    near_keys, near_bias = near_block
+    far_keys, far_bias = far_block
+    starts = [0]
+    for keys, _ in full:
+        starts.append(starts[-1] + keys.shape[0])
+    spans = [slice(low, high) for low, high in zip(starts, starts[1:])]
+    mixed = slice(starts[-1], starts[-1] + HALF)
+    lane = lax.broadcasted_iota(jnp.int32, (HALF, width), 1)
+    row = lax.broadcasted_iota(jnp.int32, (HALF, width), 0)
+    near = row <= jnp.where(lane < PAIR, lane & (HALF - 1), HALF)
+    corner = (slice(starts[2], starts[2] + EXTRA), slice(PAIR, width))
+    if past is not None:
+        past_lane = lax.broadcasted_iota(jnp.int32, (EXTRA, width - PAIR), 1)
+        past_row = lax.broadcasted_iota(jnp.int32, (EXTRA, width - PAIR), 0)
+        beyond = past_row <= (past_lane & (EXTRA - 1))
+
+    def scores(keys, bias):
+        return dot(keys[:, :HEAD], queries, NT) * (SCALE * LOG2E) + bias
+
+    def without_corner(value):
+        left = value[:EXTRA, :PAIR]
+        right = jnp.where(beyond, 0.0, value[:EXTRA, PAIR:])
+        return jnp.concatenate([jnp.concatenate([left, right], axis=1), value[EXTRA:]], axis=0)
+
+    def widened(value):
+        return jnp.concatenate([jnp.zeros((HEAD, PAIR), jnp.float32), value], axis=1)
+
+    for (keys, bias), span in zip(full, spans):
+        score_ref[span, :] = scores(keys, bias)
+    if past is not None:
+        past_score = dot(past[:, :HEAD], queries[PAIR:], NT) * (SCALE * LOG2E)
+        score_ref[corner] = jnp.where(beyond, past_score, score_ref[corner])
+    score_ref[mixed, :] = jnp.where(near, scores(near_keys, near_bias), scores(far_keys, far_bias))
+    top = jnp.full((1, width), OUTSIDE, jnp.float32)
+    for span in spans + [mixed]:
+        top = jnp.maximum(top, jnp.max(score_ref[span, :], axis=0, keepdims=True))
+    total = jnp.zeros((1, width), jnp.float32)
+    for span in spans + [mixed]:
+        weight = jnp.exp2(score_ref[span, :] - top)
+        score_ref[span, :] = weight
+        total = total + jnp.sum(weight, axis=0, keepdims=True)
+    share = 1.0 / total
+    key_columns = slice(0, HEAD)
+    value_columns = slice(HEAD, 2 * HEAD)
+    attn = jnp.zeros((HEAD, width), jnp.float32)
+    for index, ((keys, _), span) in enumerate(zip(full, spans)):
+        prob = score_ref[span, :] * share
+        if index == 2 and past is not None:
+            prob = without_corner(prob)
+        prob = prob.astype(jnp.bfloat16)
+        attn = attn + dot(keys[:, HEAD:], prob, TN)
+        give(index, value_columns, dot(prob, grads, NN))
+    prob = score_ref[mixed, :] * share
+    prob_near = jnp.where(near, prob, 0.0).astype(jnp.bfloat16)
+    prob_far = jnp.where(near, 0.0, prob).astype(jnp.bfloat16)
+    attn = attn + dot(near_keys[:, HEAD:], prob_near, TN) + dot(far_keys[:, HEAD:], prob_far, TN)
+    give("near", value_columns, dot(prob_near, grads, NN))
+    give("far", value_columns, dot(prob_far, grads, NN))
+    if past is not None:
+        prob_past = score_ref[corner] * share[:, PAIR:]
+        prob_past = jnp.where(beyond, prob_past, 0.0).astype(jnp.bfloat16)
+        attn = attn + widened(dot(past[:, HEAD:], prob_past, TN))
+        give("past", value_columns, dot(prob_past, grads[PAIR:], NN))
+    attn = attn.astype(jnp.bfloat16).astype(jnp.float32)
+    delta = jnp.sum(attn * grads.astype(jnp.float32).T, axis=0, keepdims=True)
+    scaled = share * SCALE
+    query_grad = jnp.zeros((HEAD, width), jnp.float32)
+    for index, ((keys, _), span) in enumerate(zip(full, spans)):
+        change = score_ref[span, :] * scaled * (dot(keys[:, HEAD:], grads, NT) - delta)
+        if index == 2 and past is not None:
+            change = without_corner(change)
+        change = change.astype(jnp.bfloat16)
+        query_grad = query_grad + dot(keys[:, :HEAD], change, TN)
+        give(index, key_columns, dot(change, queries, NN))
+    grad_prob = jnp.where(
+        near, dot(near_keys[:, HEAD:], grads, NT), dot(far_keys[:, HEAD:], grads, NT)
+    )
+    change = score_ref[mixed, :] * scaled * (grad_prob - delta)
+    change_near = jnp.where(near, change, 0.0).astype(jnp.bfloat16)
+    change_far = jnp.where(near, 0.0, change).astype(jnp.bfloat16)
+    query_grad = query_grad + dot(near_keys[:, :HEAD], change_near, TN)
+    query_grad = query_grad + dot(far_keys[:, :HEAD], change_far, TN)
+    give("near", key_columns, dot(change_near, queries, NN))
+    give("far", key_columns, dot(change_far, queries, NN))
+    if past is not None:
+        change = dot(past[:, HEAD:], grads[PAIR:], NT) - delta[:, PAIR:]
+        change = jnp.where(beyond, score_ref[corner] * scaled[:, PAIR:] * change, 0.0)
+        change = change.astype(jnp.bfloat16)
+        query_grad = query_grad + widened(dot(past[:, :HEAD], change, TN))
+        give("past", key_columns, dot(change, queries[PAIR:], NN))
+    return attn.T.astype(jnp.bfloat16), query_grad.T.astype(jnp.bfloat16)
+
+
+def key_units(mine_ref, first_ref, second_ref, fourth_ref):
+    place = lax.broadcasted_iota(jnp.int32, (PAIR, 1), 0) + (pair_index() * PAIR - LEAD)
+    units = (
+        mine_ref[:PAIR],
         joined(first_ref[:PAIR], second_ref[PAIR:SPAN]),
         second_ref[:PAIR],
         joined(second_ref[SPAN:], fourth_ref[PAIR:]),
-    )
-    used = jnp.where(pair == PAIRS - 1, 1.0, 0.0).astype(jnp.bfloat16)
-
-    def stacked(column):
-        parts, extras = [], []
-        for head in range(2):
-            columns = slice(column + head * HEAD, column + (head + 1) * HEAD)
-            parts.append(joined(rows_ref[:, columns], edge_ref[:, columns]))
-            extras.append(extra_ref[:EXTRA, columns] * used)
-        return jnp.concatenate(parts + extras, axis=0)
-
-    queries = stacked(0)
-    grads = stacked(2 * HEAD)
-    key_row = lax.broadcasted_iota(jnp.int32, (PAIR, width), 0)
-    lane = lax.broadcasted_iota(jnp.int32, (PAIR, width), 1)
-    near = key_row <= jnp.where(lane < main, lane & (PAIR - 1), PAIR)
-    past_row = lax.broadcasted_iota(jnp.int32, (EXTRA, 2 * EXTRA), 0)
-    past_lane = lax.broadcasted_iota(jnp.int32, (EXTRA, 2 * EXTRA), 1)
-    beyond = past_row <= (past_lane & (EXTRA - 1))
-    place = lax.broadcasted_iota(jnp.int32, (PAIR, 1), 0) + (pair * PAIR - LEAD)
-
-    def scores(keys, distance):
-        bias = jnp.where(place - distance * PAIR >= 0, 0.0, OUTSIDE)
-        return dot(keys[:, :HEAD], queries, NT) * (SCALE * LOG2E) + bias
-
-    corner = (slice(2 * PAIR, 2 * PAIR + EXTRA), slice(main, width))
-    for step, keys in enumerate(others):
-        score_ref[step * PAIR : (step + 1) * PAIR, :] = scores(keys, step + 1)
-    past_score = dot(past[:, :HEAD], queries[main:], NT) * (SCALE * LOG2E)
-    score_ref[corner] = jnp.where(beyond, past_score, score_ref[corner])
-    score_ref[3 * PAIR :, :] = jnp.where(near, scores(own, 0), scores(far, UNITS))
-    top = jnp.full((1, width), OUTSIDE, jnp.float32)
-    for step in range(UNITS):
-        score = score_ref[step * PAIR : (step + 1) * PAIR, :]
-        top = jnp.maximum(top, jnp.max(score, axis=0, keepdims=True))
-    total = jnp.zeros((1, width), jnp.float32)
-    for step in range(UNITS):
-        weight = jnp.exp2(score_ref[step * PAIR : (step + 1) * PAIR, :] - top)
-        score_ref[step * PAIR : (step + 1) * PAIR, :] = weight
-        total = total + jnp.sum(weight, axis=0, keepdims=True)
-    share = 1.0 / total
-
-    def keep(step, columns, value):
+        fourth_ref[:PAIR],
+    )
+    return [
+        (unit, jnp.where(place - distance * PAIR >= 0, 0.0, OUTSIDE))
+        for distance, unit in enumerate(units)
+    ]
+
+
+def halves(unit):
+    keys, bias = unit
+    return (keys[:HALF], bias[:HALF]), (keys[HALF:], bias[HALF:])
+
+
+def head_columns(base):
+    return [slice(base + head * HEAD, base + (head + 1) * HEAD) for head in range(2)]
+
+
+def late_kernel(
+    rows_ref, extra_ref, mine_ref, first_ref, second_ref, fourth_ref,
+    out_ref, extra_out_ref, sums_ref, past_ref, score_ref,
+):
+    units = key_units(mine_ref, first_ref, second_ref, fourth_ref)
+    own_low, own_high = halves(units[0])
+    _, far_high = halves(units[4])
+    used = jnp.where(pair_index() == PAIRS - 1, 1.0, 0.0).astype(jnp.bfloat16)
+
+    def stacked(base):
+        parts = [rows_ref[HALF:, columns] for columns in head_columns(base)]
+        parts += [extra_ref[:EXTRA, columns] * used for columns in head_columns(base)]
+        return jnp.concatenate(parts, axis=0)
+
+    def give(index, columns, value):
+        if index == "past":
+            past_ref[:, columns] = value
+            return
+        start = {0: 0, 1: PAIR, 2: 2 * PAIR, 3: 3 * PAIR, "near": 3 * PAIR + HALF, "far": 4 * PAIR}
+        start = start[index]
+        sums_ref[start : start + value.shape[0], columns] = value
+
+    results = attend(
+        stacked(0),
+        stacked(2 * HEAD),
+        [units[1], units[2], units[3], own_low],
+        own_high,
+        far_high,
+        mine_ref[PAIR : PAIR + EXTRA],
+        score_ref,
+        give,
+    )
+    for base, value in zip((0, 2 * HEAD), results):
+        for head, columns in enumerate(head_columns(base)):
+            out_ref[:, columns] = value[head * HALF : (head + 1) * HALF]
+            start = PAIR + head * EXTRA
+            extra_out_ref[:, columns] = value[start : start + EXTRA]
+
+
+def early_kernel(
+    rows_ref, edge_ref, late_ref, sums_ref, mine_ref, first_ref, second_ref, fourth_ref,
+    out_ref, edge_out_ref, kept_ref, near_ref, give2_ref, give4_ref, score_ref,
+):
+    units = key_units(mine_ref, first_ref, second_ref, fourth_ref)
+    own_low, _ = halves(units[0])
+    far_low, far_high = halves(units[4])
+
+    def stacked(base):
+        parts = [joined(rows_ref[:HALF, c], edge_ref[:, c]) for c in head_columns(base)]
+        return jnp.concatenate(parts, axis=0)
+
+    def give(index, columns, value):
+        if index == "far":
+            give4_ref[:HALF, columns] = value.astype(jnp.bfloat16)
+            return
+        start = {0: 0, 1: PAIR, 2: 2 * PAIR, 3: 4 * PAIR, "near": 3 * PAIR}[index]
+        value = value + sums_ref[start : start + value.shape[0], columns]
         rounded = value.astype(jnp.bfloat16)
-        if step == 0:
-            kept_ref[:, columns] = value
-        elif step == 1:
+        if index == 0:
             near_ref[:, columns] = value
             give2_ref[PAIR:SPAN, columns] = rounded[:EDGE]
-        elif step == 2:
+        elif index == 1:
             give2_ref[:PAIR, columns] = rounded
-        elif step == 3:
+        elif index == 2:
             give2_ref[SPAN:, columns] = rounded
             give4_ref[PAIR:, columns] = rounded[:EDGE]
+        elif index == 3:
+            give4_ref[HALF:PAIR, columns] = rounded
         else:
-            give4_ref[:PAIR, columns] = rounded
-
-    def without_corner(value):
-        left = value[:EXTRA, :main]
-        right = jnp.where(beyond, 0.0, value[:EXTRA, main:])
-        return jnp.concatenate(
-            [jnp.concatenate([left, right], axis=1), value[EXTRA:]], axis=0
-        )
-
-    def widened(value):
-        return jnp.concatenate([jnp.zeros((HEAD, main), jnp.float32), value], axis=1)
-
-    key_columns = slice(0, HEAD)
-    value_columns = slice(HEAD, 2 * HEAD)
-    attn = jnp.zeros((HEAD, width), jnp.float32)
-    for step, keys in enumerate(others):
-        prob = score_ref[step * PAIR : (step + 1) * PAIR, :] * share
-        if step == 2:
-            prob = without_corner(prob)
-        prob = prob.astype(jnp.bfloat16)
-        attn = attn + dot(keys[:, HEAD:], prob, TN)
-        keep(step + 1, value_columns, dot(prob, grads, NN))
-    prob = score_ref[3 * PAIR :, :] * share
-    prob_own = jnp.where(near, prob, 0.0).astype(jnp.bfloat16)
-    prob_far = jnp.where(near, 0.0, prob).astype(jnp.bfloat16)
-    prob_past = score_ref[corner] * share[:, main:]
-    prob_past = jnp.where(beyond, prob_past, 0.0).astype(jnp.bfloat16)
-    attn = attn + dot(own[:, HEAD:], prob_own, TN) + dot(far[:, HEAD:], prob_far, TN)
-    attn = attn + widened(dot(past[:, HEAD:], prob_past, TN))
-    keep(0, value_columns, dot(prob_own, grads, NN))
-    keep(UNITS, value_columns, dot(prob_far, grads, NN))
-    past_ref[:, value_columns] = dot(prob_past, grads[main:], NN)
-    attn = attn.astype(jnp.bfloat16).astype(jnp.float32)
-    delta = jnp.sum(attn * grads.astype(jnp.float32).T, axis=0, keepdims=True)
-
-    def store(value, column):
-        rows = value.T.astype(jnp.bfloat16)
-        for head in range(2):
-            columns = slice(column + head * HEAD, column + (head + 1) * HEAD)
-            out_ref[:, columns] = rows[head * PAIR : (head + 1) * PAIR]
-            edge_out_ref[:, columns] = rows[head * PAIR : head * PAIR + EDGE]
-            start = main + head * EXTRA
-            extra_out_ref[:, columns] = rows[start : start + EXTRA]
-
-    store(attn, 0)
-    scaled = share * SCALE
-    query_grad = jnp.zeros((HEAD, width), jnp.float32)
-    for step, keys in enumerate(others):
-        prob = score_ref[step * PAIR : (step + 1) * PAIR, :] * scaled
-        change = prob * (dot(keys[:, HEAD:], grads, NT) - delta)
-        if step == 2:
-            change = without_corner(change)
-        change = change.astype(jnp.bfloat16)
-        query_grad = query_grad + dot(keys[:, :HEAD], change, TN)
-        keep(step + 1, key_columns, dot(change, queries, NN))
-    prob = score_ref[3 * PAIR :, :] * scaled
-    grad_prob = jnp.where(near, dot(own[:, HEAD:], grads, NT), dot(far[:, HEAD:], grads, NT))
-    change = prob * (grad_prob - delta)
-    change_own = jnp.where(near, change, 0.0).astype(jnp.bfloat16)
-    change_far = jnp.where(near, 0.0, change).astype(jnp.bfloat16)
-    change = dot(past[:, HEAD:], grads[main:], NT) - delta[:, main:]
-    change = jnp.where(beyond, score_ref[corner] * scaled[:, main:] * change, 0.0)
-    change_past = change.astype(jnp.bfloat16)
-    query_grad = query_grad + dot(own[:, :HEAD], change_own, TN)
-    query_grad = query_grad + dot(far[:, :HEAD], change_far, TN)
-    query_grad = query_grad + widened(dot(past[:, :HEAD], change_past, TN))
-    keep(0, key_columns, dot(change_own, queries, NN))
-    keep(UNITS, key_columns, dot(change_far, queries, NN))
-    past_ref[:, key_columns] = dot(change_past, queries[main:], NN)
-    store(query_grad, 2 * HEAD)
+            kept_ref[:HALF, columns] = value
+
+    kept_ref[HALF:] = sums_ref[3 * PAIR + HALF : 4 * PAIR]
+    results = attend(
+        stacked(0),
+        stacked(2 * HEAD),
+        [units[1], units[2], units[3], far_high],
+        own_low,
+        far_low,
+        None,
+        score_ref,
+        give,
+    )
+    for base, value in zip((0, 2 * HEAD), results):
+        for head, columns in enumerate(head_columns(base)):
+            part = value[head * HALF : (head + 1) * HALF]
+            out_ref[:HALF, columns] = part
+            edge_out_ref[:, columns] = part[:EDGE]
+    out_ref[HALF:] = late_ref[...]
 
 
 def merge_kernel(kept_ref, near_ref, past_ref, back2_ref, back4_ref, sum_ref, give_ref):
@@ -398,27 +466,39 @@
     )(first, from_first)
     from_second = shifted(second, 2)
     from_fourth = shifted(fourth, 4)
-    results, result_edge, result_extra, kept, near, past, give2, give4 = call(
-        attend_kernel,
+    window = (second, from_first, from_second, from_fourth)
+    late, result_extra, sums, past = call(
+        late_kernel,
+        [
+            shape(HALF, wide),
+            shape(EXTRA, wide),
+            shape(4 * PAIR + HALF, narrow, dtype=jnp.float32),
+            shape(EXTRA, narrow, dtype=jnp.float32),
+        ],
+        [vmem()] * 6,
+        [pltpu.VMEM((UNITS * PAIR, PAIR + 2 * EXTRA), jnp.float32)],
+        flops=10**9,
+        limit=20,
+    )(rows, edge, *window)
+    results, result_edge, kept, near, give2, give4 = call(
+        early_kernel,
         [
             shape(PAIR, wide),
             shape(EDGE, wide),
-            shape(EXTRA, wide),
             shape(PAIR, narrow, dtype=jnp.float32),
             shape(PAIR, narrow, dtype=jnp.float32),
-            shape(EXTRA, narrow, dtype=jnp.float32),
             shape(SPAN + PAIR, narrow),
             shape(SPAN, narrow),
         ],
-        [vmem()] * 7,
-        [pltpu.VMEM((UNITS * PAIR, 2 * (PAIR + EXTRA)), jnp.float32)],
+        [vmem()] * 8,
+        [pltpu.VMEM((UNITS * PAIR, PAIR), jnp.float32)],
         flops=10**9,
-        limit=24,
-    )(rows, from_edge, edge, second, from_first, from_second, from_fourth)
+        limit=20,
+    )(rows, from_edge, late, sums, *window)
     back2 = shifted(give2, -2)
     back4 = shifted(give4, -4)
     back_edge = shifted(result_edge, -1)
-    sums, give = call(
+    totals_here, give = call(
         merge_kernel, [shape(SPAN, narrow, dtype=jnp.float32), shape(SPAN, narrow)], [vmem()] * 5
     )(kept, near, past, back2, back4)
     back = shifted(give, -1)
@@ -428,7 +508,7 @@
     other_rows = swapped(row_swap)
     totals, total_swap = call(
         total_kernel, [shape(SPAN, narrow), shape(SLOTS, narrow)], [vmem()] * 2
-    )(sums, back)
+    )(totals_here, back)
     other_totals = swapped(total_swap)
     attn_out, grad_query_out = placed(facts, span_rows, other_rows)
     grad_key_out, grad_value_out = placed(facts, totals, other_totals)

time: 88.8 us -> 83.1 us (0.936)
  the two profiles are of different devices: /device:TPU:98 before, /device:TPU:252 now
where the time goes in v5:
time: 83.1 us; the launch traced here: 82.2 us
  starting transfers between devices  40.3 us (48%)
  waiting for transfers between devices  27.5 us (33%)
  Pallas kernels  12.2 us (15%)
  local copies, waits for them, and re-layouts  1.36 us (2%)
    ppermute x8, starting transfers between devices, shifted(): return lax.ppermute(value, SEQ_AXES, route)  27.6 us
    ppermute x8, waiting for transfers between devices, shifted(): return lax.ppermute(value, SEQ_AXES, route)  13.8 us
    all_to_all x1, waiting for transfers between devices, layer(): query_slots = lax.all_to_all(packed_queries, GROUP_AXES, 0, 0, tiled=True)  7.06 us
    ppermute x2, starting transfers between devices, swapped(): return lax.ppermute(value, 'yl', [(0, 1), (1, 0)])  4.72 us
    all_to_all x1, starting transfers between devices, layer(): key_slots = lax.all_to_all(packed_keys, GROUP_AXES, 0, 0, tiled=True)  4.08 us
    all_to_all x1, starting transfers between devices, layer(): query_slots = lax.all_to_all(packed_queries, GROUP_AXES, 0, 0, tiled=True)  3.92 us
    ppermute x2, waiting for transfers between devices, swapped(): return lax.ppermute(value, 'yl', [(0, 1), (1, 0)])  3.54 us
    all_to_all x1, waiting for transfers between devices, layer(): key_slots = lax.all_to_all(packed_keys, GROUP_AXES, 0, 0, tiled=True)  3.11 us
  transfers between devices with their start and end apart: 12, of which 8 were waited for; matrix products, arithmetic and copies ran while one was open for 0% of the time, Pallas kernels for 9%

profile of v5, /device:TPU:252, one launch (start us, length us, event | category | flops | bytes accessed | tf_op | source)
XLA Modules:
  0.0 82.2 jit_solution(18399588921067475424)
XLA Ops:
  0.6 1.7 %shard_map.96 = bf16[8,56,256]{2,1,0:T(8,128)(2,1)} custom-call(bf16[56,1024]{1,0:T(8,128)(2,1)} %first_ref.3, bf16[56,1024]{1,0:T(8,128)(2,1)} %second_ref.3), custom_call_target="tpu_custom_call" | custom-call | bytes 1048576 | tf_op jit(solution)/shard_map/pallas_call | solution.py:439
  2.4 4.1 %all-to-all-start.1 = ((bf16[8,56,256]{2,1,0:T(8,128)(2,1)}), bf16[8,56,256]{2,1,0:T(8,128)(2,1)S(1)}, u32[]{:S(2)}, u32[]{:S(2)}) async-start(bf16[8,56,256]{2,1,0:T(8,128)(2,1)} %shard_map.96), calls=%async_computation.1 | async-start | bytes 458752 | tf_op jit(solution)/shard_map/all_to_all | solution.py:454
  6.4 0.0 copy-start
  6.4 0.7 copy-done
  7.1 0.0 copy-start.1
  7.1 0.7 copy-done.1
  7.8 0.6 shard_map.93.facts_ref
  8.4 3.1 %all-to-all-done.1 = bf16[8,56,256]{2,1,0:T(8,128)(2,1)S(1)} async-done(((bf16[8,56,256]{2,1,0:T(8,128)(2,1)}), bf16[8,56,256]{2,1,0:T(8,128)(2,1)S(1)}, u32[]{:S(2)}, u32[]{:S(2)}) %all-to-all-start.1) | async-done | bytes 229408 | tf_op jit(solution)/shard_map/all_to_all | solution.py:454
  11.5 0.3 shard_map.97.mine_ref
  11.9 5.8 %collective-permute-start.1 = (bf16[352,256]{1,0:T(8,128)(2,1)S(1)}, bf16[352,256]{1,0:T(8,128)(2,1)S(1)}, u32[]{:S(2)}, u32[]{:S(2)}) collective-permute-start(bf16[352,256]{1,0:T(8,128)(2,1)S(1)} %shard_map.97.mine_ref), channel_id=1, source_target_pairs={{0,12},{4,8},{8,20},{12,16},{16,28},{20,24},{24,36},{28,32},{32,44... | collective-permute-start | bytes 540680 | tf_op jit(solution)/shard_map/ppermute | solution.py:432
  17.7 1.9 %shard_map.94 = bf16[8,56,512]{2,1,0:T(8,128)(2,1)} custom-call(bf16[56,2048]{1,0:T(8,128)(2,1)} %first_ref.2, bf16[56,2048]{1,0:T(8,128)(2,1)} %second_ref.2), custom_call_target="tpu_custom_call" | custom-call | bytes 1048576 | tf_op jit(solution)/shard_map/pallas_call | solution.py:442
  19.6 3.9 %all-to-all-start = ((bf16[8,56,512]{2,1,0:T(8,128)(2,1)}), bf16[8,56,512]{2,1,0:T(8,128)(2,1)S(1)}, u32[]{:S(2)}, u32[]{:S(2)}) async-start(bf16[8,56,512]{2,1,0:T(8,128)(2,1)} %shard_map.94), calls=%async_computation | async-start | bytes 917504 | tf_op jit(solution)/shard_map/all_to_all | solution.py:455
  23.5 0.0 collective-permute-done.1.first_ref
  23.6 4.2 %collective-permute-start.2 = (bf16[608,256]{1,0:T(8,128)(2,1)S(1)}, bf16[608,256]{1,0:T(8,128)(2,1)S(1)}, u32[]{:S(2)}, u32[]{:S(2)}) collective-permute-start(bf16[608,256]{1,0:T(8,128)(2,1)S(1)} %get-tuple-element.30.mine_ref), channel_id=1, source_target_pairs={{0,16},{4,20},{8,24},{12,28},{16,32},{20,36},{24,40},{28,44},{32,4... | collective-permute-start | bytes 933896 | tf_op jit(solution)/shard_map/ppermute | solution.py:432
  27.7 2.9 %collective-permute-start.3 = (bf16[352,256]{1,0:T(8,128)(2,1)S(1)}, bf16[352,256]{1,0:T(8,128)(2,1)S(1)}, u32[]{:S(2)}, u32[]{:S(2)}) collective-permute-start(bf16[352,256]{1,0:T(8,128)(2,1)S(1)} %get-tuple-element.31), channel_id=1, source_target_pairs={{0,32},{4,36},{8,40},{12,44},{16,48},{20,52},{24,56},{28,60},{32,6... | collective-permute-start | bytes 540680 | tf_op jit(solution)/shard_map/ppermute | solution.py:432
  30.7 7.1 %all-to-all-done = bf16[8,56,512]{2,1,0:T(8,128)(2,1)S(1)} async-done(((bf16[8,56,512]{2,1,0:T(8,128)(2,1)}), bf16[8,56,512]{2,1,0:T(8,128)(2,1)S(1)}, u32[]{:S(2)}, u32[]{:S(2)}) %all-to-all-start) | async-done | bytes 458784 | tf_op jit(solution)/shard_map/all_to_all | solution.py:455
  37.7 0.4 shard_map.95
  38.1 1.9 %collective-permute-start = (bf16[96,512]{1,0:T(8,128)(2,1)S(1)}, bf16[96,512]{1,0:T(8,128)(2,1)S(1)}, u32[]{:S(2)}, u32[]{:S(2)}) collective-permute-start(bf16[96,512]{1,0:T(8,128)(2,1)S(1)} %get-tuple-element.29.extra_ref), channel_id=1, source_target_pairs={{0,12},{4,8},{8,20},{12,16},{16,28},{20,24},{24,36},{28,32},{32,44... | collective-permute-start | bytes 294920 | tf_op jit(solution)/shard_map/ppermute | solution.py:432
  40.1 0.0 collective-permute-done.3.fourth_ref
  40.1 0.0 collective-permute-done.2.second_ref
  40.1 2.8 %shard_map.99 = (bf16[128,512]{1,0:T(8,128)(2,1)S(1)}, bf16[64,512]{1,0:T(8,128)(2,1)S(1)}, f32[1152,256]{1,0:T(8,128)S(1)}, f32[64,256]{1,0:T(8,128)S(1)}) custom-call(bf16[256,512]{1,0:T(8,128)(2,1)S(1)} %get-tuple-element.28.rows_ref, bf16[96,512]{1,0:T(8,128)(2,1)S(1)} %get-tuple-element.29.extra_ref, bf16[608,256]{1,0:T(8,128)(2,1)S(1)} %get-tuple-element.30.mine_ref, ...), custom_call_target="tpu_custom_call" | custom-call | flops 1000000000 | bytes 1048576 | tf_op jit(solution)/shard_map/pallas_call | solution.py:470
  42.9 3.0 %collective-permute-done.edge_ref = bf16[96,512]{1,0:T(8,128)(2,1)S(1)} collective-permute-done((bf16[96,512]{1,0:T(8,128)(2,1)S(1)}, bf16[96,512]{1,0:T(8,128)(2,1)S(1)}, u32[]{:S(2)}, u32[]{:S(2)}) %collective-permute-start) | collective-permute-done | bytes 98336 | tf_op jit(solution)/shard_map/ppermute | solution.py:432
  45.9 2.0 %shard_map.100 = (bf16[256,512]{1,0:T(8,128)(2,1)S(1)}, bf16[96,512]{1,0:T(8,128)(2,1)S(1)}, f32[256,256]{1,0:T(8,128)S(1)}, f32[256,256]{1,0:T(8,128)S(1)}, bf1...) custom-call(bf16[256,512]{1,0:T(8,128)(2,1)S(1)} %get-tuple-element.28.rows_ref, ...), custom_call_target="tpu_custom_call" | custom-call | flops 1000000000 | bytes 1048576 | tf_op jit(solution)/shard_map/pallas_call | solution.py:483
  47.9 2.2 %collective-permute-start.6 = (bf16[608,256]{1,0:T(8,128)(2,1)S(1)}, bf16[608,256]{1,0:T(8,128)(2,1)S(1)}, u32[]{:S(2)}, u32[]{:S(2)}) collective-permute-start(bf16[608,256]{1,0:T(8,128)(2,1)S(1)} %get-tuple-element.44), channel_id=1, source_target_pairs={{16,0},{20,4},{24,8},{28,12},{32,16},{36,20},{40,24},{44,28},{48,3... | collective-permute-start | bytes 933896 | tf_op jit(solution)/shard_map/ppermute | solution.py:432
  50.1 2.0 %collective-permute-start.7 = (bf16[352,256]{1,0:T(8,128)(2,1)S(1)}, bf16[352,256]{1,0:T(8,128)(2,1)S(1)}, u32[]{:S(2)}, u32[]{:S(2)}) collective-permute-start(bf16[352,256]{1,0:T(8,128)(2,1)S(1)} %get-tuple-element.45), channel_id=1, source_target_pairs={{32,0},{36,4},{40,8},{44,12},{48,16},{52,20},{56,24},{60,28},{64,3... | collective-permute-start | bytes 540680 | tf_op jit(solution)/shard_map/ppermute | solution.py:432
  52.1 4.3 %collective-permute-start.4 = (bf16[96,512]{1,0:T(8,128)(2,1)S(1)}, bf16[96,512]{1,0:T(8,128)(2,1)S(1)}, u32[]{:S(2)}, u32[]{:S(2)}) collective-permute-start(bf16[96,512]{1,0:T(8,128)(2,1)S(1)} %get-tuple-element.35), channel_id=1, source_target_pairs={{8,4},{12,0},{16,12},{20,8},{24,20},{28,16},{32,28},{36,24},{40,36... | collective-permute-start | bytes 294920 | tf_op jit(solution)/shard_map/ppermute | solution.py:432
  56.4 2.2 %collective-permute-done.7.back4_ref = bf16[352,256]{1,0:T(8,128)(2,1)S(1)} collective-permute-done((bf16[352,256]{1,0:T(8,128)(2,1)S(1)}, bf16[352,256]{1,0:T(8,128)(2,1)S(1)}, u32[]{:S(2)}, u32[]{:S(2)}) %collective-permute-start.7) | collective-permute-done | bytes 180256 | tf_op jit(solution)/shard_map/ppermute | solution.py:432
  58.7 2.5 %collective-permute-done.6.back2_ref = bf16[608,256]{1,0:T(8,128)(2,1)S(1)} collective-permute-done((bf16[608,256]{1,0:T(8,128)(2,1)S(1)}, bf16[608,256]{1,0:T(8,128)(2,1)S(1)}, u32[]{:S(2)}, u32[]{:S(2)}) %collective-permute-start.6) | collective-permute-done | bytes 311328 | tf_op jit(solution)/shard_map/ppermute | solution.py:432
  61.2 0.1 shard_map.103
  61.3 4.2 %collective-permute-start.8 = (bf16[352,256]{1,0:T(8,128)(2,1)S(1)}, bf16[352,256]{1,0:T(8,128)(2,1)S(1)}, u32[]{:S(2)}, u32[]{:S(2)}) collective-permute-start(bf16[352,256]{1,0:T(8,128)(2,1)S(1)} %get-tuple-element.47), channel_id=1, source_target_pairs={{8,4},{12,0},{16,12},{20,8},{24,20},{28,16},{32,28},{36,24},{40,36... | collective-permute-start | bytes 540680 | tf_op jit(solution)/shard_map/ppermute | solution.py:432
  65.5 0.4 collective-permute-done.4.edge_ref
  66.0 2.8 %collective-permute-start.5 = (bf16[224,512]{1,0:T(8,128)(2,1)S(1)}, bf16[224,512]{1,0:T(8,128)(2,1)S(1)}, u32[]{:S(2)}, u32[]{:S(2)}) collective-permute-start(bf16[224,512]{1,0:T(8,128)(2,1)S(1)} %get-tuple-element.38), channel_id=1, source_target_pairs={{0,4},{4,0},{1,5},{5,1},{2,6},{6,2},{3,7},{7,3},{8,12},{12,8},{9,1... | collective-permute-start | bytes 688136 | tf_op jit(solution)/shard_map/ppermute | solution.py:423
  68.8 5.6 %collective-permute-done.8.back_ref = bf16[352,256]{1,0:T(8,128)(2,1)S(1)} collective-permute-done((bf16[352,256]{1,0:T(8,128)(2,1)S(1)}, bf16[352,256]{1,0:T(8,128)(2,1)S(1)}, u32[]{:S(2)}, u32[]{:S(2)}) %collective-permute-start.8) | collective-permute-done | bytes 180256 | tf_op jit(solution)/shard_map/ppermute | solution.py:432
  74.4 0.1 shard_map.104
  74.5 1.9 %collective-permute-start.9 = (bf16[224,256]{1,0:T(8,128)(2,1)S(1)}, bf16[224,256]{1,0:T(8,128)(2,1)S(1)}, u32[]{:S(2)}, u32[]{:S(2)}) collective-permute-start(bf16[224,256]{1,0:T(8,128)(2,1)S(1)} %get-tuple-element.49), channel_id=1, source_target_pairs={{0,4},{4,0},{1,5},{5,1},{2,6},{6,2},{3,7},{7,3},{8,12},{12,8},{9,1... | collective-permute-start | bytes 344072 | tf_op jit(solution)/shard_map/ppermute | solution.py:423
  76.4 0.0 collective-permute-done.5.swap_ref
  76.4 1.2 %shard_map.102 = (bf16[224,512]{1,0:T(8,128)(2,1)}, bf16[224,512]{1,0:T(8,128)(2,1)}) custom-call(s32[8,128]{1,0:T(8,128)S(1)} %shard_map.93.facts_ref, bf16[352,512]{1,0:T(8,128)(2,1)S(1)} %get-tuple-element.37.rows_ref, bf16[224,512]{1,0:T(8,128)(2,1)S(1)} %collective-permute-done.5.swap_ref), custom_call_target="tpu_custom_call" | custom-call | bytes 1048576 | tf_op jit(solution)/shard_map/pallas_call | solution.py:419
  77.6 3.5 %collective-permute-done.9.swap_ref = bf16[224,256]{1,0:T(8,128)(2,1)S(1)} collective-permute-done((bf16[224,256]{1,0:T(8,128)(2,1)S(1)}, bf16[224,256]{1,0:T(8,128)(2,1)S(1)}, u32[]{:S(2)}, u32[]{:S(2)}) %collective-permute-start.9) | collective-permute-done | bytes 114720 | tf_op jit(solution)/shard_map/ppermute | solution.py:423
  81.2 1.0 %shard_map.105 = (bf16[224,256]{1,0:T(8,128)(2,1)}, bf16[224,256]{1,0:T(8,128)(2,1)}) custom-call(s32[8,128]{1,0:T(8,128)S(1)} %shard_map.93.facts_ref, bf16[352,256]{1,0:T(8,128)(2,1)S(1)} %get-tuple-element.48.rows_ref, bf16[224,256]{1,0:T(8,128)(2,1)S(1)} %collective-permute-done.9.swap_ref), custom_call_target="tpu_custom_call" | custom-call | bytes 1048576 | tf_op jit(solution)/shard_map/pallas_call | solution.py:419
  (2 shorter events, 0.1 us)
Async XLA Ops:
  2.4 9.2 %all-to-all-start.1 = ((bf16[8,56,256]{2,1,0:T(8,128)(2,1)}), bf16[8,56,256]{2,1,0:T(8,128)(2,1)S(1)}, u32[]{:S(2)}, u32[]{:S(2)}) async-start(bf16[8,56,256]{2,1,0:T(8,128)(2,1)} %shard_map.96), calls=%async_computation.1 | async-start | bytes 458752 | tf_op jit(solution)/shard_map/all_to_all | solution.py:454
  6.4 0.7 copy-start
  7.1 0.7 copy-start.1
  11.9 11.7 %collective-permute-start.1 = (bf16[352,256]{1,0:T(8,128)(2,1)S(1)}, bf16[352,256]{1,0:T(8,128)(2,1)S(1)}, u32[]{:S(2)}, u32[]{:S(2)}) collective-permute-start(bf16[352,256]{1,0:T(8,128)(2,1)S(1)} %shard_map.97.mine_ref), channel_id=1, source_target_pairs={{0,12},{4,8},{8,20},{12,16},{16,28},{20,24},{24,36},{28,32},{32,44... | collective-permute-start | bytes 540680 | tf_op jit(solution)/shard_map/ppermute | solution.py:432
  19.6 18.1 %all-to-all-start = ((bf16[8,56,512]{2,1,0:T(8,128)(2,1)}), bf16[8,56,512]{2,1,0:T(8,128)(2,1)S(1)}, u32[]{:S(2)}, u32[]{:S(2)}) async-start(bf16[8,56,512]{2,1,0:T(8,128)(2,1)} %shard_map.94), calls=%async_computation | async-start | bytes 917504 | tf_op jit(solution)/shard_map/all_to_all | solution.py:455
  23.6 16.5 %collective-permute-start.2 = (bf16[608,256]{1,0:T(8,128)(2,1)S(1)}, bf16[608,256]{1,0:T(8,128)(2,1)S(1)}, u32[]{:S(2)}, u32[]{:S(2)}) collective-permute-start(bf16[608,256]{1,0:T(8,128)(2,1)S(1)} %get-tuple-element.30.mine_ref), channel_id=1, source_target_pairs={{0,16},{4,20},{8,24},{12,28},{16,32},{20,36},{24,40},{28,44},{32,4... | collective-permute-start | bytes 933896 | tf_op jit(solution)/shard_map/ppermute | solution.py:432
  27.7 12.3 %collective-permute-start.3 = (bf16[352,256]{1,0:T(8,128)(2,1)S(1)}, bf16[352,256]{1,0:T(8,128)(2,1)S(1)}, u32[]{:S(2)}, u32[]{:S(2)}) collective-permute-start(bf16[352,256]{1,0:T(8,128)(2,1)S(1)} %get-tuple-element.31), channel_id=1, source_target_pairs={{0,32},{4,36},{8,40},{12,44},{16,48},{20,52},{24,56},{28,60},{32,6... | collective-permute-start | bytes 540680 | tf_op jit(solution)/shard_map/ppermute | solution.py:432
  38.1 7.7 %collective-permute-start = (bf16[96,512]{1,0:T(8,128)(2,1)S(1)}, bf16[96,512]{1,0:T(8,128)(2,1)S(1)}, u32[]{:S(2)}, u32[]{:S(2)}) collective-permute-start(bf16[96,512]{1,0:T(8,128)(2,1)S(1)} %get-tuple-element.29.extra_ref), channel_id=1, source_target_pairs={{0,12},{4,8},{8,20},{12,16},{16,28},{20,24},{24,36},{28,32},{32,44... | collective-permute-start | bytes 294920 | tf_op jit(solution)/shard_map/ppermute | solution.py:432
  47.9 13.3 %collective-permute-start.6 = (bf16[608,256]{1,0:T(8,128)(2,1)S(1)}, bf16[608,256]{1,0:T(8,128)(2,1)S(1)}, u32[]{:S(2)}, u32[]{:S(2)}) collective-permute-start(bf16[608,256]{1,0:T(8,128)(2,1)S(1)} %get-tuple-element.44), channel_id=1, source_target_pairs={{16,0},{20,4},{24,8},{28,12},{32,16},{36,20},{40,24},{44,28},{48,3... | collective-permute-start | bytes 933896 | tf_op jit(solution)/shard_map/ppermute | solution.py:432
  50.1 8.6 %collective-permute-start.7 = (bf16[352,256]{1,0:T(8,128)(2,1)S(1)}, bf16[352,256]{1,0:T(8,128)(2,1)S(1)}, u32[]{:S(2)}, u32[]{:S(2)}) collective-permute-start(bf16[352,256]{1,0:T(8,128)(2,1)S(1)} %get-tuple-element.45), channel_id=1, source_target_pairs={{32,0},{36,4},{40,8},{44,12},{48,16},{52,20},{56,24},{60,28},{64,3... | collective-permute-start | bytes 540680 | tf_op jit(solution)/shard_map/ppermute | solution.py:432
  52.1 13.9 %collective-permute-start.4 = (bf16[96,512]{1,0:T(8,128)(2,1)S(1)}, bf16[96,512]{1,0:T(8,128)(2,1)S(1)}, u32[]{:S(2)}, u32[]{:S(2)}) collective-permute-start(bf16[96,512]{1,0:T(8,128)(2,1)S(1)} %get-tuple-element.35), channel_id=1, source_target_pairs={{8,4},{12,0},{16,12},{20,8},{24,20},{28,16},{32,28},{36,24},{40,36... | collective-permute-start | bytes 294920 | tf_op jit(solution)/shard_map/ppermute | solution.py:432
  61.3 13.1 %collective-permute-start.8 = (bf16[352,256]{1,0:T(8,128)(2,1)S(1)}, bf16[352,256]{1,0:T(8,128)(2,1)S(1)}, u32[]{:S(2)}, u32[]{:S(2)}) collective-permute-start(bf16[352,256]{1,0:T(8,128)(2,1)S(1)} %get-tuple-element.47), channel_id=1, source_target_pairs={{8,4},{12,0},{16,12},{20,8},{24,20},{28,16},{32,28},{36,24},{40,36... | collective-permute-start | bytes 540680 | tf_op jit(solution)/shard_map/ppermute | solution.py:432
  66.0 10.4 %collective-permute-start.5 = (bf16[224,512]{1,0:T(8,128)(2,1)S(1)}, bf16[224,512]{1,0:T(8,128)(2,1)S(1)}, u32[]{:S(2)}, u32[]{:S(2)}) collective-permute-start(bf16[224,512]{1,0:T(8,128)(2,1)S(1)} %get-tuple-element.38), channel_id=1, source_target_pairs={{0,4},{4,0},{1,5},{5,1},{2,6},{6,2},{3,7},{7,3},{8,12},{12,8},{9,1... | collective-permute-start | bytes 688136 | tf_op jit(solution)/shard_map/ppermute | solution.py:423
  74.5 6.7 %collective-permute-start.9 = (bf16[224,256]{1,0:T(8,128)(2,1)S(1)}, bf16[224,256]{1,0:T(8,128)(2,1)S(1)}, u32[]{:S(2)}, u32[]{:S(2)}) collective-permute-start(bf16[224,256]{1,0:T(8,128)(2,1)S(1)} %get-tuple-element.49), channel_id=1, source_target_pairs={{0,4},{4,0},{1,5},{5,1},{2,6},{6,2},{3,7},{7,3},{8,12},{12,8},{9,1... | collective-permute-start | bytes 344072 | tf_op jit(solution)/shard_map/ppermute | solution.py:423

commit v6 on v5

--- a/solution.py
+++ b/solution.py
@@ -115,24 +115,26 @@
     facts_ref[len(facts) :, :] = jnp.zeros((8 - len(facts), HEAD), jnp.int32)
 
 
-def raw_rows(facts_ref, slots_ref):
-    place = lax.broadcasted_iota(jnp.int32, (SPAN, 1), 0) + (pair_index() * PAIR - LEAD)
+def raw_rows(facts_ref, slots_ref, start, count):
+    place = lax.broadcasted_iota(jnp.int32, (count, 1), 0) + (pair_index() * PAIR - LEAD + start)
     first = facts_ref[0:1, 0:1]
     middle = facts_ref[1:2, 0:1]
     last = facts_ref[2:3, 0:1]
     source = jnp.where(place < middle, place - first, SLOTS + place - middle)
     source = jnp.where((place >= first) & (place < last), source, -1)
-    return picked(SPAN, source, slots_ref[...])
+    return picked(count, source, slots_ref[...])
 
 
 def raw_keys_kernel(facts_ref, slots_ref, out_ref):
-    out_ref[...] = raw_rows(facts_ref, slots_ref)
-
-
-def raw_queries_kernel(facts_ref, slots_ref, edge_ref, rows_ref):
-    rows = raw_rows(facts_ref, slots_ref)
-    edge_ref[...] = rows[PAIR:]
-    rows_ref[...] = rows[:PAIR]
+    out_ref[...] = raw_rows(facts_ref, slots_ref, 0, SPAN)
+
+
+def raw_edge_kernel(facts_ref, slots_ref, edge_ref):
+    edge_ref[...] = raw_rows(facts_ref, slots_ref, PAIR, EDGE)
+
+
+def raw_queries_kernel(facts_ref, slots_ref, rows_ref):
+    rows_ref[...] = raw_rows(facts_ref, slots_ref, 0, PAIR)
 
 
 def joined(rows, edge):
@@ -456,9 +458,9 @@
     first = call(raw_keys_kernel, shape(SPAN, narrow), [vmem()] * 2)(
         facts, key_slots.reshape(2 * SLOTS, narrow)
     )
-    edge, rows = call(
-        raw_queries_kernel, [shape(EDGE, wide), shape(PAIR, wide)], [vmem()] * 2
-    )(facts, query_slots.reshape(2 * SLOTS, wide))
+    query_slots = query_slots.reshape(2 * SLOTS, wide)
+    edge = call(raw_edge_kernel, shape(EDGE, wide), [vmem()] * 2)(facts, query_slots)
+    rows = call(raw_queries_kernel, shape(PAIR, wide), [vmem()] * 2)(facts, query_slots)
     from_first = shifted(first, 1)
     from_edge = shifted(edge, 1)
     second, fourth = call(

time: 83.1 us -> 83 us (level)
  waiting for transfers between devices: 27.5 us -> 26.5 us
    ppermute x8, waiting for transfers between devices: 13.8 us -> 12.8 us  [shifted(): return lax.ppermute(value, SEQ_AXES, route)]
where the time goes in v6:
time: 83 us; the launch traced here: 82.1 us
  starting transfers between devices  41 us (49%)
  waiting for transfers between devices  26.5 us (32%)
  Pallas kernels  12.4 us (15%)
  local copies, waits for them, and re-layouts  1.36 us (2%)
    ppermute x8, starting transfers between devices, shifted(): return lax.ppermute(value, SEQ_AXES, route)  27.9 us
    ppermute x8, waiting for transfers between devices, shifted(): return lax.ppermute(value, SEQ_AXES, route)  12.8 us
    all_to_all x1, waiting for transfers between devices, layer(): query_slots = lax.all_to_all(packed_queries, GROUP_AXES, 0, 0, tiled=True)  7.06 us
    ppermute x2, starting transfers between devices, swapped(): return lax.ppermute(value, 'yl', [(0, 1), (1, 0)])  5.1 us
    all_to_all x1, starting transfers between devices, layer(): key_slots = lax.all_to_all(packed_keys, GROUP_AXES, 0, 0, tiled=True)  4.08 us
    all_to_all x1, starting transfers between devices, layer(): query_slots = lax.all_to_all(packed_queries, GROUP_AXES, 0, 0, tiled=True)  3.92 us
    ppermute x2, waiting for transfers between devices, swapped(): return lax.ppermute(value, 'yl', [(0, 1), (1, 0)])  3.54 us
    all_to_all x1, waiting for transfers between devices, layer(): key_slots = lax.all_to_all(packed_keys, GROUP_AXES, 0, 0, tiled=True)  3.11 us
  transfers between devices with their start and end apart: 12, of which 8 were waited for; matrix products, arithmetic and copies ran while one was open for 0% of the time, Pallas kernels for 9%

profile of v6, /device:TPU:252, one launch (start us, length us, event | category | flops | bytes accessed | tf_op | source)
XLA Modules:
  0.0 82.1 jit_solution(16966631592548461703)
XLA Ops:
  0.6 1.7 %shard_map.97 = bf16[8,56,256]{2,1,0:T(8,128)(2,1)} custom-call(bf16[56,1024]{1,0:T(8,128)(2,1)} %first_ref.3, bf16[56,1024]{1,0:T(8,128)(2,1)} %second_ref.3), custom_call_target="tpu_custom_call" | custom-call | bytes 1048576 | tf_op jit(solution)/shard_map/pallas_call | solution.py:441
  2.4 4.1 %all-to-all-start.1 = ((bf16[8,56,256]{2,1,0:T(8,128)(2,1)}), bf16[8,56,256]{2,1,0:T(8,128)(2,1)S(1)}, u32[]{:S(2)}, u32[]{:S(2)}) async-start(bf16[8,56,256]{2,1,0:T(8,128)(2,1)} %shard_map.97), calls=%async_computation.1 | async-start | bytes 458752 | tf_op jit(solution)/shard_map/all_to_all | solution.py:456
  6.4 0.0 copy-start
  6.4 0.7 copy-done
  7.1 0.0 copy-start.1
  7.1 0.7 copy-done.1
  7.8 0.6 shard_map.93.facts_ref
  8.4 3.1 %all-to-all-done.1 = bf16[8,56,256]{2,1,0:T(8,128)(2,1)S(1)} async-done(((bf16[8,56,256]{2,1,0:T(8,128)(2,1)}), bf16[8,56,256]{2,1,0:T(8,128)(2,1)S(1)}, u32[]{:S(2)}, u32[]{:S(2)}) %all-to-all-start.1) | async-done | bytes 229408 | tf_op jit(solution)/shard_map/all_to_all | solution.py:456
  11.5 0.3 shard_map.98.mine_ref
  11.9 5.8 %collective-permute-start.1 = (bf16[352,256]{1,0:T(8,128)(2,1)S(1)}, bf16[352,256]{1,0:T(8,128)(2,1)S(1)}, u32[]{:S(2)}, u32[]{:S(2)}) collective-permute-start(bf16[352,256]{1,0:T(8,128)(2,1)S(1)} %shard_map.98.mine_ref), channel_id=1, source_target_pairs={{0,12},{4,8},{8,20},{12,16},{16,28},{20,24},{24,36},{28,32},{32,44... | collective-permute-start | bytes 540680 | tf_op jit(solution)/shard_map/ppermute | solution.py:434
  17.7 1.9 %shard_map.94 = bf16[8,56,512]{2,1,0:T(8,128)(2,1)} custom-call(bf16[56,2048]{1,0:T(8,128)(2,1)} %first_ref.2, bf16[56,2048]{1,0:T(8,128)(2,1)} %second_ref.2), custom_call_target="tpu_custom_call" | custom-call | bytes 1048576 | tf_op jit(solution)/shard_map/pallas_call | solution.py:444
  19.6 3.9 %all-to-all-start = ((bf16[8,56,512]{2,1,0:T(8,128)(2,1)}), bf16[8,56,512]{2,1,0:T(8,128)(2,1)S(1)}, u32[]{:S(2)}, u32[]{:S(2)}) async-start(bf16[8,56,512]{2,1,0:T(8,128)(2,1)} %shard_map.94), calls=%async_computation | async-start | bytes 917504 | tf_op jit(solution)/shard_map/all_to_all | solution.py:457
  23.5 0.0 collective-permute-done.1.first_ref
  23.5 4.2 %collective-permute-start.2 = (bf16[608,256]{1,0:T(8,128)(2,1)S(1)}, bf16[608,256]{1,0:T(8,128)(2,1)S(1)}, u32[]{:S(2)}, u32[]{:S(2)}) collective-permute-start(bf16[608,256]{1,0:T(8,128)(2,1)S(1)} %get-tuple-element.26.mine_ref), channel_id=1, source_target_pairs={{0,16},{4,20},{8,24},{12,28},{16,32},{20,36},{24,40},{28,44},{32,4... | collective-permute-start | bytes 933896 | tf_op jit(solution)/shard_map/ppermute | solution.py:434
  27.7 2.9 %collective-permute-start.3 = (bf16[352,256]{1,0:T(8,128)(2,1)S(1)}, bf16[352,256]{1,0:T(8,128)(2,1)S(1)}, u32[]{:S(2)}, u32[]{:S(2)}) collective-permute-start(bf16[352,256]{1,0:T(8,128)(2,1)S(1)} %get-tuple-element.27), channel_id=1, source_target_pairs={{0,32},{4,36},{8,40},{12,44},{16,48},{20,52},{24,56},{28,60},{32,6... | collective-permute-start | bytes 540680 | tf_op jit(solution)/shard_map/ppermute | solution.py:434
  30.7 7.1 %all-to-all-done = bf16[8,56,512]{2,1,0:T(8,128)(2,1)S(1)} async-done(((bf16[8,56,512]{2,1,0:T(8,128)(2,1)}), bf16[8,56,512]{2,1,0:T(8,128)(2,1)S(1)}, u32[]{:S(2)}, u32[]{:S(2)}) %all-to-all-start) | async-done | bytes 458784 | tf_op jit(solution)/shard_map/all_to_all | solution.py:457
  37.7 0.3 shard_map.96.extra_ref
  38.0 1.9 %collective-permute-start = (bf16[96,512]{1,0:T(8,128)(2,1)S(1)}, bf16[96,512]{1,0:T(8,128)(2,1)S(1)}, u32[]{:S(2)}, u32[]{:S(2)}) collective-permute-start(bf16[96,512]{1,0:T(8,128)(2,1)S(1)} %shard_map.96.extra_ref), channel_id=1, source_target_pairs={{0,12},{4,8},{8,20},{12,16},{16,28},{20,24},{24,36},{28,32},{32,44... | collective-permute-start | bytes 294920 | tf_op jit(solution)/shard_map/ppermute | solution.py:434
  39.9 0.4 shard_map.95.rows_ref
  40.3 0.0 collective-permute-done.3.fourth_ref
  40.3 0.0 collective-permute-done.2.second_ref
  40.3 2.8 %shard_map.100 = (bf16[128,512]{1,0:T(8,128)(2,1)S(1)}, bf16[64,512]{1,0:T(8,128)(2,1)S(1)}, f32[1152,256]{1,0:T(8,128)S(1)}, f32[64,256]{1,0:T(8,128)S(1)}) custom-call(bf16[256,512]{1,0:T(8,128)(2,1)S(1)} %shard_map.95.rows_ref, bf16[96,512]{1,0:T(8,128)(2,1)S(1)} %shard_map.96.extra_ref, bf16[608,256]{1,0:T(8,128)(2,1)S(1)} %get-tuple-element.26.mine_ref, ...), custom_call_target="tpu_custom_call" | custom-call | flops 1000000000 | bytes 1048576 | tf_op jit(solution)/shard_map/pallas_call | solution.py:472
  43.1 2.6 %collective-permute-done.edge_ref = bf16[96,512]{1,0:T(8,128)(2,1)S(1)} collective-permute-done((bf16[96,512]{1,0:T(8,128)(2,1)S(1)}, bf16[96,512]{1,0:T(8,128)(2,1)S(1)}, u32[]{:S(2)}, u32[]{:S(2)}) %collective-permute-start) | collective-permute-done | bytes 98336 | tf_op jit(solution)/shard_map/ppermute | solution.py:434
  45.7 2.0 %shard_map.101 = (bf16[256,512]{1,0:T(8,128)(2,1)S(1)}, bf16[96,512]{1,0:T(8,128)(2,1)S(1)}, f32[256,256]{1,0:T(8,128)S(1)}, f32[256,256]{1,0:T(8,128)S(1)}, bf1...) custom-call(bf16[256,512]{1,0:T(8,128)(2,1)S(1)} %shard_map.95.rows_ref, ...), custom_call_target="tpu_custom_call" | custom-call | flops 1000000000 | bytes 1048576 | tf_op jit(solution)/shard_map/pallas_call | solution.py:485
  47.7 2.6 %collective-permute-start.6 = (bf16[608,256]{1,0:T(8,128)(2,1)S(1)}, bf16[608,256]{1,0:T(8,128)(2,1)S(1)}, u32[]{:S(2)}, u32[]{:S(2)}) collective-permute-start(bf16[608,256]{1,0:T(8,128)(2,1)S(1)} %get-tuple-element.40), channel_id=1, source_target_pairs={{16,0},{20,4},{24,8},{28,12},{32,16},{36,20},{40,24},{44,28},{48,3... | collective-permute-start | bytes 933896 | tf_op jit(solution)/shard_map/ppermute | solution.py:434
  50.3 2.0 %collective-permute-start.7 = (bf16[352,256]{1,0:T(8,128)(2,1)S(1)}, bf16[352,256]{1,0:T(8,128)(2,1)S(1)}, u32[]{:S(2)}, u32[]{:S(2)}) collective-permute-start(bf16[352,256]{1,0:T(8,128)(2,1)S(1)} %get-tuple-element.41), channel_id=1, source_target_pairs={{32,0},{36,4},{40,8},{44,12},{48,16},{52,20},{56,24},{60,28},{64,3... | collective-permute-start | bytes 540680 | tf_op jit(solution)/shard_map/ppermute | solution.py:434
  52.3 4.0 %collective-permute-start.4 = (bf16[96,512]{1,0:T(8,128)(2,1)S(1)}, bf16[96,512]{1,0:T(8,128)(2,1)S(1)}, u32[]{:S(2)}, u32[]{:S(2)}) collective-permute-start(bf16[96,512]{1,0:T(8,128)(2,1)S(1)} %get-tuple-element.31), channel_id=1, source_target_pairs={{8,4},{12,0},{16,12},{20,8},{24,20},{28,16},{32,28},{36,24},{40,36... | collective-permute-start | bytes 294920 | tf_op jit(solution)/shard_map/ppermute | solution.py:434
  56.3 2.6 %collective-permute-done.7.back4_ref = bf16[352,256]{1,0:T(8,128)(2,1)S(1)} collective-permute-done((bf16[352,256]{1,0:T(8,128)(2,1)S(1)}, bf16[352,256]{1,0:T(8,128)(2,1)S(1)}, u32[]{:S(2)}, u32[]{:S(2)}) %collective-permute-start.7) | collective-permute-done | bytes 180256 | tf_op jit(solution)/shard_map/ppermute | solution.py:434
  58.9 2.2 %collective-permute-done.6.back2_ref = bf16[608,256]{1,0:T(8,128)(2,1)S(1)} collective-permute-done((bf16[608,256]{1,0:T(8,128)(2,1)S(1)}, bf16[608,256]{1,0:T(8,128)(2,1)S(1)}, u32[]{:S(2)}, u32[]{:S(2)}) %collective-permute-start.6) | collective-permute-done | bytes 311328 | tf_op jit(solution)/shard_map/ppermute | solution.py:434
  61.1 0.1 shard_map.104
  61.2 4.5 %collective-permute-start.8 = (bf16[352,256]{1,0:T(8,128)(2,1)S(1)}, bf16[352,256]{1,0:T(8,128)(2,1)S(1)}, u32[]{:S(2)}, u32[]{:S(2)}) collective-permute-start(bf16[352,256]{1,0:T(8,128)(2,1)S(1)} %get-tuple-element.43), channel_id=1, source_target_pairs={{8,4},{12,0},{16,12},{20,8},{24,20},{28,16},{32,28},{36,24},{40,36... | collective-permute-start | bytes 540680 | tf_op jit(solution)/shard_map/ppermute | solution.py:434
  65.6 0.5 collective-permute-done.4.edge_ref
  66.2 3.2 %collective-permute-start.5 = (bf16[224,512]{1,0:T(8,128)(2,1)S(1)}, bf16[224,512]{1,0:T(8,128)(2,1)S(1)}, u32[]{:S(2)}, u32[]{:S(2)}) collective-permute-start(bf16[224,512]{1,0:T(8,128)(2,1)S(1)} %get-tuple-element.34), channel_id=1, source_target_pairs={{0,4},{4,0},{1,5},{5,1},{2,6},{6,2},{3,7},{7,3},{8,12},{12,8},{9,1... | collective-permute-start | bytes 688136 | tf_op jit(solution)/shard_map/ppermute | solution.py:425
  69.4 4.9 %collective-permute-done.8.back_ref = bf16[352,256]{1,0:T(8,128)(2,1)S(1)} collective-permute-done((bf16[352,256]{1,0:T(8,128)(2,1)S(1)}, bf16[352,256]{1,0:T(8,128)(2,1)S(1)}, u32[]{:S(2)}, u32[]{:S(2)}) %collective-permute-start.8) | collective-permute-done | bytes 180256 | tf_op jit(solution)/shard_map/ppermute | solution.py:434
  74.3 0.1 shard_map.105
  74.3 1.9 %collective-permute-start.9 = (bf16[224,256]{1,0:T(8,128)(2,1)S(1)}, bf16[224,256]{1,0:T(8,128)(2,1)S(1)}, u32[]{:S(2)}, u32[]{:S(2)}) collective-permute-start(bf16[224,256]{1,0:T(8,128)(2,1)S(1)} %get-tuple-element.45), channel_id=1, source_target_pairs={{0,4},{4,0},{1,5},{5,1},{2,6},{6,2},{3,7},{7,3},{8,12},{12,8},{9,1... | collective-permute-start | bytes 344072 | tf_op jit(solution)/shard_map/ppermute | solution.py:425
  76.3 0.0 collective-permute-done.5.swap_ref
  76.3 1.2 %shard_map.103 = (bf16[224,512]{1,0:T(8,128)(2,1)}, bf16[224,512]{1,0:T(8,128)(2,1)}) custom-call(s32[8,128]{1,0:T(8,128)S(1)} %shard_map.93.facts_ref, bf16[352,512]{1,0:T(8,128)(2,1)S(1)} %get-tuple-element.33.rows_ref, bf16[224,512]{1,0:T(8,128)(2,1)S(1)} %collective-permute-done.5.swap_ref), custom_call_target="tpu_custom_call" | custom-call | bytes 1048576 | tf_op jit(solution)/shard_map/pallas_call | solution.py:421
  77.5 3.5 %collective-permute-done.9.swap_ref = bf16[224,256]{1,0:T(8,128)(2,1)S(1)} collective-permute-done((bf16[224,256]{1,0:T(8,128)(2,1)S(1)}, bf16[224,256]{1,0:T(8,128)(2,1)S(1)}, u32[]{:S(2)}, u32[]{:S(2)}) %collective-permute-start.9) | collective-permute-done | bytes 114720 | tf_op jit(solution)/shard_map/ppermute | solution.py:425
  81.0 1.0 %shard_map.106 = (bf16[224,256]{1,0:T(8,128)(2,1)}, bf16[224,256]{1,0:T(8,128)(2,1)}) custom-call(s32[8,128]{1,0:T(8,128)S(1)} %shard_map.93.facts_ref, bf16[352,256]{1,0:T(8,128)(2,1)S(1)} %get-tuple-element.44.rows_ref, bf16[224,256]{1,0:T(8,128)(2,1)S(1)} %collective-permute-done.9.swap_ref), custom_call_target="tpu_custom_call" | custom-call | bytes 1048576 | tf_op jit(solution)/shard_map/pallas_call | solution.py:421
  (2 shorter events, 0.1 us)
Async XLA Ops:
  2.4 9.2 %all-to-all-start.1 = ((bf16[8,56,256]{2,1,0:T(8,128)(2,1)}), bf16[8,56,256]{2,1,0:T(8,128)(2,1)S(1)}, u32[]{:S(2)}, u32[]{:S(2)}) async-start(bf16[8,56,256]{2,1,0:T(8,128)(2,1)} %shard_map.97), calls=%async_computation.1 | async-start | bytes 458752 | tf_op jit(solution)/shard_map/all_to_all | solution.py:456
  6.4 0.7 copy-start
  7.1 0.7 copy-start.1
  11.9 11.7 %collective-permute-start.1 = (bf16[352,256]{1,0:T(8,128)(2,1)S(1)}, bf16[352,256]{1,0:T(8,128)(2,1)S(1)}, u32[]{:S(2)}, u32[]{:S(2)}) collective-permute-start(bf16[352,256]{1,0:T(8,128)(2,1)S(1)} %shard_map.98.mine_ref), channel_id=1, source_target_pairs={{0,12},{4,8},{8,20},{12,16},{16,28},{20,24},{24,36},{28,32},{32,44... | collective-permute-start | bytes 540680 | tf_op jit(solution)/shard_map/ppermute | solution.py:434
  19.6 18.1 %all-to-all-start = ((bf16[8,56,512]{2,1,0:T(8,128)(2,1)}), bf16[8,56,512]{2,1,0:T(8,128)(2,1)S(1)}, u32[]{:S(2)}, u32[]{:S(2)}) async-start(bf16[8,56,512]{2,1,0:T(8,128)(2,1)} %shard_map.94), calls=%async_computation | async-start | bytes 917504 | tf_op jit(solution)/shard_map/all_to_all | solution.py:457
  23.5 16.8 %collective-permute-start.2 = (bf16[608,256]{1,0:T(8,128)(2,1)S(1)}, bf16[608,256]{1,0:T(8,128)(2,1)S(1)}, u32[]{:S(2)}, u32[]{:S(2)}) collective-permute-start(bf16[608,256]{1,0:T(8,128)(2,1)S(1)} %get-tuple-element.26.mine_ref), channel_id=1, source_target_pairs={{0,16},{4,20},{8,24},{12,28},{16,32},{20,36},{24,40},{28,44},{32,4... | collective-permute-start | bytes 933896 | tf_op jit(solution)/shard_map/ppermute | solution.py:434
  27.7 12.6 %collective-permute-start.3 = (bf16[352,256]{1,0:T(8,128)(2,1)S(1)}, bf16[352,256]{1,0:T(8,128)(2,1)S(1)}, u32[]{:S(2)}, u32[]{:S(2)}) collective-permute-start(bf16[352,256]{1,0:T(8,128)(2,1)S(1)} %get-tuple-element.27), channel_id=1, source_target_pairs={{0,32},{4,36},{8,40},{12,44},{16,48},{20,52},{24,56},{28,60},{32,6... | collective-permute-start | bytes 540680 | tf_op jit(solution)/shard_map/ppermute | solution.py:434
  38.0 7.7 %collective-permute-start = (bf16[96,512]{1,0:T(8,128)(2,1)S(1)}, bf16[96,512]{1,0:T(8,128)(2,1)S(1)}, u32[]{:S(2)}, u32[]{:S(2)}) collective-permute-start(bf16[96,512]{1,0:T(8,128)(2,1)S(1)} %shard_map.96.extra_ref), channel_id=1, source_target_pairs={{0,12},{4,8},{8,20},{12,16},{16,28},{20,24},{24,36},{28,32},{32,44... | collective-permute-start | bytes 294920 | tf_op jit(solution)/shard_map/ppermute | solution.py:434
  47.7 13.4 %collective-permute-start.6 = (bf16[608,256]{1,0:T(8,128)(2,1)S(1)}, bf16[608,256]{1,0:T(8,128)(2,1)S(1)}, u32[]{:S(2)}, u32[]{:S(2)}) collective-permute-start(bf16[608,256]{1,0:T(8,128)(2,1)S(1)} %get-tuple-element.40), channel_id=1, source_target_pairs={{16,0},{20,4},{24,8},{28,12},{32,16},{36,20},{40,24},{44,28},{48,3... | collective-permute-start | bytes 933896 | tf_op jit(solution)/shard_map/ppermute | solution.py:434
  50.3 8.6 %collective-permute-start.7 = (bf16[352,256]{1,0:T(8,128)(2,1)S(1)}, bf16[352,256]{1,0:T(8,128)(2,1)S(1)}, u32[]{:S(2)}, u32[]{:S(2)}) collective-permute-start(bf16[352,256]{1,0:T(8,128)(2,1)S(1)} %get-tuple-element.41), channel_id=1, source_target_pairs={{32,0},{36,4},{40,8},{44,12},{48,16},{52,20},{56,24},{60,28},{64,3... | collective-permute-start | bytes 540680 | tf_op jit(solution)/shard_map/ppermute | solution.py:434
  52.3 13.8 %collective-permute-start.4 = (bf16[96,512]{1,0:T(8,128)(2,1)S(1)}, bf16[96,512]{1,0:T(8,128)(2,1)S(1)}, u32[]{:S(2)}, u32[]{:S(2)}) collective-permute-start(bf16[96,512]{1,0:T(8,128)(2,1)S(1)} %get-tuple-element.31), channel_id=1, source_target_pairs={{8,4},{12,0},{16,12},{20,8},{24,20},{28,16},{32,28},{36,24},{40,36... | collective-permute-start | bytes 294920 | tf_op jit(solution)/shard_map/ppermute | solution.py:434
  61.2 13.1 %collective-permute-start.8 = (bf16[352,256]{1,0:T(8,128)(2,1)S(1)}, bf16[352,256]{1,0:T(8,128)(2,1)S(1)}, u32[]{:S(2)}, u32[]{:S(2)}) collective-permute-start(bf16[352,256]{1,0:T(8,128)(2,1)S(1)} %get-tuple-element.43), channel_id=1, source_target_pairs={{8,4},{12,0},{16,12},{20,8},{24,20},{28,16},{32,28},{36,24},{40,36... | collective-permute-start | bytes 540680 | tf_op jit(solution)/shard_map/ppermute | solution.py:434
  66.2 10.1 %collective-permute-start.5 = (bf16[224,512]{1,0:T(8,128)(2,1)S(1)}, bf16[224,512]{1,0:T(8,128)(2,1)S(1)}, u32[]{:S(2)}, u32[]{:S(2)}) collective-permute-start(bf16[224,512]{1,0:T(8,128)(2,1)S(1)} %get-tuple-element.34), channel_id=1, source_target_pairs={{0,4},{4,0},{1,5},{5,1},{2,6},{6,2},{3,7},{7,3},{8,12},{12,8},{9,1... | collective-permute-start | bytes 688136 | tf_op jit(solution)/shard_map/ppermute | solution.py:425
  74.3 6.7 %collective-permute-start.9 = (bf16[224,256]{1,0:T(8,128)(2,1)S(1)}, bf16[224,256]{1,0:T(8,128)(2,1)S(1)}, u32[]{:S(2)}, u32[]{:S(2)}) collective-permute-start(bf16[224,256]{1,0:T(8,128)(2,1)S(1)} %get-tuple-element.45), channel_id=1, source_target_pairs={{0,4},{4,0},{1,5},{5,1},{2,6},{6,2},{3,7},{7,3},{8,12},{12,8},{9,1... | collective-permute-start | bytes 344072 | tf_op jit(solution)/shard_map/ppermute | solution.py:425
